TPU v7x, 32 devices: a whole 2x2x4 slice. The times are simulated.
32 devices in a mesh: group: 2 (over core), gx: 4 (over y, x), gy: 4 (over z).
Axes of the slice: x: 2, y: 2, z: 4, core: 2. Of those that a mesh axis runs over, the one named last changes fastest.
Arguments:
- forcing: float32 [2, 80, 32, 1024], P('group', None, 'gx', 'gy'), may hold values from -24 to 24
- conduct: bfloat16 [2, 80, 32, 1024], P('group', None, 'gx', 'gy'), may hold values from 0.25 to 4
- diag_add: bfloat16 [2, 80, 32, 1024], P('group', None, 'gx', 'gy'), may hold values from 0.049804688 to 0.5
- ice_mask: int32 [32, 1024], P('gx', 'gy'), may hold values 0 or 1
- grounded: int32 [32, 1024], P('gx', 'gy'), may hold values 0 or 1
Outputs:
- solution: float32 [2, 80, 32, 1024], P('group', None, 'gx', 'gy')
- residual: float32 [2, 80, 32, 1024], P('group', None, 'gx', 'gy')
All inputs are finite; a program needn't handle non-finite values. No bound on the sum of `ice_mask` or of `grounded` on one device may be relied on, other than what follows from the above.
Results may differ from a plain program's by a relative error of at most 0.0003.
Values sent between devices are 32-bit elements; how exact they have to be, the bound alone decides.
No kernel may reach another device: no remote copies, remote signals or barrier semaphores. Data moves between devices by JAX's collectives and lax.ppermute only.
A program may use at most 64 MiB of HBM per device.

v0:
```python
import math

import jax
import jax.numpy as jnp
from jax import lax
from jax.experimental import pallas as pl
from jax.experimental.pallas import tpu as pltpu
from jax.sharding import PartitionSpec as P

ITERS = 6
LANES = 128
SUBLANES = 8
HALO = 16
SHIFTS = (0.0, 0.75, 1.5, 0.25, 1.75, 1.0)
PAIRS = tuple((i, j) for i in range(ITERS + 1) for j in range(i + 1) if j < ITERS)


far_weight = 0.25
cross_weight = 0.5
vertical_weight = 4.0
friction_gain = 8.0
NEIGHBOURS = (
    (1, 0, 1.0),
    (-1, 0, 1.0),
    (0, 1, 1.0),
    (0, -1, 1.0),
    (2, 0, far_weight),
    (-2, 0, far_weight),
    (0, 2, far_weight),
    (0, -2, far_weight),
    (1, 1, cross_weight),
    (1, -1, cross_weight),
    (-1, 1, cross_weight),
    (-1, -1, cross_weight),
)


def with_halo(block, sides, width):
    for axis, dim in sides:
        count = lax.axis_size(axis)
        place = lax.axis_index(axis)
        ahead = [(i, (i + 1) % count) for i in range(count)]
        back = [(target, source) for source, target in ahead]
        low = lax.ppermute(
            lax.slice_in_dim(block, block.shape[dim] - width, None, axis=dim), axis, ahead
        )
        high = lax.ppermute(lax.slice_in_dim(block, 0, width, axis=dim), axis, back)
        low = jnp.where(place > 0, low, 0.0)
        high = jnp.where(place < count - 1, high, 0.0)
        block = jnp.concatenate([low, block, high], axis=dim)
    return block


def from_partner(shard, axis, distance):
    return lax.ppermute(shard, axis, [(i, i ^ 1 << distance) for i in range(lax.axis_size(axis))])


def beside_sum(padded, extent_x, extent_y):
    summed = jnp.zeros((padded.shape[0], extent_x, extent_y), jnp.float32)
    for shift_x, shift_y, weight in NEIGHBOURS:
        summed = (
            summed
            + weight
            * padded[:, 2 + shift_x : 2 + shift_x + extent_x, 2 + shift_y : 2 + shift_y + extent_y]
        )
    return summed


def vertical_sum(values):
    zeroes = jnp.zeros_like(values[:1])
    return jnp.concatenate([values[1:], zeroes], 0) + jnp.concatenate([zeroes, values[:-1]], 0)


def spread_padded(padded, values):
    return beside_sum(padded, values.shape[1], values.shape[2]) + vertical_weight * vertical_sum(
        values
    )


def operate(vector, coupling, diagonal):
    scaled = coupling * vector
    padded = with_halo(scaled, (("gx", 1), ("gy", 2)), 2)
    return diagonal * vector - coupling * spread_padded(padded, scaled)


def sum_over(partial, axes):
    count = math.prod(lax.axis_size(axis) for axis in axes)
    sent = jnp.broadcast_to(partial[None, None], (count, 1) + partial.shape)
    return jnp.sum(lax.all_to_all(sent, axes, 0, 0, tiled=True), axis=(0, 1))


def paired_sums(residual, precond, applied):
    partial = jnp.stack([jnp.sum(residual * precond), jnp.sum(applied * precond)])
    summed = sum_over(partial, ("gx", "gy"))
    return summed[0], summed[1]


def on_device(forcing, conduct, diag_add, ice_mask, grounded):
    own_force = forcing[0]
    layers = own_force.shape[0]
    group_id = lax.axis_index("group")
    is_ice = (group_id == 0).astype(jnp.float32)
    ice_cells = ice_mask.astype(jnp.float32)
    ground_cells = grounded.astype(jnp.float32)
    active = ice_cells * (1.0 - (1.0 - is_ice) * ground_cells)
    coupling = jnp.sqrt(conduct[0].astype(jnp.float32)) * active
    layer_index = lax.broadcasted_iota(jnp.int32, (layers, 1, 1), 0)
    edge_layer = jnp.where(group_id == 0, 0, layers - 1).astype(jnp.int32)
    edge_pick = (layer_index == edge_layer).astype(jnp.float32)
    bottom = (layer_index == 0).astype(jnp.float32)
    base_diag = diag_add[0].astype(jnp.float32) + bottom * (
        is_ice * friction_gain * ground_cells * ice_cells
    )
    padded_coupling = with_halo(coupling, (("gx", 1), ("gy", 2)), 2)
    diagonal = base_diag + coupling * spread_padded(padded_coupling, coupling)
    shared_value = active * jnp.mean(own_force, axis=0)
    shared_weight = lax.dynamic_index_in_dim(coupling, edge_layer, 0, keepdims=False)
    received = from_partner(jnp.stack([shared_value, shared_weight]), "group", 0)
    source = active * own_force + edge_pick * (active * received[1] * received[0])
    inverse = 1.0 / diagonal
    solution = jnp.zeros_like(source)
    residual = source
    precond = inverse * residual
    applied = operate(precond, coupling, diagonal)
    norm_now, curve = paired_sums(residual, precond, applied)
    step_size = norm_now / curve
    direction = precond
    along = applied
    for iteration in range(ITERS):
        solution = solution + step_size * direction
        residual = residual - step_size * along
        if iteration + 1 < ITERS:
            precond = inverse * residual
            applied = operate(precond, coupling, diagonal)
            norm_next, curve = paired_sums(residual, precond, applied)
            step_ratio = norm_next / norm_now
            step_size = norm_next / (curve - step_ratio * norm_next / step_size)
            direction = precond + step_ratio * direction
            along = applied + step_ratio * along
            norm_now = norm_next
    return (solution[None], residual[None])


def ring(count, step):
    return [(i, (i + step) % count) for i in range(count)]


def lanes_of(rows):
    return lax.broadcasted_iota(jnp.int32, (rows, LANES), 1)


def prepare_kernel(group_ref, force_ref, conduct_ref, diag_ref, ice_ref, ground_ref, fields_ref, low_ref, high_ref):
    layers = force_ref.shape[1]
    per_group = LANES // HALO
    is_ice = jnp.where(group_ref[0] == 0, 1.0, 0.0)
    ice = ice_ref[...].astype(jnp.float32)
    ground = ground_ref[...].astype(jnp.float32)
    active = ice * (1.0 - (1.0 - is_ice) * ground)
    friction = is_ice * friction_gain * ground * ice
    lane = lanes_of(SUBLANES)

    def step(q, carry):
        low, high = [None] * 3, [None] * 3
        for j in range(per_group):
            layer = q * per_group + j
            coupling = jnp.sqrt(conduct_ref[0, layer].astype(jnp.float32)) * active
            base = diag_ref[0, layer].astype(jnp.float32)
            if j == 0:
                base = base + friction * jnp.where(q == 0, 1.0, 0.0)
            force = active * force_ref[0, layer]
            for k, value in enumerate((coupling, base, force)):
                fields_ref[k, layer] = value
                first = pltpu.roll(value[:, :LANES], HALO * j, 1) if j else value[:, :LANES]
                last = value[:, -LANES:]
                turn = (HALO * (j + 1)) % LANES
                last = pltpu.roll(last, turn, 1) if turn else last
                if j == 0:
                    low[k], high[k] = first, last
                else:
                    here = lane >= HALO * j
                    low[k] = jnp.where(here, first, low[k])
                    high[k] = jnp.where(here, last, high[k])
        for k in range(3):
            low_ref[k, q] = low[k]
            high_ref[k, q] = high[k]
        return carry

    lax.fori_loop(0, layers // per_group, step, 0)


def pack_kernel(edge_ref, fields_ref, low_ref, high_ref, out_ref):
    layers = fields_ref.shape[1]
    count = out_ref.shape[0]
    per_group = LANES // HALO
    spare = LANES - 3 * LANES // 4
    width = fields_ref.shape[3] // count
    lane = lanes_of(SUBLANES)

    def step(q, carry):
        for k in range(3):
            low, high = low_ref[k, q], high_ref[k, q]
            if k == 0:
                low, high = low * edge_ref[0], high * edge_ref[1]
            main = [[None] * 3 for _ in range(count)]
            for j in range(per_group):
                value = fields_ref[k, q * per_group + j]
                pieces = [
                    pltpu.roll(value[:, p * LANES : (p + 1) * LANES], HALO, 1)
                    for p in range(value.shape[1] // LANES)
                ]
                turn = (LANES - HALO * j) % LANES
                before = pltpu.roll(low, turn, 1) if turn else low
                turn = (LANES - HALO * j + HALO) % LANES
                after = pltpu.roll(high, turn, 1) if turn else high
                wide = [jnp.where(lane < HALO, before, pieces[0])]
                for p in range(1, len(pieces)):
                    wide.append(jnp.where(lane < HALO, pieces[p - 1], pieces[p]))
                wide.append(jnp.where(lane < HALO, pieces[-1], after))
                turned = [pltpu.roll(piece, width, 1) for piece in wide]
                for d in range(count):
                    p = d * width // LANES
                    if d * width % LANES == 0:
                        window = wide[p]
                    else:
                        window = jnp.where(lane < width, turned[p], turned[p + 1])
                    m = j % 4
                    if m < 3:
                        main[d][m] = window
                    else:
                        for n in range(3):
                            tail = pltpu.roll(window, LANES - spare * (n + 1), 1)
                            out_ref[d, k, q * (per_group // 4) + j // 4, n] = jnp.where(
                                lane < LANES - spare, main[d][n], tail
                            )
        return carry

    lax.fori_loop(0, layers // per_group, step, 0)


def unpack_kernel(edge_ref, got_ref, fields_ref, shared_ref):
    count, _, groups = got_ref.shape[:3]
    layers = 4 * groups
    spare = LANES // 4
    lane = lanes_of(SUBLANES)
    for d in range(count):
        rows = pl.ds(SUBLANES * d, SUBLANES)

        def step(g, total, d=d, rows=rows):
            for k in range(3):
                fill = 1.0 if k == 1 else 0.0
                held = [got_ref[d, k, g, n] for n in range(3)]
                last = jnp.where(
                    lane < spare,
                    pltpu.roll(held[0], spare, 1),
                    jnp.where(
                        lane < 2 * spare, pltpu.roll(held[1], 2 * spare, 1), pltpu.roll(held[2], 3 * spare, 1)
                    ),
                )
                for n, value in enumerate(held + [last]):
                    value = jnp.where(lane < LANES - spare, value, fill)
                    fields_ref[k, 4 * g + n, rows] = value
                    if k == 2:
                        total = total + value
            return total

        total = lax.fori_loop(0, groups, step, jnp.zeros((SUBLANES, LANES), jnp.float32), unroll=2)
        shared_ref[0, rows] = total / layers
        shared_ref[1, rows] = fields_ref[0, edge_ref[0], rows]


def two_sum(a, b):
    total = a + b
    part = total - a
    return total, (a - (total - part)) + (b - part)


def add_pairs(high, low, other_high, other_low):
    total, error = two_sum(high, other_high)
    return total, low + other_low + error


def stencil(held_ref, layer, rows):
    def at(shift):
        return held_ref[layer + 1, pl.ds(SUBLANES + shift, rows)]

    here = at(0)
    near = at(1) + at(-1)
    mixed = here + cross_weight * near
    far = at(2) + at(-2) + pltpu.roll(here, 2, 1) + pltpu.roll(here, LANES - 2, 1)
    beside = near + pltpu.roll(mixed, 1, 1) + pltpu.roll(mixed, LANES - 1, 1) + far_weight * far
    above = held_ref[layer + 2, pl.ds(SUBLANES, rows)] + held_ref[layer, pl.ds(SUBLANES, rows)]
    return beside + vertical_weight * above


def krylov_kernel(edge_ref, fields_ref, got_ref, basis_ref, scale_ref, sums_ref, held_ref, factor_ref, gram_ref):
    layers, rows = fields_ref.shape[1:3]
    inner = pl.ds(SUBLANES, rows)
    empty = jnp.zeros((layers + 2, SUBLANES, LANES), jnp.float32)
    for side in range(2):
        held_ref[side, :, :SUBLANES] = empty
        held_ref[side, :, SUBLANES + rows :] = empty
        held_ref[side, 0] = jnp.zeros((rows + 2 * SUBLANES, LANES), jnp.float32)
        held_ref[side, layers + 1] = jnp.zeros((rows + 2 * SUBLANES, LANES), jnp.float32)

    def fill(layer, carry):
        held_ref[0, layer + 1, inner] = fields_ref[0, layer]
        return carry

    lax.fori_loop(0, layers, fill, 0, unroll=4)
    active = jnp.where(fields_ref[0, 0] > 0.0, 1.0, 0.0)
    term = active * got_ref[1] * got_ref[0]

    def begin(layer, carry):
        coupling = fields_ref[0, layer]
        diagonal = fields_ref[1, layer] + coupling * stencil(held_ref.at[0], layer, rows)
        root = jnp.sqrt(diagonal)
        inverse = 1.0 / root
        factor = coupling * inverse
        source = fields_ref[2, layer] + term * jnp.where(layer == edge_ref[0], 1.0, 0.0)
        vector = source * inverse
        scale_ref[0, layer] = inverse
        scale_ref[1, layer] = root
        factor_ref[layer] = factor
        basis_ref[0, layer] = vector
        held_ref[1, layer + 1, inner] = factor * vector
        return carry

    lax.fori_loop(0, layers, begin, 0, unroll=2)
    for k in range(ITERS):
        source_side = (k + 1) % 2

        def apply(layer, carry, k=k, source_side=source_side):
            factor = factor_ref[layer]
            spread = stencil(held_ref.at[source_side], layer, rows)
            vector = (1.0 - SHIFTS[k]) * basis_ref[k, layer] - factor * spread
            basis_ref[k + 1, layer] = vector
            if k + 1 < ITERS:
                held_ref[1 - source_side, layer + 1, inner] = factor * vector
            return carry

        lax.fori_loop(0, layers, apply, 0, unroll=2)

    lane = lanes_of(SUBLANES)
    width = LANES - LANES // 4 - 2 * HALO
    own = (lane >= HALO) & (lane < HALO + width)
    gram_ref[...] = jnp.zeros(gram_ref.shape, jnp.float32)

    def products(g, carry):
        sums = [None] * len(PAIRS)
        for n in range(2):
            for d in range(rows // SUBLANES):
                vectors = [basis_ref[k, 2 * g + n, pl.ds(SUBLANES * d, SUBLANES)] for k in range(ITERS + 1)]
                masked = [jnp.where(own, vector, 0.0) for vector in vectors]
                for p, (i, j) in enumerate(PAIRS):
                    product = masked[j] * vectors[i]
                    sums[p] = product if sums[p] is None else sums[p] + product
        for p in range(len(PAIRS)):
            high, low = add_pairs(gram_ref[0, p], gram_ref[1, p], sums[p], 0.0)
            gram_ref[0, p] = high
            gram_ref[1, p] = low
        return carry

    lax.fori_loop(0, layers // 2, products, 0)
    high, low = gram_ref[0, :, 0], gram_ref[1, :, 0]
    for row in range(1, SUBLANES):
        high, low = add_pairs(high, low, gram_ref[0, :, row], gram_ref[1, :, row])
    turn = LANES // 2
    while turn:
        high, low = add_pairs(high, low, pltpu.roll(high, turn, 1), pltpu.roll(low, turn, 1))
        turn //= 2
    packed = high[:SUBLANES]
    share = LANES // 4
    for g in range(4):
        part = slice(SUBLANES * g, SUBLANES * (g + 1))
        if g:
            packed = jnp.where(lane >= share * g, high[part], packed)
        packed = jnp.where((lane >= share * g + share // 2) & (lane < share * (g + 1)), low[part], packed)
    for d in range(sums_ref.shape[0]):
        sums_ref[d] = packed


def tree_sum(terms):
    while len(terms) > 1:
        terms = [sum(terms[i : i + 2]) for i in range(0, len(terms), 2)]
    return terms[0]


def quadratic(gram, left, right):
    products = []
    for i, a in enumerate(left):
        inside = [gram[max(i, j), min(i, j)] * b for j, b in enumerate(right)]
        products.append(a * tree_sum(inside))
    return tree_sum(products)


def iterate(gram):
    one = jnp.ones_like(gram[0, 0])
    zero = jnp.zeros_like(one)
    residual, direction, answer = [one], [one], []
    norm = gram[0, 0]
    for iteration in range(ITERS):
        applied = [SHIFTS[k] * c if SHIFTS[k] else zero for k, c in enumerate(direction)] + [zero]
        for k, c in enumerate(direction):
            applied[k + 1] = applied[k + 1] + c
        curve = quadratic(gram, direction, applied)
        step = norm / curve
        answer = [a + step * c for a, c in zip(answer + [zero], direction)]
        residual = [r - step * c for r, c in zip(residual + [zero], applied)]
        if iteration + 1 < ITERS:
            following = quadratic(gram, residual, residual)
            ratio = following / norm
            direction = [r + ratio * c for r, c in zip(residual, direction + [zero])]
            norm = following
    return answer, residual


def combine_kernel(sums_ref, basis_ref, scale_ref, out_ref, gram_ref):
    layers, rows = basis_ref.shape[1:3]
    share = LANES // 4
    parts = [(sums_ref[d], pltpu.roll(sums_ref[d], LANES - share // 2, 1)) for d in range(sums_ref.shape[0])]
    while len(parts) > 1:
        parts = [add_pairs(*parts[i], *parts[i + 1]) if i + 1 < len(parts) else parts[i] for i in range(0, len(parts), 2)]
    gram_ref[...] = parts[0][0] + parts[0][1]
    gram = {
        pair: gram_ref[pl.ds(p % SUBLANES, 1), pl.ds(share * (p // SUBLANES), 1)] for p, pair in enumerate(PAIRS)
    }
    answer, residual = iterate(gram)
    answer = [jnp.broadcast_to(c, (SUBLANES, LANES)) for c in answer]
    residual = [jnp.broadcast_to(c, (SUBLANES, LANES)) for c in residual]
    half = LANES // 2
    lane = lanes_of(SUBLANES)

    def step(layer, carry):
        for d in range(rows // SUBLANES):
            part = pl.ds(SUBLANES * d, SUBLANES)
            vectors = [basis_ref[k, layer, part] for k in range(ITERS + 1)]
            first = tree_sum([c * v for c, v in zip(answer, vectors)]) * scale_ref[0, layer, part]
            second = tree_sum([c * v for c, v in zip(residual, vectors)]) * scale_ref[1, layer, part]
            out_ref[d, layer] = jnp.where(
                lane < half, pltpu.roll(first, LANES - HALO, 1), pltpu.roll(second, half - HALO, 1)
            )
        return carry

    lax.fori_loop(0, layers, step, 0, unroll=2)


def finish_kernel(got_ref, solution_ref, residual_ref):
    count, layers = got_ref.shape[:2]
    half = LANES // 2
    lane = lanes_of(SUBLANES)

    def step(layer, carry):
        for p in range(count // 2):
            left, right = got_ref[2 * p, layer], got_ref[2 * p + 1, layer]
            place = pl.ds(LANES * p, LANES)
            solution_ref[0, layer, :, place] = jnp.where(lane < half, left, pltpu.roll(right, half, 1))
            residual_ref[0, layer, :, place] = jnp.where(lane < half, pltpu.roll(left, half, 1), right)
        return carry

    lax.fori_loop(0, layers, step, 0, unroll=4)


def call(kernel, outs, specs, *args, scratch=(), limit=24):
    return pl.pallas_call(
        kernel,
        name=kernel.__name__,
        out_shape=[jax.ShapeDtypeStruct(shape, jnp.float32) for shape in outs],
        in_specs=[pl.BlockSpec(memory_space=pltpu.SMEM)] * specs
        + [pl.BlockSpec(memory_space=pltpu.VMEM)] * (len(args) - specs),
        out_specs=[pl.BlockSpec(memory_space=pltpu.VMEM)] * len(outs),
        scratch_shapes=[pltpu.VMEM(shape, jnp.float32) for shape in scratch],
        compiler_params=pltpu.CompilerParams(vmem_limit_bytes=limit * 2**20),
    )(*args)


def in_windows(forcing, conduct, diag_add, ice_mask, grounded):
    _, layers, block_x, block_y = forcing.shape
    count_x, count_y = lax.axis_size("gx"), lax.axis_size("gy")
    rows = count_x * block_x
    group = lax.axis_index("group").astype(jnp.int32)
    place = lax.axis_index("gy")
    edge = jnp.where(group == 0, 0, layers - 1).astype(jnp.int32)[None]
    inside = jnp.stack([place > 0, place < count_y - 1]).astype(jnp.float32)
    rim = (3, layers * HALO // LANES, block_x, LANES)
    fields, low, high = call(
        prepare_kernel, [(3, layers, block_x, block_y), rim, rim], 1,
        group[None], forcing, conduct, diag_add, ice_mask, grounded,
    )
    before = lax.ppermute(high, "gy", ring(count_y, 1))
    after = lax.ppermute(low, "gy", ring(count_y, -1))
    (packed,) = call(
        pack_kernel, [(count_x, 3, layers // 4, 3, block_x, LANES)], 1, inside, fields, before, after
    )
    got = lax.all_to_all(packed, "gx", 0, 0, tiled=True)
    windows, shared = call(
        unpack_kernel, [(3, layers, rows, LANES), (2, rows, LANES)], 1, edge, got
    )
    received = from_partner(shared, "group", 0)
    padded = rows + 2 * SUBLANES
    basis, scale, sums = call(
        krylov_kernel,
        [(ITERS + 1, layers, rows, LANES), (2, layers, rows, LANES), (count_x * count_y, SUBLANES, LANES)],
        1, edge, windows, received,
        scratch=[(2, layers + 2, padded, LANES), (layers, rows, LANES), (2, 32, SUBLANES, LANES)],
        limit=32,
    )
    sums = lax.all_to_all(sums, ("gx", "gy"), 0, 0, tiled=True)
    (mixed,) = call(
        combine_kernel, [(count_x, layers, block_x, LANES)], 0, sums, basis, scale,
        scratch=[(SUBLANES, LANES)],
    )
    mixed = lax.all_to_all(mixed, "gx", 0, 0, tiled=True)
    return tuple(call(finish_kernel, [forcing.shape, forcing.shape], 0, mixed))


def fits_windows(layers, block_x, block_y, count_x):
    width = block_y // count_x
    return (
        layers % (LANES // HALO) == 0
        and block_x == SUBLANES
        and block_y % LANES == 0
        and 2 * width == LANES
        and HALO >= 2 * (ITERS + 1)
    )


def per_device(forcing, conduct, diag_add, ice_mask, grounded):
    _, layers, block_x, block_y = forcing.shape
    way = in_windows if fits_windows(layers, block_x, block_y, lax.axis_size("gx")) else on_device
    return way(forcing, conduct, diag_add, ice_mask, grounded)


def solution(mesh):
    in_specs = (
        P("group", None, "gx", "gy"),
        P("group", None, "gx", "gy"),
        P("group", None, "gx", "gy"),
        P("gx", "gy"),
        P("gx", "gy"),
    )
    out_specs = (P("group", None, "gx", "gy"), P("group", None, "gx", "gy"))
    return jax.shard_map(
        per_device, mesh=mesh, in_specs=in_specs, out_specs=out_specs, check_vma=False
    )
```

profile of v0, /device:TPU:0, one launch (start us, length us, event | category | flops | bytes accessed | tf_op | source)
XLA Modules:
  0.0 143.9 jit_solution(3017910967154054322)
XLA Ops:
  0.6 0.0 copy-start.1
  0.6 1.1 copy-done.1
  1.7 1.0 copy-done.2
  2.7 1.0 copy-done.3
  3.7 0.7 copy-done.4
  4.4 0.7 copy-done.5
  5.1 1.1 prepare_kernel.1
  6.2 3.1 %collective-permute-start = (f32[3,10,8,128]{3,2,1,0:T(8,128)S(1)}, f32[3,10,8,128]{3,2,1,0:T(8,128)S(1)}, u32[]{:S(2)}, u32[]{:S(2)}) collective-permute-start(f32[3,10,8,128]{3,2,1,0:T(8,128)S(1)} %get-tuple-element.11), channel_id=1, source_target_pairs={{0,1},{1,2},{2,3},{3,0},{4,5},{5,6},{6,7},{7,4},{8,9},{9,10},{10,1... | collective-permute-start | bytes 368648 | tf_op jit(solution)/shard_map/ppermute | solution.py:489
  9.3 2.1 %collective-permute-start.1 = (f32[3,10,8,128]{3,2,1,0:T(8,128)S(1)}, f32[3,10,8,128]{3,2,1,0:T(8,128)S(1)}, u32[]{:S(2)}, u32[]{:S(2)}) collective-permute-start(f32[3,10,8,128]{3,2,1,0:T(8,128)S(1)} %get-tuple-element.12), channel_id=1, source_target_pairs={{0,3},{1,0},{2,1},{3,2},{4,7},{5,4},{6,5},{7,6},{8,11},{9,8},{10,9... | collective-permute-start | bytes 368648 | tf_op jit(solution)/shard_map/ppermute | solution.py:490
  11.3 0.1 add_convert_fusion.edge_ref
  11.4 4.0 %collective-permute-done.low_ref = f32[3,10,8,128]{3,2,1,0:T(8,128)S(1)} collective-permute-done((f32[3,10,8,128]{3,2,1,0:T(8,128)S(1)}, f32[3,10,8,128]{3,2,1,0:T(8,128)S(1)}, u32[]{:S(2)}, u32[]{:S(2)}) %collective-permute-start) | collective-permute-done | bytes 122912 | tf_op jit(solution)/shard_map/ppermute | solution.py:489
  15.5 1.2 collective-permute-done.1.high_ref
  16.7 9.0 %pack_kernel.1 = f32[4,3,20,3,8,128]{5,4,3,2,1,0:T(8,128)S(1)} custom-call(f32[2]{0:T(128)S(1)} %add_convert_fusion.edge_ref, f32[3,80,8,256]{3,2,1,0:T(8,128)S(1)} %get-tuple-element.10.fields_ref, f32[3,10,8,128]{3,2,1,0:T(8,128)S(1)} %collective-permute-done.low_ref, f32[3,10,8,128]{3,2,1,0:T(8,128)S(1)} %collective-permute-done.1.high_ref), custom_call_target="tpu_custom_call" | custom-call | tf_op jit(solution)/shard_map/pack_kernel/pallas_call | solution.py:464
  25.7 1.6 %copy-done = f32[4,3,20,3,8,128]{5,4,3,2,1,0:T(8,128)} copy-done((f32[4,3,20,3,8,128]{5,4,3,2,1,0:T(8,128)}, f32[4,3,20,3,8,128]{5,4,3,2,1,0:T(8,128)S(1)}, u32[]{:S(2)}) %copy-start) | copy-done | bytes 2949144
  27.3 3.7 %all-to-all-start = ((f32[4,3,20,3,8,128]{5,4,3,2,1,0:T(8,128)}), f32[4,3,20,3,8,128]{5,4,3,2,1,0:T(8,128)S(1)}, u32[]{:S(2)}, u32[]{:S(2)}) async-start(f32[4,3,20,3,8,128]{5,4,3,2,1,0:T(8,128)} %copy-done), calls=%async_computation | async-start | bytes 5898240 | tf_op jit(solution)/shard_map/all_to_all | solution.py:494
  31.0 33.8 %all-to-all-done.got_ref = f32[4,3,20,3,8,128]{5,4,3,2,1,0:T(8,128)S(1)} async-done(((f32[4,3,20,3,8,128]{5,4,3,2,1,0:T(8,128)}), f32[4,3,20,3,8,128]{5,4,3,2,1,0:T(8,128)S(1)}, u32[]{:S(2)}, u32[]{:S(2)}) %all-to-all-start) | async-done | bytes 2949152 | tf_op jit(solution)/shard_map/all_to_all | solution.py:494
  64.8 3.7 %unpack_kernel.1 = (f32[3,80,32,128]{3,2,1,0:T(8,128)S(1)}, f32[2,32,128]{2,1,0:T(8,128)S(1)}) custom-call(s32[1]{0:T(128)} %bitcast.edge_ref, f32[4,3,20,3,8,128]{5,4,3,2,1,0:T(8,128)S(1)} %all-to-all-done.got_ref), custom_call_target="tpu_custom_call" | custom-call | tf_op jit(solution)/shard_map/unpack_kernel/pallas_call | solution.py:464
  68.5 0.1 collective-permute-start.2
  68.6 1.2 collective-permute-done.2.got_ref
  69.8 35.6 %krylov_kernel.1 = (f32[7,80,32,128]{3,2,1,0:T(8,128)S(1)}, f32[2,80,32,128]{3,2,1,0:T(8,128)S(1)}, f32[16,8,128]{2,1,0:T(8,128)S(1)}) custom-call(s32[1]{0:T(128)} %bitcast.edge_ref, f32[3,80,32,128]{3,2,1,0:T(8,128)S(1)} %get-tuple-element.13.fields_ref, f32[2,32,128]{2,1,0:T(8,128)S(1)} %collective-permute-done.2.got_ref), custom_call_target="tpu_custom_call" | custom-call | tf_op jit(solution)/shard_map/krylov_kernel/pallas_call | solution.py:464
  105.4 11.7 %all_to_all.15.sums_ref = f32[16,8,128]{2,1,0:T(8,128)S(1)} all-to-all(f32[16,8,128]{2,1,0:T(8,128)S(1)} %get-tuple-element.15), channel_id=1, replica_groups=mesh['group'=2,'gx'=4,'gy'=4] {'gx','gy'}, dimensions={0} | all-to-all | bytes 131072 | tf_op jit(solution)/shard_map/all_to_all | solution.py:507
  117.1 5.5 %combine_kernel.1 = f32[4,80,8,128]{3,2,1,0:T(8,128)S(1)} custom-call(f32[16,8,128]{2,1,0:T(8,128)S(1)} %all_to_all.15.sums_ref, f32[7,80,32,128]{3,2,1,0:T(8,128)S(1)} %get-tuple-element.16.basis_ref, f32[2,80,32,128]{3,2,1,0:T(8,128)S(1)} %get-tuple-element.17.scale_ref), custom_call_target="tpu_custom_call" | custom-call | tf_op jit(solution)/shard_map/combine_kernel/pallas_call | solution.py:464
  122.6 18.6 %all_to_all.16.got_ref = f32[4,80,8,128]{3,2,1,0:T(8,128)S(1)} all-to-all(f32[4,80,8,128]{3,2,1,0:T(8,128)S(1)} %combine_kernel.1), channel_id=1, replica_groups=mesh['group'=2,'gx'=4,'gy'=4] {'gx'}, dimensions={0} | all-to-all | bytes 2621440 | tf_op jit(solution)/shard_map/all_to_all | solution.py:512
  141.2 2.7 %finish_kernel.1 = (f32[1,80,8,256]{3,2,1,0:T(8,128)}, f32[1,80,8,256]{3,2,1,0:T(8,128)}) custom-call(f32[4,80,8,128]{3,2,1,0:T(8,128)S(1)} %all_to_all.16.got_ref), custom_call_target="tpu_custom_call" | custom-call | tf_op jit(solution)/shard_map/finish_kernel/pallas_call | solution.py:464
  (5 shorter events, 0.0 us)
Async XLA Ops:
  0.6 1.1 copy-start.1
  1.7 1.0 copy-start.2
  2.7 1.0 copy-start.3
  3.7 0.7 copy-start.4
  4.4 0.7 copy-start.5
  6.2 9.3 %collective-permute-start = (f32[3,10,8,128]{3,2,1,0:T(8,128)S(1)}, f32[3,10,8,128]{3,2,1,0:T(8,128)S(1)}, u32[]{:S(2)}, u32[]{:S(2)}) collective-permute-start(f32[3,10,8,128]{3,2,1,0:T(8,128)S(1)} %get-tuple-element.11), channel_id=1, source_target_pairs={{0,1},{1,2},{2,3},{3,0},{4,5},{5,6},{6,7},{7,4},{8,9},{9,10},{10,1... | collective-permute-start | bytes 368648 | tf_op jit(solution)/shard_map/ppermute | solution.py:489
  9.3 7.4 %collective-permute-start.1 = (f32[3,10,8,128]{3,2,1,0:T(8,128)S(1)}, f32[3,10,8,128]{3,2,1,0:T(8,128)S(1)}, u32[]{:S(2)}, u32[]{:S(2)}) collective-permute-start(f32[3,10,8,128]{3,2,1,0:T(8,128)S(1)} %get-tuple-element.12), channel_id=1, source_target_pairs={{0,3},{1,0},{2,1},{3,2},{4,7},{5,4},{6,5},{7,6},{8,11},{9,8},{10,9... | collective-permute-start | bytes 368648 | tf_op jit(solution)/shard_map/ppermute | solution.py:490
  25.7 1.6 %copy-start = (f32[4,3,20,3,8,128]{5,4,3,2,1,0:T(8,128)}, f32[4,3,20,3,8,128]{5,4,3,2,1,0:T(8,128)S(1)}, u32[]{:S(2)}) copy-start(f32[4,3,20,3,8,128]{5,4,3,2,1,0:T(8,128)S(1)} %pack_kernel.1) | copy-start | bytes 8847364
  27.3 37.5 %all-to-all-start = ((f32[4,3,20,3,8,128]{5,4,3,2,1,0:T(8,128)}), f32[4,3,20,3,8,128]{5,4,3,2,1,0:T(8,128)S(1)}, u32[]{:S(2)}, u32[]{:S(2)}) async-start(f32[4,3,20,3,8,128]{5,4,3,2,1,0:T(8,128)} %copy-done), calls=%async_computation | async-start | bytes 5898240 | tf_op jit(solution)/shard_map/all_to_all | solution.py:494
  68.5 1.3 collective-permute-start.2
where the time goes:
time: 144 us
  Pallas kernels  57.6 us (40%)
  waiting for transfers between devices  40.3 us (28%)
  blocking collectives  30.3 us (21%)
  starting transfers between devices  8.98 us (6%)
  local copies, waits for them, and re-layouts  6.01 us (4%)
    pallas_call x6, Pallas kernels, call(): pl.pallas_call(kernel, name=kernel.__name__, out_shape=[jax.ShapeDtypeStr...  57.6 us
    all_to_all x1, waiting for transfers between devices, in_windows(): got = lax.all_to_all(packed, 'gx', 0, 0, tiled=True)  33.8 us
    all_to_all x1, blocking collectives, in_windows(): mixed = lax.all_to_all(mixed, 'gx', 0, 0, tiled=True)  18.6 us
    all_to_all x1, blocking collectives, in_windows(): sums = lax.all_to_all(sums, ('gx', 'gy'), 0, 0, tiled=True)  11.7 us
    unnamed x12, local copies, waits for them, and re-layouts  6.01 us
    ppermute x1, waiting for transfers between devices, in_windows(): before = lax.ppermute(high, 'gy', ring(count_y, 1))  4.03 us
    all_to_all x1, starting transfers between devices, in_windows(): got = lax.all_to_all(packed, 'gx', 0, 0, tiled=True)  3.72 us
    ppermute x1, starting transfers between devices, in_windows(): before = lax.ppermute(high, 'gy', ring(count_y, 1))  3.1 us
  transfers between devices with their start and end apart: 4, of which 4 were waited for; matrix products, arithmetic and copies ran while one was open for 0% of the time, Pallas kernels for 0%

commit v1 on v0

--- a/solution.py
+++ b/solution.py
@@ -12,6 +12,7 @@
 SUBLANES = 8
 HALO = 16
 SHIFTS = (0.0, 0.75, 1.5, 0.25, 1.75, 1.0)
+UNROLL = 8
 PAIRS = tuple((i, j) for i in range(ITERS + 1) for j in range(i + 1) if j < ITERS)
 
 
@@ -292,75 +293,95 @@
     return beside + vertical_weight * above
 
 
-def krylov_kernel(edge_ref, fields_ref, got_ref, basis_ref, scale_ref, sums_ref, held_ref, factor_ref, gram_ref):
+def blocks(total, size, body):
+    def step(g, carry):
+        body(g * size)
+        return carry
+
+    lax.fori_loop(0, total // size, step, 0)
+
+
+def krylov_kernel(edge_ref, fields_ref, got_ref, *refs):
+    basis = refs[: ITERS + 1]
+    scale_ref, sums_ref, even_ref, odd_ref, factor_ref, gram_ref = refs[ITERS + 1 :]
+    held = (even_ref, odd_ref)
     layers, rows = fields_ref.shape[1:3]
     inner = pl.ds(SUBLANES, rows)
     empty = jnp.zeros((layers + 2, SUBLANES, LANES), jnp.float32)
-    for side in range(2):
-        held_ref[side, :, :SUBLANES] = empty
-        held_ref[side, :, SUBLANES + rows :] = empty
-        held_ref[side, 0] = jnp.zeros((rows + 2 * SUBLANES, LANES), jnp.float32)
-        held_ref[side, layers + 1] = jnp.zeros((rows + 2 * SUBLANES, LANES), jnp.float32)
-
-    def fill(layer, carry):
-        held_ref[0, layer + 1, inner] = fields_ref[0, layer]
-        return carry
-
-    lax.fori_loop(0, layers, fill, 0, unroll=4)
+    for ref in held:
+        ref[:, :SUBLANES] = empty
+        ref[:, SUBLANES + rows :] = empty
+        ref[0] = jnp.zeros((rows + 2 * SUBLANES, LANES), jnp.float32)
+        ref[layers + 1] = jnp.zeros((rows + 2 * SUBLANES, LANES), jnp.float32)
+
+    def fill(first):
+        for layer in range(8):
+            even_ref[first + layer + 1, inner] = fields_ref[0, first + layer]
+
+    blocks(layers, 8, fill)
     active = jnp.where(fields_ref[0, 0] > 0.0, 1.0, 0.0)
     term = active * got_ref[1] * got_ref[0]
 
-    def begin(layer, carry):
-        coupling = fields_ref[0, layer]
-        diagonal = fields_ref[1, layer] + coupling * stencil(held_ref.at[0], layer, rows)
-        root = jnp.sqrt(diagonal)
-        inverse = 1.0 / root
-        factor = coupling * inverse
-        source = fields_ref[2, layer] + term * jnp.where(layer == edge_ref[0], 1.0, 0.0)
-        vector = source * inverse
-        scale_ref[0, layer] = inverse
-        scale_ref[1, layer] = root
-        factor_ref[layer] = factor
-        basis_ref[0, layer] = vector
-        held_ref[1, layer + 1, inner] = factor * vector
-        return carry
-
-    lax.fori_loop(0, layers, begin, 0, unroll=2)
+    def begin(first):
+        for layer in range(UNROLL):
+            layer = first + layer
+            coupling = fields_ref[0, layer]
+            diagonal = fields_ref[1, layer] + coupling * stencil(even_ref, layer, rows)
+            root = jnp.sqrt(diagonal)
+            inverse = 1.0 / root
+            factor = coupling * inverse
+            source = fields_ref[2, layer] + term * jnp.where(layer == edge_ref[0], 1.0, 0.0)
+            vector = source * inverse
+            scale_ref[0, layer] = inverse
+            scale_ref[1, layer] = root
+            factor_ref[layer] = factor
+            basis[0][layer] = vector
+            odd_ref[layer + 1, inner] = factor * vector
+
+    blocks(layers, UNROLL, begin)
     for k in range(ITERS):
-        source_side = (k + 1) % 2
-
-        def apply(layer, carry, k=k, source_side=source_side):
-            factor = factor_ref[layer]
-            spread = stencil(held_ref.at[source_side], layer, rows)
-            vector = (1.0 - SHIFTS[k]) * basis_ref[k, layer] - factor * spread
-            basis_ref[k + 1, layer] = vector
-            if k + 1 < ITERS:
-                held_ref[1 - source_side, layer + 1, inner] = factor * vector
-            return carry
-
-        lax.fori_loop(0, layers, apply, 0, unroll=2)
+        source_ref, target_ref = held[(k + 1) % 2], held[k % 2]
+
+        def apply(first):
+            for layer in range(UNROLL):
+                layer = first + layer
+                factor = factor_ref[layer]
+                spread = stencil(source_ref, layer, rows)
+                before = basis[k][layer]
+                before = (1.0 - SHIFTS[k]) * before if SHIFTS[k] else before
+                vector = before - factor * spread
+                basis[k + 1][layer] = vector
+                if k + 1 < ITERS:
+                    target_ref[layer + 1, inner] = factor * vector
+
+        blocks(layers, UNROLL, apply)
 
     lane = lanes_of(SUBLANES)
-    width = LANES - LANES // 4 - 2 * HALO
-    own = (lane >= HALO) & (lane < HALO + width)
+    half = LANES // 2
     gram_ref[...] = jnp.zeros(gram_ref.shape, jnp.float32)
 
-    def products(g, carry):
+    def products(first):
         sums = [None] * len(PAIRS)
-        for n in range(2):
+        for n in range(0, 4, 2):
             for d in range(rows // SUBLANES):
-                vectors = [basis_ref[k, 2 * g + n, pl.ds(SUBLANES * d, SUBLANES)] for k in range(ITERS + 1)]
-                masked = [jnp.where(own, vector, 0.0) for vector in vectors]
+                part = pl.ds(SUBLANES * d, SUBLANES)
+                vectors = [
+                    jnp.where(
+                        lane < half,
+                        pltpu.roll(ref[first + n, part], LANES - HALO, 1),
+                        pltpu.roll(ref[first + n + 1, part], half - HALO, 1),
+                    )
+                    for ref in basis
+                ]
                 for p, (i, j) in enumerate(PAIRS):
-                    product = masked[j] * vectors[i]
+                    product = vectors[j] * vectors[i]
                     sums[p] = product if sums[p] is None else sums[p] + product
         for p in range(len(PAIRS)):
             high, low = add_pairs(gram_ref[0, p], gram_ref[1, p], sums[p], 0.0)
             gram_ref[0, p] = high
             gram_ref[1, p] = low
-        return carry
-
-    lax.fori_loop(0, layers // 2, products, 0)
+
+    blocks(layers, 4, products)
     high, low = gram_ref[0, :, 0], gram_ref[1, :, 0]
     for row in range(1, SUBLANES):
         high, low = add_pairs(high, low, gram_ref[0, :, row], gram_ref[1, :, row])
@@ -414,8 +435,10 @@
     return answer, residual
 
 
-def combine_kernel(sums_ref, basis_ref, scale_ref, out_ref, gram_ref):
-    layers, rows = basis_ref.shape[1:3]
+def combine_kernel(sums_ref, *refs):
+    basis = refs[: ITERS + 1]
+    scale_ref, out_ref, gram_ref = refs[ITERS + 1 :]
+    layers, rows = scale_ref.shape[1:3]
     share = LANES // 4
     parts = [(sums_ref[d], pltpu.roll(sums_ref[d], LANES - share // 2, 1)) for d in range(sums_ref.shape[0])]
     while len(parts) > 1:
@@ -430,34 +453,31 @@
     half = LANES // 2
     lane = lanes_of(SUBLANES)
 
-    def step(layer, carry):
-        for d in range(rows // SUBLANES):
-            part = pl.ds(SUBLANES * d, SUBLANES)
-            vectors = [basis_ref[k, layer, part] for k in range(ITERS + 1)]
-            first = tree_sum([c * v for c, v in zip(answer, vectors)]) * scale_ref[0, layer, part]
-            second = tree_sum([c * v for c, v in zip(residual, vectors)]) * scale_ref[1, layer, part]
-            out_ref[d, layer] = jnp.where(
-                lane < half, pltpu.roll(first, LANES - HALO, 1), pltpu.roll(second, half - HALO, 1)
-            )
-        return carry
-
-    lax.fori_loop(0, layers, step, 0, unroll=2)
+    def mix(first):
+        for layer in range(UNROLL):
+            layer = first + layer
+            for d in range(rows // SUBLANES):
+                part = pl.ds(SUBLANES * d, SUBLANES)
+                vectors = [ref[layer, part] for ref in basis]
+                answered = tree_sum([c * v for c, v in zip(answer, vectors)]) * scale_ref[0, layer, part]
+                left = tree_sum([c * v for c, v in zip(residual, vectors)]) * scale_ref[1, layer, part]
+                out_ref[d, layer] = jnp.where(
+                    lane < half, pltpu.roll(answered, LANES - HALO, 1), pltpu.roll(left, half - HALO, 1)
+                )
+
+    blocks(layers, UNROLL, mix)
 
 
 def finish_kernel(got_ref, solution_ref, residual_ref):
     count, layers = got_ref.shape[:2]
     half = LANES // 2
     lane = lanes_of(SUBLANES)
-
-    def step(layer, carry):
+    for layer in range(layers):
         for p in range(count // 2):
             left, right = got_ref[2 * p, layer], got_ref[2 * p + 1, layer]
             place = pl.ds(LANES * p, LANES)
             solution_ref[0, layer, :, place] = jnp.where(lane < half, left, pltpu.roll(right, half, 1))
             residual_ref[0, layer, :, place] = jnp.where(lane < half, pltpu.roll(left, half, 1), right)
-        return carry
-
-    lax.fori_loop(0, layers, step, 0, unroll=4)
 
 
 def call(kernel, outs, specs, *args, scratch=(), limit=24):
@@ -497,20 +517,33 @@
     )
     received = from_partner(shared, "group", 0)
     padded = rows + 2 * SUBLANES
-    basis, scale, sums = call(
+    window = (layers, rows, LANES)
+    *basis, scale, sums = call(
         krylov_kernel,
-        [(ITERS + 1, layers, rows, LANES), (2, layers, rows, LANES), (count_x * count_y, SUBLANES, LANES)],
+        [window] * (ITERS + 1) + [(2,) + window, (count_x * count_y, SUBLANES, LANES)],
         1, edge, windows, received,
-        scratch=[(2, layers + 2, padded, LANES), (layers, rows, LANES), (2, 32, SUBLANES, LANES)],
+        scratch=[(layers + 2, padded, LANES)] * 2 + [window, (2, 32, SUBLANES, LANES)],
         limit=32,
     )
     sums = lax.all_to_all(sums, ("gx", "gy"), 0, 0, tiled=True)
     (mixed,) = call(
-        combine_kernel, [(count_x, layers, block_x, LANES)], 0, sums, basis, scale,
+        combine_kernel, [(count_x, layers, block_x, LANES)], 0, sums, *basis, scale,
         scratch=[(SUBLANES, LANES)],
     )
     mixed = lax.all_to_all(mixed, "gx", 0, 0, tiled=True)
-    return tuple(call(finish_kernel, [forcing.shape, forcing.shape], 0, mixed))
+    steps = 4
+    part = pl.BlockSpec((1, layers // steps, block_x, block_y), lambda i: (0, i, 0, 0))
+    return tuple(
+        pl.pallas_call(
+            finish_kernel,
+            name="finish_kernel",
+            grid=(steps,),
+            out_shape=[jax.ShapeDtypeStruct(forcing.shape, jnp.float32)] * 2,
+            in_specs=[pl.BlockSpec((count_x, layers // steps, block_x, LANES), lambda i: (0, i, 0, 0))],
+            out_specs=[part, part],
+            compiler_params=pltpu.CompilerParams(vmem_limit_bytes=24 * 2**20),
+        )(mixed)
+    )
 
 
 def fits_windows(layers, block_x, block_y, count_x):

time: 144 us -> 126 us (0.88)
  Pallas kernels: 57.6 us -> 39.5 us
    pallas_call x6 -> x5, Pallas kernels: 57.6 us -> 37.5 us  [call(): pl.pallas_call(kernel, name=kernel.__name__, out_shape=[jax.ShapeDtypeStr...]
    pallas_call x0 -> x1, Pallas kernels: none -> 2 us  [in_windows(): pl.pallas_call(finish_kernel, name='finish_kernel', grid=(steps,), out_sh...]
where the time goes in v1:
time: 126 us
  waiting for transfers between devices  40.3 us (32%)
  Pallas kernels  39.5 us (31%)
  blocking collectives  30.3 us (24%)
  starting transfers between devices  8.98 us (7%)
  local copies, waits for them, and re-layouts  6.01 us (5%)
    pallas_call x5, Pallas kernels, call(): pl.pallas_call(kernel, name=kernel.__name__, out_shape=[jax.ShapeDtypeStr...  37.5 us
    all_to_all x1, waiting for transfers between devices, in_windows(): got = lax.all_to_all(packed, 'gx', 0, 0, tiled=True)  33.8 us
    all_to_all x1, blocking collectives, in_windows(): mixed = lax.all_to_all(mixed, 'gx', 0, 0, tiled=True)  18.6 us
    all_to_all x1, blocking collectives, in_windows(): sums = lax.all_to_all(sums, ('gx', 'gy'), 0, 0, tiled=True)  11.7 us
    unnamed x12, local copies, waits for them, and re-layouts  6.01 us
    ppermute x1, waiting for transfers between devices, in_windows(): before = lax.ppermute(high, 'gy', ring(count_y, 1))  4.03 us
    all_to_all x1, starting transfers between devices, in_windows(): got = lax.all_to_all(packed, 'gx', 0, 0, tiled=True)  3.72 us
    ppermute x1, starting transfers between devices, in_windows(): before = lax.ppermute(high, 'gy', ring(count_y, 1))  3.1 us
  transfers between devices with their start and end apart: 4, of which 4 were waited for; matrix products, arithmetic and copies ran while one was open for 0% of the time, Pallas kernels for 0%

profile of v1, /device:TPU:0, one launch (start us, length us, event | category | flops | bytes accessed | tf_op | source)
XLA Modules:
  0.0 125.8 jit_solution(10000344076479336952)
XLA Ops:
  0.6 0.0 copy-start.1
  0.6 1.1 copy-done.1
  1.7 1.0 copy-done.2
  2.7 1.0 copy-done.3
  3.7 0.7 copy-done.4
  4.4 0.7 copy-done.5
  5.1 1.1 prepare_kernel.1
  6.2 3.1 %collective-permute-start = (f32[3,10,8,128]{3,2,1,0:T(8,128)S(1)}, f32[3,10,8,128]{3,2,1,0:T(8,128)S(1)}, u32[]{:S(2)}, u32[]{:S(2)}) collective-permute-start(f32[3,10,8,128]{3,2,1,0:T(8,128)S(1)} %get-tuple-element.17), channel_id=1, source_target_pairs={{0,1},{1,2},{2,3},{3,0},{4,5},{5,6},{6,7},{7,4},{8,9},{9,10},{10,1... | collective-permute-start | bytes 368648 | tf_op jit(solution)/shard_map/ppermute | solution.py:509
  9.3 2.1 %collective-permute-start.1 = (f32[3,10,8,128]{3,2,1,0:T(8,128)S(1)}, f32[3,10,8,128]{3,2,1,0:T(8,128)S(1)}, u32[]{:S(2)}, u32[]{:S(2)}) collective-permute-start(f32[3,10,8,128]{3,2,1,0:T(8,128)S(1)} %get-tuple-element.18), channel_id=1, source_target_pairs={{0,3},{1,0},{2,1},{3,2},{4,7},{5,4},{6,5},{7,6},{8,11},{9,8},{10,9... | collective-permute-start | bytes 368648 | tf_op jit(solution)/shard_map/ppermute | solution.py:510
  11.3 0.1 add_convert_fusion.edge_ref
  11.4 4.0 %collective-permute-done.low_ref = f32[3,10,8,128]{3,2,1,0:T(8,128)S(1)} collective-permute-done((f32[3,10,8,128]{3,2,1,0:T(8,128)S(1)}, f32[3,10,8,128]{3,2,1,0:T(8,128)S(1)}, u32[]{:S(2)}, u32[]{:S(2)}) %collective-permute-start) | collective-permute-done | bytes 122912 | tf_op jit(solution)/shard_map/ppermute | solution.py:509
  15.5 1.2 collective-permute-done.1.high_ref
  16.7 9.0 %pack_kernel.1 = f32[4,3,20,3,8,128]{5,4,3,2,1,0:T(8,128)S(1)} custom-call(f32[2]{0:T(128)S(1)} %add_convert_fusion.edge_ref, f32[3,80,8,256]{3,2,1,0:T(8,128)S(1)} %get-tuple-element.16.fields_ref, f32[3,10,8,128]{3,2,1,0:T(8,128)S(1)} %collective-permute-done.low_ref, f32[3,10,8,128]{3,2,1,0:T(8,128)S(1)} %collective-permute-done.1.high_ref), custom_call_target="tpu_custom_call" | custom-call | tf_op jit(solution)/shard_map/pack_kernel/pallas_call | solution.py:484
  25.7 1.6 %copy-done = f32[4,3,20,3,8,128]{5,4,3,2,1,0:T(8,128)} copy-done((f32[4,3,20,3,8,128]{5,4,3,2,1,0:T(8,128)}, f32[4,3,20,3,8,128]{5,4,3,2,1,0:T(8,128)S(1)}, u32[]{:S(2)}) %copy-start) | copy-done | bytes 2949144
  27.3 3.7 %all-to-all-start = ((f32[4,3,20,3,8,128]{5,4,3,2,1,0:T(8,128)}), f32[4,3,20,3,8,128]{5,4,3,2,1,0:T(8,128)S(1)}, u32[]{:S(2)}, u32[]{:S(2)}) async-start(f32[4,3,20,3,8,128]{5,4,3,2,1,0:T(8,128)} %copy-done), calls=%async_computation | async-start | bytes 5898240 | tf_op jit(solution)/shard_map/all_to_all | solution.py:514
  31.0 33.8 %all-to-all-done.got_ref = f32[4,3,20,3,8,128]{5,4,3,2,1,0:T(8,128)S(1)} async-done(((f32[4,3,20,3,8,128]{5,4,3,2,1,0:T(8,128)}), f32[4,3,20,3,8,128]{5,4,3,2,1,0:T(8,128)S(1)}, u32[]{:S(2)}, u32[]{:S(2)}) %all-to-all-start) | async-done | bytes 2949152 | tf_op jit(solution)/shard_map/all_to_all | solution.py:514
  64.8 3.6 %unpack_kernel.1 = (f32[3,80,32,128]{3,2,1,0:T(8,128)S(1)}, f32[2,32,128]{2,1,0:T(8,128)S(1)}) custom-call(s32[1]{0:T(128)} %bitcast.edge_ref, f32[4,3,20,3,8,128]{5,4,3,2,1,0:T(8,128)S(1)} %all-to-all-done.got_ref), custom_call_target="tpu_custom_call" | custom-call | tf_op jit(solution)/shard_map/unpack_kernel/pallas_call | solution.py:484
  68.5 0.1 collective-permute-start.2
  68.6 1.2 collective-permute-done.2.got_ref
  69.8 20.1 %krylov_kernel.1 = (f32[80,32,128]{2,1,0:T(8,128)S(1)}, f32[80,32,128]{2,1,0:T(8,128)S(1)}, f32[80,32,128]{2,1,0:T(8,128)S(1)}, f32[80,32,128]{2,1,0:T(8,128)S(1...) custom-call(s32[1]{0:T(128)} %bitcast.edge_ref, ...), custom_call_target="tpu_custom_call" | custom-call | tf_op jit(solution)/shard_map/krylov_kernel/pallas_call | solution.py:484
  89.9 11.7 %all_to_all.15.sums_ref = f32[16,8,128]{2,1,0:T(8,128)S(1)} all-to-all(f32[16,8,128]{2,1,0:T(8,128)S(1)} %get-tuple-element.21), channel_id=1, replica_groups=mesh['group'=2,'gx'=4,'gy'=4] {'gx','gy'}, dimensions={0} | all-to-all | bytes 131072 | tf_op jit(solution)/shard_map/all_to_all | solution.py:528
  101.6 3.6 %combine_kernel.1 = f32[4,80,8,128]{3,2,1,0:T(8,128)S(1)} custom-call(f32[16,8,128]{2,1,0:T(8,128)S(1)} %all_to_all.15.sums_ref, f32[80,32,128]{2,1,0:T(8,128)S(1)} %get-tuple-element.22.refs_0_, f32[80,32,128]{2,1,0:T(8,128)S(1)} %get-tuple-element.23.refs_1_, f32[80,32,128]{2,1,0:T(8,128)S(1)} %get-tuple-element.24.refs_2_, ...), custom_call_target="tpu_custom_call" | custom-call | tf_op jit(solution)/shard_map/combine_kernel/pallas_call | solution.py:484
  105.2 18.6 %all_to_all.16.got_ref = f32[4,80,8,128]{3,2,1,0:T(8,128)S(1)} all-to-all(f32[4,80,8,128]{3,2,1,0:T(8,128)S(1)} %combine_kernel.1), channel_id=1, replica_groups=mesh['group'=2,'gx'=4,'gy'=4] {'gx'}, dimensions={0} | all-to-all | bytes 2621440 | tf_op jit(solution)/shard_map/all_to_all | solution.py:533
  123.8 2.0 %finish_kernel.1 = (f32[1,80,8,256]{3,2,1,0:T(8,128)}, f32[1,80,8,256]{3,2,1,0:T(8,128)}) custom-call(f32[4,80,8,128]{3,2,1,0:T(8,128)S(1)} %all_to_all.16.got_ref), custom_call_target="tpu_custom_call" | custom-call | tf_op jit(solution)/shard_map/finish_kernel/pallas_call | solution.py:537
  (5 shorter events, 0.0 us)
Async XLA Ops:
  0.6 1.1 copy-start.1
  1.7 1.0 copy-start.2
  2.7 1.0 copy-start.3
  3.7 0.7 copy-start.4
  4.4 0.7 copy-start.5
  6.2 9.3 %collective-permute-start = (f32[3,10,8,128]{3,2,1,0:T(8,128)S(1)}, f32[3,10,8,128]{3,2,1,0:T(8,128)S(1)}, u32[]{:S(2)}, u32[]{:S(2)}) collective-permute-start(f32[3,10,8,128]{3,2,1,0:T(8,128)S(1)} %get-tuple-element.17), channel_id=1, source_target_pairs={{0,1},{1,2},{2,3},{3,0},{4,5},{5,6},{6,7},{7,4},{8,9},{9,10},{10,1... | collective-permute-start | bytes 368648 | tf_op jit(solution)/shard_map/ppermute | solution.py:509
  9.3 7.4 %collective-permute-start.1 = (f32[3,10,8,128]{3,2,1,0:T(8,128)S(1)}, f32[3,10,8,128]{3,2,1,0:T(8,128)S(1)}, u32[]{:S(2)}, u32[]{:S(2)}) collective-permute-start(f32[3,10,8,128]{3,2,1,0:T(8,128)S(1)} %get-tuple-element.18), channel_id=1, source_target_pairs={{0,3},{1,0},{2,1},{3,2},{4,7},{5,4},{6,5},{7,6},{8,11},{9,8},{10,9... | collective-permute-start | bytes 368648 | tf_op jit(solution)/shard_map/ppermute | solution.py:510
  25.7 1.6 %copy-start = (f32[4,3,20,3,8,128]{5,4,3,2,1,0:T(8,128)}, f32[4,3,20,3,8,128]{5,4,3,2,1,0:T(8,128)S(1)}, u32[]{:S(2)}) copy-start(f32[4,3,20,3,8,128]{5,4,3,2,1,0:T(8,128)S(1)} %pack_kernel.1) | copy-start | bytes 8847364
  27.3 37.5 %all-to-all-start = ((f32[4,3,20,3,8,128]{5,4,3,2,1,0:T(8,128)}), f32[4,3,20,3,8,128]{5,4,3,2,1,0:T(8,128)S(1)}, u32[]{:S(2)}, u32[]{:S(2)}) async-start(f32[4,3,20,3,8,128]{5,4,3,2,1,0:T(8,128)} %copy-done), calls=%async_computation | async-start | bytes 5898240 | tf_op jit(solution)/shard_map/all_to_all | solution.py:514
  68.5 1.3 %collective-permute-start.2 = (f32[2,32,128]{2,1,0:T(8,128)S(1)}, f32[2,32,128]{2,1,0:T(8,128)S(1)}, u32[]{:S(2)}, u32[]{:S(2)}) collective-permute-start(f32[2,32,128]{2,1,0:T(8,128)S(1)} %get-tuple-element.20), channel_id=1, source_target_pairs={{0,16},{16,0},{1,17},{17,1},{2,18},{18,2},{3,19},{19,3},{4,20},{20... | collective-permute-start | bytes 98312 | tf_op jit(solution)/shard_map/ppermute | solution.py:56

commit v2 on v1

--- a/solution.py
+++ b/solution.py
@@ -12,7 +12,7 @@
 SUBLANES = 8
 HALO = 16
 SHIFTS = (0.0, 0.75, 1.5, 0.25, 1.75, 1.0)
-UNROLL = 8
+UNROLL = 16
 PAIRS = tuple((i, j) for i in range(ITERS + 1) for j in range(i + 1) if j < ITERS)
 
 
@@ -150,123 +150,191 @@
     return lax.broadcasted_iota(jnp.int32, (rows, LANES), 1)
 
 
-def prepare_kernel(group_ref, force_ref, conduct_ref, diag_ref, ice_ref, ground_ref, fields_ref, low_ref, high_ref):
-    layers = force_ref.shape[1]
-    per_group = LANES // HALO
-    is_ice = jnp.where(group_ref[0] == 0, 1.0, 0.0)
-    ice = ice_ref[...].astype(jnp.float32)
-    ground = ground_ref[...].astype(jnp.float32)
-    active = ice * (1.0 - (1.0 - is_ice) * ground)
-    friction = is_ice * friction_gain * ground * ice
+def blocks(total, size, body):
+    def step(g, carry):
+        body(g * size)
+        return carry
+
+    lax.fori_loop(0, total // size, step, 0)
+
+
+def slots_of(rows):
+    return lanes_of(rows) // HALO
+
+
+RIGHT = tuple((4 + 2 * j) % 8 for j in range(4))
+LEFT = tuple((7 + 2 * j) % 8 for j in range(4))
+
+
+def turned(value, amount):
+    return pltpu.roll(value, amount % LANES, 1) if amount % LANES else value
+
+
+def by_partner(place, values):
+    bit = 1
+    while bit < len(values):
+        swap = (place & bit) != 0
+        values = [jnp.where(swap, values[d ^ bit], values[d]) for d in range(len(values))]
+        bit *= 2
+    return values
+
+
+def prepare_kernel(where_ref, force_ref, conduct_ref, diag_ref, ice_ref, ground_ref, *refs):
+    count = (len(refs) - 10) // 2
+    own_refs, rim_refs = refs[:count], refs[count : 2 * count]
+    low_ref, high_ref, force, conduct, diag, ice, ground, sems, small_sems, _ = refs[2 * count :]
+    layers = force.shape[0]
+    chunks = sems.shape[0]
+    depth = layers // chunks
+    small = [
+        pltpu.make_async_copy(ice_ref, ice, small_sems.at[0]),
+        pltpu.make_async_copy(ground_ref, ground, small_sems.at[1]),
+    ]
+    copies = []
+    for copy in small:
+        copy.start()
+    for c in range(chunks):
+        part = pl.ds(c * depth, depth)
+        row = []
+        for n, (source, target) in enumerate(((force_ref, force), (conduct_ref, conduct), (diag_ref, diag))):
+            copy = pltpu.make_async_copy(source.at[0, part], target.at[part], sems.at[c, n])
+            copy.start()
+            row.append(copy)
+        copies.append(row)
+    place = where_ref[1]
+    is_ice = jnp.where(where_ref[0] == 0, 1.0, 0.0)
+    for copy in small:
+        copy.wait()
+    ice_cells = ice[...].astype(jnp.float32)
+    ground_cells = ground[...].astype(jnp.float32)
+    active = ice_cells * (1.0 - (1.0 - is_ice) * ground_cells)
+    friction = is_ice * friction_gain * ground_cells * ice_cells
     lane = lanes_of(SUBLANES)
-
-    def step(q, carry):
-        low, high = [None] * 3, [None] * 3
-        for j in range(per_group):
-            layer = q * per_group + j
-            coupling = jnp.sqrt(conduct_ref[0, layer].astype(jnp.float32)) * active
-            base = diag_ref[0, layer].astype(jnp.float32)
-            if j == 0:
-                base = base + friction * jnp.where(q == 0, 1.0, 0.0)
-            force = active * force_ref[0, layer]
-            for k, value in enumerate((coupling, base, force)):
-                fields_ref[k, layer] = value
-                first = pltpu.roll(value[:, :LANES], HALO * j, 1) if j else value[:, :LANES]
-                last = value[:, -LANES:]
-                turn = (HALO * (j + 1)) % LANES
-                last = pltpu.roll(last, turn, 1) if turn else last
-                if j == 0:
-                    low[k], high[k] = first, last
-                else:
-                    here = lane >= HALO * j
-                    low[k] = jnp.where(here, first, low[k])
-                    high[k] = jnp.where(here, last, high[k])
-        for k in range(3):
-            low_ref[k, q] = low[k]
-            high_ref[k, q] = high[k]
-        return carry
-
-    lax.fori_loop(0, layers // per_group, step, 0)
-
-
-def pack_kernel(edge_ref, fields_ref, low_ref, high_ref, out_ref):
-    layers = fields_ref.shape[1]
-    count = out_ref.shape[0]
-    per_group = LANES // HALO
-    spare = LANES - 3 * LANES // 4
-    width = fields_ref.shape[3] // count
-    lane = lanes_of(SUBLANES)
+    slot = slots_of(SUBLANES)
+    half = LANES // 2
 
     def step(q, carry):
         for k in range(3):
-            low, high = low_ref[k, q], high_ref[k, q]
+            low = high = None
+            for group in range(2):
+                rims = [None] * count
+                pair = []
+                for j in range(4):
+                    layer = q * 8 + group * 4 + j
+                    if k == 0:
+                        value = jnp.sqrt(conduct[layer].astype(jnp.float32)) * active
+                    elif k == 1:
+                        value = diag[layer].astype(jnp.float32)
+                        if group == 0 and j == 0:
+                            value = value + friction * jnp.where(q == 0, 1.0, 0.0)
+                    else:
+                        value = active * force[layer]
+                    pieces = [value[:, LANES * p : LANES * (p + 1)] for p in range(count // 2)]
+                    halves = [turned(piece, half) for piece in pieces]
+                    pair.append((pieces, halves))
+                    even = halves if j == 2 else [turned(piece, 32 * j) for piece in pieces]
+                    odd = halves if j == 0 else pieces if j == 2 else [turned(piece, half + 32 * j) for piece in pieces]
+                    for d in range(count):
+                        p = d // 2
+                        sources = []
+                        if d % 2 == 0:
+                            sources.append((RIGHT[j], even[p]))
+                            if d:
+                                sources.append((LEFT[j], even[p - 1]))
+                        else:
+                            sources.append((LEFT[j], odd[p]))
+                            if d + 1 < count:
+                                sources.append((RIGHT[j], odd[p + 1]))
+                        for target, source in sources:
+                            rims[d] = source if rims[d] is None else jnp.where(slot == target, source, rims[d])
+                    if group == 0:
+                        first, last, first_slot, last_slot = odd[0], even[-1], RIGHT[j], LEFT[j]
+                    else:
+                        first, last = turned(pieces[0], 112 + 32 * j), turned(pieces[-1], 80 + 32 * j)
+                        first_slot, last_slot = LEFT[j], RIGHT[j]
+                    low = first if low is None else jnp.where(slot == first_slot, first, low)
+                    high = last if high is None else jnp.where(slot == last_slot, last, high)
+                    if j % 2:
+                        (even_pieces, even_halves), (odd_pieces, odd_halves) = pair[-2:]
+                        packed = []
+                        for d in range(count):
+                            p = d // 2
+                            if d % 2 == 0:
+                                packed.append(jnp.where(lane < half, even_pieces[p], odd_halves[p]))
+                            else:
+                                packed.append(jnp.where(lane < half, even_halves[p], odd_pieces[p]))
+                        for ref, packed_value in zip(own_refs, by_partner(place, packed)):
+                            ref[k, q * 4 + group * 2 + j // 2] = packed_value
+                for ref, rim in zip(rim_refs, by_partner(place, rims)):
+                    ref[k, q * 2 + group] = rim
+            low_ref[k, q] = low
+            high_ref[k, q] = high
+        return carry
+
+    for c in range(chunks):
+        for copy in copies[c]:
+            copy.wait()
+        lax.fori_loop(c * depth // 8, (c + 1) * depth // 8, step, 0)
+
+
+def rims_kernel(place_ref, edge_ref, low_ref, high_ref, *refs):
+    count = len(refs) // 2
+    groups = low_ref.shape[1]
+    odd = slots_of(SUBLANES) % 2 == 1
+    first = [jnp.where(odd, place_ref[0], -1) == k for k in range(count)]
+    last = [jnp.where(odd, -1, place_ref[0] ^ (count - 1)) == k for k in range(count)]
+
+    def step(q):
+        for k in range(3):
+            before, after = low_ref[k, q], high_ref[k, q]
             if k == 0:
-                low, high = low * edge_ref[0], high * edge_ref[1]
-            main = [[None] * 3 for _ in range(count)]
-            for j in range(per_group):
-                value = fields_ref[k, q * per_group + j]
-                pieces = [
-                    pltpu.roll(value[:, p * LANES : (p + 1) * LANES], HALO, 1)
-                    for p in range(value.shape[1] // LANES)
-                ]
-                turn = (LANES - HALO * j) % LANES
-                before = pltpu.roll(low, turn, 1) if turn else low
-                turn = (LANES - HALO * j + HALO) % LANES
-                after = pltpu.roll(high, turn, 1) if turn else high
-                wide = [jnp.where(lane < HALO, before, pieces[0])]
-                for p in range(1, len(pieces)):
-                    wide.append(jnp.where(lane < HALO, pieces[p - 1], pieces[p]))
-                wide.append(jnp.where(lane < HALO, pieces[-1], after))
-                turned = [pltpu.roll(piece, width, 1) for piece in wide]
-                for d in range(count):
-                    p = d * width // LANES
-                    if d * width % LANES == 0:
-                        window = wide[p]
-                    else:
-                        window = jnp.where(lane < width, turned[p], turned[p + 1])
-                    m = j % 4
-                    if m < 3:
-                        main[d][m] = window
-                    else:
-                        for n in range(3):
-                            tail = pltpu.roll(window, LANES - spare * (n + 1), 1)
-                            out_ref[d, k, q * (per_group // 4) + j // 4, n] = jnp.where(
-                                lane < LANES - spare, main[d][n], tail
-                            )
-        return carry
-
-    lax.fori_loop(0, layers // per_group, step, 0)
-
-
-def unpack_kernel(edge_ref, got_ref, fields_ref, shared_ref):
-    count, _, groups = got_ref.shape[:3]
-    layers = 4 * groups
-    spare = LANES // 4
+                before, after = before * edge_ref[0], after * edge_ref[1]
+            befores, afters = (before, turned(before, 48)), (after, turned(after, 80))
+            for n in range(count):
+                for group in range(2):
+                    rim = refs[n][k, 2 * q + group]
+                    rim = jnp.where(first[n], befores[group], rim)
+                    refs[count + n][k, 2 * q + group] = jnp.where(last[n], afters[group], rim)
+
+    def pair(start):
+        step(start)
+        step(start + 1)
+
+    blocks(groups, 2, pair)
+
+
+def assemble_kernel(where_ref, *refs):
+    count = (len(refs) - 2) // 2
+    own_refs, rim_refs = refs[:count], refs[count : 2 * count]
+    fields_ref, shared_ref = refs[2 * count :]
+    groups = rim_refs[0].shape[1]
     lane = lanes_of(SUBLANES)
-    for d in range(count):
-        rows = pl.ds(SUBLANES * d, SUBLANES)
-
-        def step(g, total, d=d, rows=rows):
+    half = LANES // 2
+    inside = (lane < half + HALO) | (lane >= LANES - HALO)
+    rows = [pl.ds(pl.multiple_of(SUBLANES * (where_ref[1] ^ n), SUBLANES), SUBLANES) for n in range(count)]
+
+    def step(i, totals):
+        totals = list(totals)
+        for u in range(2):
+            g = 2 * i + u
             for k in range(3):
                 fill = 1.0 if k == 1 else 0.0
-                held = [got_ref[d, k, g, n] for n in range(3)]
-                last = jnp.where(
-                    lane < spare,
-                    pltpu.roll(held[0], spare, 1),
-                    jnp.where(
-                        lane < 2 * spare, pltpu.roll(held[1], 2 * spare, 1), pltpu.roll(held[2], 3 * spare, 1)
-                    ),
-                )
-                for n, value in enumerate(held + [last]):
-                    value = jnp.where(lane < LANES - spare, value, fill)
-                    fields_ref[k, 4 * g + n, rows] = value
-                    if k == 2:
-                        total = total + value
-            return total
-
-        total = lax.fori_loop(0, groups, step, jnp.zeros((SUBLANES, LANES), jnp.float32), unroll=2)
-        shared_ref[0, rows] = total / layers
-        shared_ref[1, rows] = fields_ref[0, edge_ref[0], rows]
+                for n in range(count):
+                    rim = rim_refs[n][k, g]
+                    for pair in range(2):
+                        packed = own_refs[n][k, 2 * g + pair]
+                        for own, j in ((packed, 2 * pair), (turned(packed, half), 2 * pair + 1)):
+                            value = jnp.where(lane < half, own, jnp.where(inside, turned(rim, -32 * j), fill))
+                            fields_ref[k, 4 * g + j, rows[n]] = value
+                            if k == 2:
+                                totals[n] = totals[n] + value
+        return tuple(totals)
+
+    zero = jnp.zeros((SUBLANES, LANES), jnp.float32)
+    totals = lax.fori_loop(0, groups // 2, step, (zero,) * count)
+    for n in range(count):
+        shared_ref[0, rows[n]] = totals[n] / (4 * groups)
+        shared_ref[1, rows[n]] = fields_ref[0, where_ref[0], rows[n]]
 
 
 def two_sum(a, b):
@@ -293,50 +361,58 @@
     return beside + vertical_weight * above
 
 
-def blocks(total, size, body):
-    def step(g, carry):
-        body(g * size)
-        return carry
-
-    lax.fori_loop(0, total // size, step, 0)
-
-
-def krylov_kernel(edge_ref, fields_ref, got_ref, *refs):
-    basis = refs[: ITERS + 1]
-    scale_ref, sums_ref, even_ref, odd_ref, factor_ref, gram_ref = refs[ITERS + 1 :]
-    held = (even_ref, odd_ref)
+def scale_kernel(fields_ref, scale_ref, factor_ref, held_ref):
     layers, rows = fields_ref.shape[1:3]
     inner = pl.ds(SUBLANES, rows)
-    empty = jnp.zeros((layers + 2, SUBLANES, LANES), jnp.float32)
-    for ref in held:
-        ref[:, :SUBLANES] = empty
-        ref[:, SUBLANES + rows :] = empty
-        ref[0] = jnp.zeros((rows + 2 * SUBLANES, LANES), jnp.float32)
-        ref[layers + 1] = jnp.zeros((rows + 2 * SUBLANES, LANES), jnp.float32)
+    clear_edges(held_ref, rows)
 
     def fill(first):
-        for layer in range(8):
-            even_ref[first + layer + 1, inner] = fields_ref[0, first + layer]
-
-    blocks(layers, 8, fill)
-    active = jnp.where(fields_ref[0, 0] > 0.0, 1.0, 0.0)
-    term = active * got_ref[1] * got_ref[0]
+        for layer in range(UNROLL):
+            held_ref[first + layer + 1, inner] = fields_ref[0, first + layer]
+
+    blocks(layers, UNROLL, fill)
 
     def begin(first):
         for layer in range(UNROLL):
             layer = first + layer
             coupling = fields_ref[0, layer]
-            diagonal = fields_ref[1, layer] + coupling * stencil(even_ref, layer, rows)
+            diagonal = fields_ref[1, layer] + coupling * stencil(held_ref, layer, rows)
             root = jnp.sqrt(diagonal)
             inverse = 1.0 / root
-            factor = coupling * inverse
-            source = fields_ref[2, layer] + term * jnp.where(layer == edge_ref[0], 1.0, 0.0)
-            vector = source * inverse
             scale_ref[0, layer] = inverse
             scale_ref[1, layer] = root
-            factor_ref[layer] = factor
+            factor_ref[layer] = coupling * inverse
+
+    blocks(layers, UNROLL, begin)
+
+
+def clear_edges(ref, rows):
+    layers = ref.shape[0]
+    empty = jnp.zeros((layers, SUBLANES, LANES), jnp.float32)
+    ref[:, :SUBLANES] = empty
+    ref[:, SUBLANES + rows :] = empty
+    ref[0] = jnp.zeros((rows + 2 * SUBLANES, LANES), jnp.float32)
+    ref[layers - 1] = jnp.zeros((rows + 2 * SUBLANES, LANES), jnp.float32)
+
+
+def krylov_kernel(edge_ref, fields_ref, got_ref, scale_ref, factor_ref, *refs):
+    basis = refs[: ITERS + 1]
+    sums_ref, even_ref, odd_ref, gram_ref = refs[ITERS + 1 :]
+    held = (even_ref, odd_ref)
+    layers, rows = fields_ref.shape[1:3]
+    inner = pl.ds(SUBLANES, rows)
+    for ref in held:
+        clear_edges(ref, rows)
+    active = jnp.where(fields_ref[0, 0] > 0.0, 1.0, 0.0)
+    term = active * got_ref[1] * got_ref[0]
+
+    def begin(first):
+        for layer in range(UNROLL):
+            layer = first + layer
+            source = fields_ref[2, layer] + term * jnp.where(layer == edge_ref[0], 1.0, 0.0)
+            vector = source * scale_ref[0, layer]
             basis[0][layer] = vector
-            odd_ref[layer + 1, inner] = factor * vector
+            odd_ref[layer + 1, inner] = factor_ref[layer] * vector
 
     blocks(layers, UNROLL, begin)
     for k in range(ITERS):
@@ -362,15 +438,11 @@
 
     def products(first):
         sums = [None] * len(PAIRS)
-        for n in range(0, 4, 2):
+        for n in range(0, 8, 2):
             for d in range(rows // SUBLANES):
                 part = pl.ds(SUBLANES * d, SUBLANES)
                 vectors = [
-                    jnp.where(
-                        lane < half,
-                        pltpu.roll(ref[first + n, part], LANES - HALO, 1),
-                        pltpu.roll(ref[first + n + 1, part], half - HALO, 1),
-                    )
+                    jnp.where(lane < half, ref[first + n, part], turned(ref[first + n + 1, part], half))
                     for ref in basis
                 ]
                 for p, (i, j) in enumerate(PAIRS):
@@ -381,7 +453,7 @@
             gram_ref[0, p] = high
             gram_ref[1, p] = low
 
-    blocks(layers, 4, products)
+    blocks(layers, 8, products)
     high, low = gram_ref[0, :, 0], gram_ref[1, :, 0]
     for row in range(1, SUBLANES):
         high, low = add_pairs(high, low, gram_ref[0, :, row], gram_ref[1, :, row])
@@ -461,9 +533,7 @@
                 vectors = [ref[layer, part] for ref in basis]
                 answered = tree_sum([c * v for c, v in zip(answer, vectors)]) * scale_ref[0, layer, part]
                 left = tree_sum([c * v for c, v in zip(residual, vectors)]) * scale_ref[1, layer, part]
-                out_ref[d, layer] = jnp.where(
-                    lane < half, pltpu.roll(answered, LANES - HALO, 1), pltpu.roll(left, half - HALO, 1)
-                )
+                out_ref[d, layer] = jnp.where(lane < half, answered, turned(left, half))
 
     blocks(layers, UNROLL, mix)
 
@@ -480,17 +550,26 @@
             residual_ref[0, layer, :, place] = jnp.where(lane < half, pltpu.roll(left, half, 1), right)
 
 
-def call(kernel, outs, specs, *args, scratch=(), limit=24):
+def call(kernel, outs, specs, *args, scratch=(), limit=24, flops=10**6, apart=0):
     return pl.pallas_call(
         kernel,
         name=kernel.__name__,
         out_shape=[jax.ShapeDtypeStruct(shape, jnp.float32) for shape in outs],
         in_specs=[pl.BlockSpec(memory_space=pltpu.SMEM)] * specs
-        + [pl.BlockSpec(memory_space=pltpu.VMEM)] * (len(args) - specs),
+        + [pl.BlockSpec(memory_space=pl.ANY)] * apart
+        + [pl.BlockSpec(memory_space=pltpu.VMEM)] * (len(args) - specs - apart),
         out_specs=[pl.BlockSpec(memory_space=pltpu.VMEM)] * len(outs),
-        scratch_shapes=[pltpu.VMEM(shape, jnp.float32) for shape in scratch],
+        scratch_shapes=[pltpu.VMEM(shape, jnp.float32) if isinstance(shape, tuple) else shape for shape in scratch],
         compiler_params=pltpu.CompilerParams(vmem_limit_bytes=limit * 2**20),
+        cost_estimate=pl.CostEstimate(flops=flops, bytes_accessed=0, transcendentals=0),
     )(*args)
+
+
+def exchanged(parts):
+    count = len(parts)
+    return [parts[0]] + [
+        lax.ppermute(parts[k], "gx", [(i, i ^ k) for i in range(count)]) for k in range(1, count)
+    ]
 
 
 def in_windows(forcing, conduct, diag_add, ice_mask, grounded):
@@ -498,31 +577,50 @@
     count_x, count_y = lax.axis_size("gx"), lax.axis_size("gy")
     rows = count_x * block_x
     group = lax.axis_index("group").astype(jnp.int32)
-    place = lax.axis_index("gy")
-    edge = jnp.where(group == 0, 0, layers - 1).astype(jnp.int32)[None]
-    inside = jnp.stack([place > 0, place < count_y - 1]).astype(jnp.float32)
-    rim = (3, layers * HALO // LANES, block_x, LANES)
-    fields, low, high = call(
-        prepare_kernel, [(3, layers, block_x, block_y), rim, rim], 1,
-        group[None], forcing, conduct, diag_add, ice_mask, grounded,
+    place_x = lax.axis_index("gx").astype(jnp.int32)
+    place_y = lax.axis_index("gy")
+    edge = jnp.where(group == 0, 0, layers - 1).astype(jnp.int32)
+    inside = jnp.stack([place_y > 0, place_y < count_y - 1]).astype(jnp.float32)
+    own = (3, layers // 2, block_x, LANES)
+    rim = (3, layers // 4, block_x, LANES)
+    side = (3, layers // 8, block_x, LANES)
+    block = (layers, block_x, block_y)
+    chunks = 5 if layers % 40 == 0 else 1
+    *made, low, high = call(
+        prepare_kernel, [own] * count_x + [rim] * count_x + [side] * 2, 1,
+        jnp.stack([group, place_x]), forcing, conduct, diag_add, ice_mask, grounded,
+        scratch=[
+            block,
+            pltpu.VMEM(block, conduct.dtype),
+            pltpu.VMEM(block, diag_add.dtype),
+            pltpu.VMEM(ice_mask.shape, ice_mask.dtype),
+            pltpu.VMEM(grounded.shape, grounded.dtype),
+            pltpu.SemaphoreType.DMA((chunks, 3)),
+            pltpu.SemaphoreType.DMA((2,)),
+            (SUBLANES, LANES),
+        ],
+        apart=5,
     )
     before = lax.ppermute(high, "gy", ring(count_y, 1))
     after = lax.ppermute(low, "gy", ring(count_y, -1))
-    (packed,) = call(
-        pack_kernel, [(count_x, 3, layers // 4, 3, block_x, LANES)], 1, inside, fields, before, after
-    )
-    got = lax.all_to_all(packed, "gx", 0, 0, tiled=True)
+    owns = exchanged(made[:count_x])
+    rims = call(
+        rims_kernel, [rim] * count_x, 2, place_x[None], inside, before, after, *made[count_x:]
+    )
+    rims = exchanged(rims)
     windows, shared = call(
-        unpack_kernel, [(3, layers, rows, LANES), (2, rows, LANES)], 1, edge, got
+        assemble_kernel, [(3, layers, rows, LANES), (2, rows, LANES)], 1,
+        jnp.stack([edge, place_x]), *owns, *rims,
     )
     received = from_partner(shared, "group", 0)
-    padded = rows + 2 * SUBLANES
+    padded = (layers + 2, rows + 2 * SUBLANES, LANES)
     window = (layers, rows, LANES)
-    *basis, scale, sums = call(
+    scale, factor = call(scale_kernel, [(2,) + window, window], 0, windows, scratch=[padded], flops=4 * 10**7)
+    *basis, sums = call(
         krylov_kernel,
-        [window] * (ITERS + 1) + [(2,) + window, (count_x * count_y, SUBLANES, LANES)],
-        1, edge, windows, received,
-        scratch=[(layers + 2, padded, LANES)] * 2 + [window, (2, 32, SUBLANES, LANES)],
+        [window] * (ITERS + 1) + [(count_x * count_y, SUBLANES, LANES)],
+        1, edge[None], windows, received, scale, factor,
+        scratch=[padded] * 2 + [(2, 32, SUBLANES, LANES)],
         limit=32,
     )
     sums = lax.all_to_all(sums, ("gx", "gy"), 0, 0, tiled=True)

time: 126 us -> 113 us (0.90)
  Pallas kernels: 39.5 us -> 30.4 us
  waiting for transfers between devices: 40.3 us -> 31.6 us
  starting transfers between devices: 8.98 us -> 14.2 us
  local copies, waits for them, and re-layouts: 6.01 us -> 4.42 us
    all_to_all x1 -> x0, waiting for transfers between devices: 33.8 us -> none  [in_windows(): got = lax.all_to_all(packed, 'gx', 0, 0, tiled=True)]
    ppermute x0 -> x6, waiting for transfers between devices: none -> 26.3 us  [exchanged(): lax.ppermute(parts[k], 'gx', [(i, i ^ k) for i in range(count)])]
    pallas_call x5 -> x6, Pallas kernels: 37.5 us -> 28.4 us  [call(): pl.pallas_call(kernel, name=kernel.__name__, out_shape=[jax.ShapeDtypeStr...]
    ppermute x0 -> x6, starting transfers between devices: none -> 8.95 us  [exchanged(): lax.ppermute(parts[k], 'gx', [(i, i ^ k) for i in range(count)])]
    all_to_all x1 -> x0, starting transfers between devices: 3.72 us -> none  [in_windows(): got = lax.all_to_all(packed, 'gx', 0, 0, tiled=True)]
    unnamed x12 -> x10, local copies, waits for them, and re-layouts: 6.01 us -> 4.42 us
  transfers between devices with their start and end apart: 4 -> 9, of which waited for: 4 -> 4; matrix products, arithmetic and copies ran while one was open for 0% -> 0% of each run, Pallas kernels for 0% -> 2%
where the time goes in v2:
time: 113 us
  waiting for transfers between devices  31.6 us (28%)
  blocking collectives  31.5 us (28%)
  Pallas kernels  30.4 us (27%)
  starting transfers between devices  14.2 us (13%)
  local copies, waits for them, and re-layouts  4.42 us (4%)
    pallas_call x6, Pallas kernels, call(): pl.pallas_call(kernel, name=kernel.__name__, out_shape=[jax.ShapeDtypeStr...  28.4 us
    ppermute x6, waiting for transfers between devices, exchanged(): lax.ppermute(parts[k], 'gx', [(i, i ^ k) for i in range(count)])  26.3 us
    all_to_all x1, blocking collectives, in_windows(): mixed = lax.all_to_all(mixed, 'gx', 0, 0, tiled=True)  19 us
    all_to_all x1, blocking collectives, in_windows(): sums = lax.all_to_all(sums, ('gx', 'gy'), 0, 0, tiled=True)  12.5 us
    ppermute x6, starting transfers between devices, exchanged(): lax.ppermute(parts[k], 'gx', [(i, i ^ k) for i in range(count)])  8.95 us
    unnamed x10, local copies, waits for them, and re-layouts  4.42 us
    ppermute x1, waiting for transfers between devices, in_windows(): before = lax.ppermute(high, 'gy', ring(count_y, 1))  4.03 us
    ppermute x1, starting transfers between devices, in_windows(): before = lax.ppermute(high, 'gy', ring(count_y, 1))  3.1 us
  transfers between devices with their start and end apart: 9, of which 4 were waited for; matrix products, arithmetic and copies ran while one was open for 0% of the time, Pallas kernels for 2%

profile of v2, /device:TPU:0, one launch (start us, length us, event | category | flops | bytes accessed | tf_op | source)
XLA Modules:
  0.0 113.1 jit_solution(5891422086978106493)
XLA Ops:
  0.7 1.1 copy-done
  1.8 1.0 copy-done.1
  2.8 1.0 copy-done.2
  3.8 0.7 copy-done.3
  5.1 5.2 %prepare_kernel.1 = (f32[3,40,8,128]{3,2,1,0:T(8,128)S(1)}, f32[3,40,8,128]{3,2,1,0:T(8,128)}, f32[3,40,8,128]{3,2,1,0:T(8,128)}, f32[3,40,8,128]{3,2,1,0:T(8,12...) custom-call(s32[2]{0:T(128)S(1)} %pad_add_fusion.1.where_ref, ...), custom_call_target="tpu_custom_call" | custom-call | flops 1000000 | tf_op jit(solution)/shard_map/prepare_kernel/pallas_call | solution.py:554
  10.4 3.1 %collective-permute-start.3 = (f32[3,10,8,128]{3,2,1,0:T(8,128)S(1)}, f32[3,10,8,128]{3,2,1,0:T(8,128)S(1)}, u32[]{:S(2)}, u32[]{:S(2)}) collective-permute-start(f32[3,10,8,128]{3,2,1,0:T(8,128)S(1)} %get-tuple-element.32), channel_id=1, source_target_pairs={{0,1},{1,2},{2,3},{3,0},{4,5},{5,6},{6,7},{7,4},{8,9},{9,10},{10,1... | collective-permute-start | bytes 368648 | tf_op jit(solution)/shard_map/ppermute | solution.py:604
  13.5 2.1 %collective-permute-start.4 = (f32[3,10,8,128]{3,2,1,0:T(8,128)S(1)}, f32[3,10,8,128]{3,2,1,0:T(8,128)S(1)}, u32[]{:S(2)}, u32[]{:S(2)}) collective-permute-start(f32[3,10,8,128]{3,2,1,0:T(8,128)S(1)} %get-tuple-element.33), channel_id=1, source_target_pairs={{0,3},{1,0},{2,1},{3,2},{4,7},{5,4},{6,5},{7,6},{8,11},{9,8},{10,9... | collective-permute-start | bytes 368648 | tf_op jit(solution)/shard_map/ppermute | solution.py:605
  15.7 4.0 %collective-permute-done.3.low_ref = f32[3,10,8,128]{3,2,1,0:T(8,128)S(1)} collective-permute-done((f32[3,10,8,128]{3,2,1,0:T(8,128)S(1)}, f32[3,10,8,128]{3,2,1,0:T(8,128)S(1)}, u32[]{:S(2)}, u32[]{:S(2)}) %collective-permute-start.3) | collective-permute-done | bytes 122912 | tf_op jit(solution)/shard_map/ppermute | solution.py:604
  19.7 1.2 %collective-permute-done.4.high_ref = f32[3,10,8,128]{3,2,1,0:T(8,128)S(1)} collective-permute-done((f32[3,10,8,128]{3,2,1,0:T(8,128)S(1)}, f32[3,10,8,128]{3,2,1,0:T(8,128)S(1)}, u32[]{:S(2)}, u32[]{:S(2)}) %collective-permute-start.4) | collective-permute-done | bytes 122912 | tf_op jit(solution)/shard_map/ppermute | solution.py:605
  20.9 1.8 %rims_kernel.1 = (f32[3,20,8,128]{3,2,1,0:T(8,128)S(1)}, f32[3,20,8,128]{3,2,1,0:T(8,128)S(1)}, f32[3,20,8,128]{3,2,1,0:T(8,128)}, f32[3,20,8,128]{3,2,1,0:T(8,128)}) custom-call(s32[1]{0:T(128)} %bitcast.1.place_ref, f32[2]{0:T(128)S(1)} %add_convert_fusion.edge_ref, f32[3,10,8,128]{3,2,1,0:T(8,128)S(1)} %collective-permute-done.3.low_ref, ...), custom_call_target="tpu_custom_call" | custom-call | flops 1000000 | tf_op jit(solution)/shard_map/rims_kernel/pallas_call | solution.py:554
  22.7 1.5 %collective-permute-start.5 = (f32[3,20,8,128]{3,2,1,0:T(8,128)S(1)}, f32[3,20,8,128]{3,2,1,0:T(8,128)S(1)}, u32[]{:S(2)}, u32[]{:S(2)}) collective-permute-start(f32[3,20,8,128]{3,2,1,0:T(8,128)S(1)} %get-tuple-element.39), channel_id=1, source_target_pairs={{0,4},{4,0},{8,12},{12,8},{1,5},{5,1},{9,13},{13,9},{2,6},{6,2},{1... | collective-permute-start | bytes 737288 | tf_op jit(solution)/shard_map/ppermute | solution.py:571
  24.7 1.5 %collective-permute-start.1 = (f32[3,40,8,128]{3,2,1,0:T(8,128)}, f32[3,40,8,128]{3,2,1,0:T(8,128)S(1)}, u32[]{:S(2)}, u32[]{:S(2)}) collective-permute-start(f32[3,40,8,128]{3,2,1,0:T(8,128)} %get-tuple-element.30), channel_id=1, source_target_pairs={{0,8},{4,12},{8,0},{12,4},{1,9},{5,13},{9,1},{13,5},{2,10},{6,14},... | collective-permute-start | bytes 1474568 | tf_op jit(solution)/shard_map/ppermute | solution.py:571
  26.2 1.4 %collective-permute-start.2 = (f32[3,40,8,128]{3,2,1,0:T(8,128)S(1)}, f32[3,40,8,128]{3,2,1,0:T(8,128)S(1)}, u32[]{:S(2)}, u32[]{:S(2)}) collective-permute-start(f32[3,40,8,128]{3,2,1,0:T(8,128)S(1)} %get-tuple-element.31), channel_id=1, source_target_pairs={{0,12},{4,8},{8,4},{12,0},{1,13},{5,9},{9,5},{13,1},{2,14},{6,10},... | collective-permute-start | bytes 1474568 | tf_op jit(solution)/shard_map/ppermute | solution.py:571
  27.7 1.5 %collective-permute-start.6 = (f32[3,20,8,128]{3,2,1,0:T(8,128)}, f32[3,20,8,128]{3,2,1,0:T(8,128)S(1)}, u32[]{:S(2)}, u32[]{:S(2)}) collective-permute-start(f32[3,20,8,128]{3,2,1,0:T(8,128)} %get-tuple-element.40), channel_id=1, source_target_pairs={{0,8},{4,12},{8,0},{12,4},{1,9},{5,13},{9,1},{13,5},{2,10},{6,14},... | collective-permute-start | bytes 737288 | tf_op jit(solution)/shard_map/ppermute | solution.py:571
  29.2 2.3 %collective-permute-done.5.refs_5_ = f32[3,20,8,128]{3,2,1,0:T(8,128)S(1)} collective-permute-done((f32[3,20,8,128]{3,2,1,0:T(8,128)S(1)}, f32[3,20,8,128]{3,2,1,0:T(8,128)S(1)}, u32[]{:S(2)}, u32[]{:S(2)}) %collective-permute-start.5) | collective-permute-done | bytes 245792 | tf_op jit(solution)/shard_map/ppermute | solution.py:571
  31.5 2.4 %collective-permute-start.7 = (f32[3,20,8,128]{3,2,1,0:T(8,128)}, f32[3,20,8,128]{3,2,1,0:T(8,128)S(1)}, u32[]{:S(2)}, u32[]{:S(2)}) collective-permute-start(f32[3,20,8,128]{3,2,1,0:T(8,128)} %get-tuple-element.41), channel_id=1, source_target_pairs={{0,12},{4,8},{8,4},{12,0},{1,13},{5,9},{9,5},{13,1},{2,14},{6,10},... | collective-permute-start | bytes 737288 | tf_op jit(solution)/shard_map/ppermute | solution.py:571
  34.0 24.0 %collective-permute-done.6.refs_6_ = f32[3,20,8,128]{3,2,1,0:T(8,128)S(1)} collective-permute-done((f32[3,20,8,128]{3,2,1,0:T(8,128)}, f32[3,20,8,128]{3,2,1,0:T(8,128)S(1)}, u32[]{:S(2)}, u32[]{:S(2)}) %collective-permute-start.6) | collective-permute-done | bytes 245792 | tf_op jit(solution)/shard_map/ppermute | solution.py:571
  58.0 2.5 %assemble_kernel.1 = (f32[3,80,32,128]{3,2,1,0:T(8,128)S(1)}, f32[2,32,128]{2,1,0:T(8,128)S(1)}) custom-call(s32[2]{0:T(128)S(1)} %pad_add_fusion.where_ref, f32[3,40,8,128]{3,2,1,0:T(8,128)S(1)} %get-tuple-element.28.refs_0_, f32[3,40,8,128]{3,2,1,0:T(8,128)S(1)} %collective-permute-done.refs_1_, f32[3,40,8,128]{3,2,1,0:T(8,128)S(1)} %collective-permute-done.1.refs_2_, ...), custom_call_target="tpu_custom_call" | custom-call | flops 1000000 | tf_op jit(solution)/shard_map/assemble_kernel/pallas_call | solution.py:554
  60.6 2.0 %scale_kernel.1 = (f32[2,80,32,128]{3,2,1,0:T(8,128)S(1)}, f32[80,32,128]{2,1,0:T(8,128)S(1)}) custom-call(f32[3,80,32,128]{3,2,1,0:T(8,128)S(1)} %get-tuple-element.42.fields_ref), custom_call_target="tpu_custom_call" | custom-call | flops 40000000 | tf_op jit(solution)/shard_map/scale_kernel/pallas_call | solution.py:554
  62.7 13.9 %krylov_kernel.1 = (f32[80,32,128]{2,1,0:T(8,128)S(1)}, f32[80,32,128]{2,1,0:T(8,128)S(1)}, f32[80,32,128]{2,1,0:T(8,128)S(1)}, f32[80,32,128]{2,1,0:T(8,128)S(1...) custom-call(s32[1]{0:T(128)} %bitcast.edge_ref, ...), custom_call_target="tpu_custom_call" | custom-call | flops 1000000 | tf_op jit(solution)/shard_map/krylov_kernel/pallas_call | solution.py:554
  76.6 12.5 %all_to_all.10.sums_ref = f32[16,8,128]{2,1,0:T(8,128)S(1)} all-to-all(f32[16,8,128]{2,1,0:T(8,128)S(1)} %get-tuple-element.46), channel_id=1, replica_groups=mesh['group'=2,'gx'=4,'gy'=4] {'gx','gy'}, dimensions={0} | all-to-all | bytes 131072 | tf_op jit(solution)/shard_map/all_to_all | solution.py:626
  89.1 3.0 %combine_kernel.1 = f32[4,80,8,128]{3,2,1,0:T(8,128)S(1)} custom-call(f32[16,8,128]{2,1,0:T(8,128)S(1)} %all_to_all.10.sums_ref, f32[80,32,128]{2,1,0:T(8,128)S(1)} %get-tuple-element.47.refs_0_, f32[80,32,128]{2,1,0:T(8,128)S(1)} %get-tuple-element.48.refs_1_, f32[80,32,128]{2,1,0:T(8,128)S(1)} %get-tuple-element.49.refs_2_, ...), custom_call_target="tpu_custom_call" | custom-call | flops 1000000 | tf_op jit(solution)/shard_map/combine_kernel/pallas_call | solution.py:554
  92.1 19.0 %all_to_all.11.got_ref = f32[4,80,8,128]{3,2,1,0:T(8,128)S(1)} all-to-all(f32[4,80,8,128]{3,2,1,0:T(8,128)S(1)} %combine_kernel.1), channel_id=1, replica_groups=mesh['group'=2,'gx'=4,'gy'=4] {'gx'}, dimensions={0} | all-to-all | bytes 2621440 | tf_op jit(solution)/shard_map/all_to_all | solution.py:631
  111.1 2.0 %finish_kernel.1 = (f32[1,80,8,256]{3,2,1,0:T(8,128)}, f32[1,80,8,256]{3,2,1,0:T(8,128)}) custom-call(f32[4,80,8,128]{3,2,1,0:T(8,128)S(1)} %all_to_all.11.got_ref), custom_call_target="tpu_custom_call" | custom-call | tf_op jit(solution)/shard_map/finish_kernel/pallas_call | solution.py:635
  (16 shorter events, 1.5 us)
Async XLA Ops:
  0.7 1.1 copy-start
  1.8 1.0 copy-start.1
  2.8 1.0 copy-start.2
  3.7 0.7 copy-start.3
  4.4 0.7 copy-start.4
  10.4 9.3 %collective-permute-start.3 = (f32[3,10,8,128]{3,2,1,0:T(8,128)S(1)}, f32[3,10,8,128]{3,2,1,0:T(8,128)S(1)}, u32[]{:S(2)}, u32[]{:S(2)}) collective-permute-start(f32[3,10,8,128]{3,2,1,0:T(8,128)S(1)} %get-tuple-element.32), channel_id=1, source_target_pairs={{0,1},{1,2},{2,3},{3,0},{4,5},{5,6},{6,7},{7,4},{8,9},{9,10},{10,1... | collective-permute-start | bytes 368648 | tf_op jit(solution)/shard_map/ppermute | solution.py:604
  13.5 7.4 %collective-permute-start.4 = (f32[3,10,8,128]{3,2,1,0:T(8,128)S(1)}, f32[3,10,8,128]{3,2,1,0:T(8,128)S(1)}, u32[]{:S(2)}, u32[]{:S(2)}) collective-permute-start(f32[3,10,8,128]{3,2,1,0:T(8,128)S(1)} %get-tuple-element.33), channel_id=1, source_target_pairs={{0,3},{1,0},{2,1},{3,2},{4,7},{5,4},{6,5},{7,6},{8,11},{9,8},{10,9... | collective-permute-start | bytes 368648 | tf_op jit(solution)/shard_map/ppermute | solution.py:605
  22.7 8.8 %collective-permute-start.5 = (f32[3,20,8,128]{3,2,1,0:T(8,128)S(1)}, f32[3,20,8,128]{3,2,1,0:T(8,128)S(1)}, u32[]{:S(2)}, u32[]{:S(2)}) collective-permute-start(f32[3,20,8,128]{3,2,1,0:T(8,128)S(1)} %get-tuple-element.39), channel_id=1, source_target_pairs={{0,4},{4,0},{8,12},{12,8},{1,5},{5,1},{9,13},{13,9},{2,6},{6,2},{1... | collective-permute-start | bytes 737288 | tf_op jit(solution)/shard_map/ppermute | solution.py:571
  24.2 33.8 %collective-permute-start = (f32[3,40,8,128]{3,2,1,0:T(8,128)}, f32[3,40,8,128]{3,2,1,0:T(8,128)S(1)}, u32[]{:S(2)}, u32[]{:S(2)}) collective-permute-start(f32[3,40,8,128]{3,2,1,0:T(8,128)} %get-tuple-element.29), channel_id=1, source_target_pairs={{0,4},{4,0},{8,12},{12,8},{1,5},{5,1},{9,13},{13,9},{2,6},{6,2},{1... | collective-permute-start | bytes 1474568 | tf_op jit(solution)/shard_map/ppermute | solution.py:571
  24.7 33.3 %collective-permute-start.1 = (f32[3,40,8,128]{3,2,1,0:T(8,128)}, f32[3,40,8,128]{3,2,1,0:T(8,128)S(1)}, u32[]{:S(2)}, u32[]{:S(2)}) collective-permute-start(f32[3,40,8,128]{3,2,1,0:T(8,128)} %get-tuple-element.30), channel_id=1, source_target_pairs={{0,8},{4,12},{8,0},{12,4},{1,9},{5,13},{9,1},{13,5},{2,10},{6,14},... | collective-permute-start | bytes 1474568 | tf_op jit(solution)/shard_map/ppermute | solution.py:571
  26.2 31.8 %collective-permute-start.2 = (f32[3,40,8,128]{3,2,1,0:T(8,128)S(1)}, f32[3,40,8,128]{3,2,1,0:T(8,128)S(1)}, u32[]{:S(2)}, u32[]{:S(2)}) collective-permute-start(f32[3,40,8,128]{3,2,1,0:T(8,128)S(1)} %get-tuple-element.31), channel_id=1, source_target_pairs={{0,12},{4,8},{8,4},{12,0},{1,13},{5,9},{9,5},{13,1},{2,14},{6,10},... | collective-permute-start | bytes 1474568 | tf_op jit(solution)/shard_map/ppermute | solution.py:571
  27.7 30.3 %collective-permute-start.6 = (f32[3,20,8,128]{3,2,1,0:T(8,128)}, f32[3,20,8,128]{3,2,1,0:T(8,128)S(1)}, u32[]{:S(2)}, u32[]{:S(2)}) collective-permute-start(f32[3,20,8,128]{3,2,1,0:T(8,128)} %get-tuple-element.40), channel_id=1, source_target_pairs={{0,8},{4,12},{8,0},{12,4},{1,9},{5,13},{9,1},{13,5},{2,10},{6,14},... | collective-permute-start | bytes 737288 | tf_op jit(solution)/shard_map/ppermute | solution.py:571
  31.5 26.5 %collective-permute-start.7 = (f32[3,20,8,128]{3,2,1,0:T(8,128)}, f32[3,20,8,128]{3,2,1,0:T(8,128)S(1)}, u32[]{:S(2)}, u32[]{:S(2)}) collective-permute-start(f32[3,20,8,128]{3,2,1,0:T(8,128)} %get-tuple-element.41), channel_id=1, source_target_pairs={{0,12},{4,8},{8,4},{12,0},{1,13},{5,9},{9,5},{13,1},{2,14},{6,10},... | collective-permute-start | bytes 737288 | tf_op jit(solution)/shard_map/ppermute | solution.py:571
  60.5 2.1 %collective-permute-start.8 = (f32[2,32,128]{2,1,0:T(8,128)S(1)}, f32[2,32,128]{2,1,0:T(8,128)S(1)}, u32[]{:S(2)}, u32[]{:S(2)}) collective-permute-start(f32[2,32,128]{2,1,0:T(8,128)S(1)} %get-tuple-element.43), channel_id=1, source_target_pairs={{0,16},{16,0},{1,17},{17,1},{2,18},{18,2},{3,19},{19,3},{4,20},{20... | collective-permute-start | bytes 98312 | tf_op jit(solution)/shard_map/ppermute | solution.py:56

commit v3 on v2

--- a/solution.py
+++ b/solution.py
@@ -1,3 +1,4 @@
+import functools
 import math
 
 import jax
@@ -7,12 +8,14 @@
 from jax.experimental.pallas import tpu as pltpu
 from jax.sharding import PartitionSpec as P
 
+
 ITERS = 6
 LANES = 128
 SUBLANES = 8
 HALO = 16
 SHIFTS = (0.0, 0.75, 1.5, 0.25, 1.75, 1.0)
 UNROLL = 16
+PARTS = 2
 PAIRS = tuple((i, j) for i in range(ITERS + 1) for j in range(i + 1) if j < ITERS)
 
 
@@ -177,6 +180,10 @@
         values = [jnp.where(swap, values[d ^ bit], values[d]) for d in range(len(values))]
         bit *= 2
     return values
+
+
+def partner_rows(place, count):
+    return [pl.ds(pl.multiple_of(SUBLANES * (place ^ n), SUBLANES), SUBLANES) for n in range(count)]
 
 
 def prepare_kernel(where_ref, force_ref, conduct_ref, diag_ref, ice_ref, ground_ref, *refs):
@@ -311,7 +318,7 @@
     lane = lanes_of(SUBLANES)
     half = LANES // 2
     inside = (lane < half + HALO) | (lane >= LANES - HALO)
-    rows = [pl.ds(pl.multiple_of(SUBLANES * (where_ref[1] ^ n), SUBLANES), SUBLANES) for n in range(count)]
+    rows = partner_rows(where_ref[1], count)
 
     def step(i, totals):
         totals = list(totals)
@@ -355,10 +362,11 @@
     here = at(0)
     near = at(1) + at(-1)
     mixed = here + cross_weight * near
-    far = at(2) + at(-2) + pltpu.roll(here, 2, 1) + pltpu.roll(here, LANES - 2, 1)
-    beside = near + pltpu.roll(mixed, 1, 1) + pltpu.roll(mixed, LANES - 1, 1) + far_weight * far
+    wide = turned(mixed, 1) + far_weight * (here + turned(here, 2))
+    far = at(2) + at(-2) - 2.0 * here
     above = held_ref[layer + 2, pl.ds(SUBLANES, rows)] + held_ref[layer, pl.ds(SUBLANES, rows)]
-    return beside + vertical_weight * above
+    flat = near + far_weight * far + vertical_weight * above
+    return (flat + wide) + turned(wide, -2)
 
 
 def scale_kernel(fields_ref, scale_ref, factor_ref, held_ref):
@@ -507,12 +515,9 @@
     return answer, residual
 
 
-def combine_kernel(sums_ref, *refs):
-    basis = refs[: ITERS + 1]
-    scale_ref, out_ref, gram_ref = refs[ITERS + 1 :]
-    layers, rows = scale_ref.shape[1:3]
+def solve_kernel(sums_ref, coefs_ref, gram_ref):
     share = LANES // 4
-    parts = [(sums_ref[d], pltpu.roll(sums_ref[d], LANES - share // 2, 1)) for d in range(sums_ref.shape[0])]
+    parts = [(sums_ref[d], turned(sums_ref[d], -share // 2)) for d in range(sums_ref.shape[0])]
     while len(parts) > 1:
         parts = [add_pairs(*parts[i], *parts[i + 1]) if i + 1 < len(parts) else parts[i] for i in range(0, len(parts), 2)]
     gram_ref[...] = parts[0][0] + parts[0][1]
@@ -520,48 +525,67 @@
         pair: gram_ref[pl.ds(p % SUBLANES, 1), pl.ds(share * (p // SUBLANES), 1)] for p, pair in enumerate(PAIRS)
     }
     answer, residual = iterate(gram)
-    answer = [jnp.broadcast_to(c, (SUBLANES, LANES)) for c in answer]
-    residual = [jnp.broadcast_to(c, (SUBLANES, LANES)) for c in residual]
+    for n, coef in enumerate(answer + residual):
+        coefs_ref[n] = jnp.broadcast_to(coef, (SUBLANES, LANES))
+
+
+def combine_kernel(start, depth, where_ref, coefs_ref, *refs):
+    basis = refs[: ITERS + 1]
+    scale_ref, *out_refs = refs[ITERS + 1 :]
     half = LANES // 2
     lane = lanes_of(SUBLANES)
+    rows = partner_rows(where_ref[1], len(out_refs))
 
     def mix(first):
-        for layer in range(UNROLL):
+        answer = [coefs_ref[n] for n in range(ITERS)]
+        residual = [coefs_ref[ITERS + n] for n in range(ITERS + 1)]
+        for layer in range(8):
             layer = first + layer
-            for d in range(rows // SUBLANES):
-                part = pl.ds(SUBLANES * d, SUBLANES)
-                vectors = [ref[layer, part] for ref in basis]
-                answered = tree_sum([c * v for c, v in zip(answer, vectors)]) * scale_ref[0, layer, part]
-                left = tree_sum([c * v for c, v in zip(residual, vectors)]) * scale_ref[1, layer, part]
-                out_ref[d, layer] = jnp.where(lane < half, answered, turned(left, half))
-
-    blocks(layers, UNROLL, mix)
-
-
-def finish_kernel(got_ref, solution_ref, residual_ref):
-    count, layers = got_ref.shape[:2]
+            for ref, part in zip(out_refs, rows):
+                vectors = [basis_ref[start + layer, part] for basis_ref in basis]
+                answered = tree_sum([c * v for c, v in zip(answer, vectors)]) * scale_ref[0, start + layer, part]
+                left = tree_sum([c * v for c, v in zip(residual, vectors)]) * scale_ref[1, start + layer, part]
+                ref[layer] = jnp.where(lane < half, answered, turned(left, half))
+
+    blocks(depth, 8, mix)
+
+
+def finish_kernel(start, depth, count, where_ref, *refs):
+    parts = refs[:count]
+    solution_ref, residual_ref, solved, left, sems = refs[-5:]
     half = LANES // 2
     lane = lanes_of(SUBLANES)
-    for layer in range(layers):
-        for p in range(count // 2):
-            left, right = got_ref[2 * p, layer], got_ref[2 * p + 1, layer]
-            place = pl.ds(LANES * p, LANES)
-            solution_ref[0, layer, :, place] = jnp.where(lane < half, left, pltpu.roll(right, half, 1))
-            residual_ref[0, layer, :, place] = jnp.where(lane < half, pltpu.roll(left, half, 1), right)
-
-
-def call(kernel, outs, specs, *args, scratch=(), limit=24, flops=10**6, apart=0):
+    copies = []
+    for first in range(0, depth, 8):
+        for layer in range(first, first + 8):
+            got = by_partner(where_ref[1], [ref[layer] for ref in parts])
+            for p in range(count // 2):
+                place = pl.ds(LANES * p, LANES)
+                low, high = got[2 * p : 2 * p + 2]
+                solved[layer, :, place] = jnp.where(lane < half, low, turned(high, half))
+                left[layer, :, place] = jnp.where(lane < half, turned(low, half), high)
+    for n, (held, target) in enumerate(((solved, solution_ref), (left, residual_ref))):
+        copy = pltpu.make_async_copy(held, target.at[0, pl.ds(start, depth)], sems.at[n])
+        copy.start()
+        copies.append(copy)
+    for copy in copies:
+        copy.wait()
+
+
+def call(kernel, outs, args, smem=0, hbm=0, tail=0, scratch=(), limit=24, flops=10**6, aliases=None, hbm_outs=False):
+    out_space = pltpu.HBM if hbm_outs else pltpu.VMEM
     return pl.pallas_call(
         kernel,
-        name=kernel.__name__,
         out_shape=[jax.ShapeDtypeStruct(shape, jnp.float32) for shape in outs],
-        in_specs=[pl.BlockSpec(memory_space=pltpu.SMEM)] * specs
-        + [pl.BlockSpec(memory_space=pl.ANY)] * apart
-        + [pl.BlockSpec(memory_space=pltpu.VMEM)] * (len(args) - specs - apart),
-        out_specs=[pl.BlockSpec(memory_space=pltpu.VMEM)] * len(outs),
+        in_specs=[pl.BlockSpec(memory_space=pltpu.SMEM)] * smem
+        + [pl.BlockSpec(memory_space=pltpu.HBM)] * hbm
+        + [pl.BlockSpec(memory_space=pltpu.VMEM)] * (len(args) - smem - hbm - tail)
+        + [pl.BlockSpec(memory_space=pltpu.HBM)] * tail,
+        out_specs=[pl.BlockSpec(memory_space=out_space)] * len(outs),
         scratch_shapes=[pltpu.VMEM(shape, jnp.float32) if isinstance(shape, tuple) else shape for shape in scratch],
         compiler_params=pltpu.CompilerParams(vmem_limit_bytes=limit * 2**20),
         cost_estimate=pl.CostEstimate(flops=flops, bytes_accessed=0, transcendentals=0),
+        input_output_aliases=aliases or {},
     )(*args)
 
 
@@ -586,9 +610,11 @@
     side = (3, layers // 8, block_x, LANES)
     block = (layers, block_x, block_y)
     chunks = 5 if layers % 40 == 0 else 1
+    where = jnp.stack([edge, place_x])
     *made, low, high = call(
-        prepare_kernel, [own] * count_x + [rim] * count_x + [side] * 2, 1,
-        jnp.stack([group, place_x]), forcing, conduct, diag_add, ice_mask, grounded,
+        prepare_kernel, [own] * count_x + [rim] * count_x + [side] * 2,
+        (jnp.stack([group, place_x]), forcing, conduct, diag_add, ice_mask, grounded),
+        smem=1, hbm=5,
         scratch=[
             block,
             pltpu.VMEM(block, conduct.dtype),
@@ -599,49 +625,43 @@
             pltpu.SemaphoreType.DMA((2,)),
             (SUBLANES, LANES),
         ],
-        apart=5,
     )
+    owns = exchanged(made[:count_x])
     before = lax.ppermute(high, "gy", ring(count_y, 1))
     after = lax.ppermute(low, "gy", ring(count_y, -1))
-    owns = exchanged(made[:count_x])
-    rims = call(
-        rims_kernel, [rim] * count_x, 2, place_x[None], inside, before, after, *made[count_x:]
-    )
+    rims = call(rims_kernel, [rim] * count_x, (place_x[None], inside, before, after, *made[count_x:]), smem=2)
     rims = exchanged(rims)
-    windows, shared = call(
-        assemble_kernel, [(3, layers, rows, LANES), (2, rows, LANES)], 1,
-        jnp.stack([edge, place_x]), *owns, *rims,
-    )
+    windows, shared = call(assemble_kernel, [(3, layers, rows, LANES), (2, rows, LANES)], (where, *owns, *rims), smem=1)
     received = from_partner(shared, "group", 0)
     padded = (layers + 2, rows + 2 * SUBLANES, LANES)
     window = (layers, rows, LANES)
-    scale, factor = call(scale_kernel, [(2,) + window, window], 0, windows, scratch=[padded], flops=4 * 10**7)
+    scale, factor = call(scale_kernel, [(2,) + window, window], (windows,), scratch=[padded], flops=4 * 10**7)
     *basis, sums = call(
-        krylov_kernel,
-        [window] * (ITERS + 1) + [(count_x * count_y, SUBLANES, LANES)],
-        1, edge[None], windows, received, scale, factor,
-        scratch=[padded] * 2 + [(2, 32, SUBLANES, LANES)],
-        limit=32,
+        krylov_kernel, [window] * (ITERS + 1) + [(count_x * count_y, SUBLANES, LANES)],
+        (edge[None], windows, received, scale, factor), smem=1,
+        scratch=[padded] * 2 + [(2, 32, SUBLANES, LANES)], limit=32,
     )
     sums = lax.all_to_all(sums, ("gx", "gy"), 0, 0, tiled=True)
-    (mixed,) = call(
-        combine_kernel, [(count_x, layers, block_x, LANES)], 0, sums, *basis, scale,
-        scratch=[(SUBLANES, LANES)],
-    )
-    mixed = lax.all_to_all(mixed, "gx", 0, 0, tiled=True)
-    steps = 4
-    part = pl.BlockSpec((1, layers // steps, block_x, block_y), lambda i: (0, i, 0, 0))
-    return tuple(
-        pl.pallas_call(
-            finish_kernel,
-            name="finish_kernel",
-            grid=(steps,),
-            out_shape=[jax.ShapeDtypeStruct(forcing.shape, jnp.float32)] * 2,
-            in_specs=[pl.BlockSpec((count_x, layers // steps, block_x, LANES), lambda i: (0, i, 0, 0))],
-            out_specs=[part, part],
-            compiler_params=pltpu.CompilerParams(vmem_limit_bytes=24 * 2**20),
-        )(mixed)
-    )
+    (coefs,) = call(solve_kernel, [(2 * ITERS + 1, SUBLANES, LANES)], (sums,), scratch=[(SUBLANES, LANES)])
+    depth = layers // PARTS
+    arrived = []
+    for n in range(PARTS):
+        mixed = call(
+            functools.partial(combine_kernel, n * depth, depth),
+            [(depth, block_x, LANES)] * count_x, (where, coefs, *basis, scale), smem=1,
+        )
+        arrived.append(exchanged(mixed))
+    outs = ()
+    for n in range(PARTS):
+        outs = tuple(
+            call(
+                functools.partial(finish_kernel, n * depth, depth, count_x),
+                [forcing.shape] * 2, (where, *arrived[n], *outs), smem=1, tail=len(outs), hbm_outs=True,
+                scratch=[(depth, block_x, block_y)] * 2 + [pltpu.SemaphoreType.DMA((2,))],
+                aliases={1 + count_x + i: i for i in range(len(outs))},
+            )
+        )
+    return outs
 
 
 def fits_windows(layers, block_x, block_y, count_x):
@@ -657,8 +677,9 @@
 
 def per_device(forcing, conduct, diag_add, ice_mask, grounded):
     _, layers, block_x, block_y = forcing.shape
-    way = in_windows if fits_windows(layers, block_x, block_y, lax.axis_size("gx")) else on_device
-    return way(forcing, conduct, diag_add, ice_mask, grounded)
+    if not fits_windows(layers, block_x, block_y, lax.axis_size("gx")):
+        return on_device(forcing, conduct, diag_add, ice_mask, grounded)
+    return in_windows(forcing, conduct, diag_add, ice_mask, grounded)
 
 
 def solution(mesh):

time: 113 us -> 120 us (1.062)
  blocking collectives: 31.5 us -> 12.5 us
  Pallas kernels: 30.4 us -> 43.1 us
  starting transfers between devices: 14.2 us -> 20.9 us
  waiting for transfers between devices: 31.6 us -> 37.9 us
    all_to_all x1 -> x0, blocking collectives: 19 us -> none  [in_windows(): mixed = lax.all_to_all(mixed, 'gx', 0, 0, tiled=True)]
    pallas_call x7 -> x10, Pallas kernels: 30.4 us -> 43.1 us  [call(): pl.pallas_call(kernel, out_shape=[jax.ShapeDtypeStruct(shape, jnp.float32...]
    ppermute x6 -> x12, starting transfers between devices: 8.95 us -> 15.6 us  [exchanged(): lax.ppermute(parts[k], 'gx', [(i, i ^ k) for i in range(count)])]
    ppermute x6 -> x12, waiting for transfers between devices: 26.3 us -> 32.7 us  [exchanged(): lax.ppermute(parts[k], 'gx', [(i, i ^ k) for i in range(count)])]
  transfers between devices with their start and end apart: 9 -> 15, of which waited for: 4 -> 9; matrix products, arithmetic and copies ran while one was open for 0% -> 0% of each run, Pallas kernels for 2% -> 5%
where the time goes in v3:
time: 120 us
  Pallas kernels  43.1 us (36%)
  waiting for transfers between devices  37.9 us (32%)
  starting transfers between devices  20.9 us (17%)
  blocking collectives  12.5 us (10%)
  local copies, waits for them, and re-layouts  4.42 us (4%)
    pallas_call x10, Pallas kernels, call(): pl.pallas_call(kernel, out_shape=[jax.ShapeDtypeStruct(shape, jnp.float32...  43.1 us
    ppermute x12, waiting for transfers between devices, exchanged(): lax.ppermute(parts[k], 'gx', [(i, i ^ k) for i in range(count)])  32.7 us
    ppermute x12, starting transfers between devices, exchanged(): lax.ppermute(parts[k], 'gx', [(i, i ^ k) for i in range(count)])  15.6 us
    all_to_all x1, blocking collectives, in_windows(): sums = lax.all_to_all(sums, ('gx', 'gy'), 0, 0, tiled=True)  12.5 us
    unnamed x10, local copies, waits for them, and re-layouts  4.42 us
    ppermute x1, waiting for transfers between devices, in_windows(): before = lax.ppermute(high, 'gy', ring(count_y, 1))  4.03 us
    ppermute x1, starting transfers between devices, in_windows(): before = lax.ppermute(high, 'gy', ring(count_y, 1))  3.1 us
  transfers between devices with their start and end apart: 15, of which 9 were waited for; matrix products, arithmetic and copies ran while one was open for 0% of the time, Pallas kernels for 5%

profile of v3, /device:TPU:0, one launch (start us, length us, event | category | flops | bytes accessed | tf_op | source)
XLA Modules:
  0.0 119.8 jit_solution(16708946351747099362)
XLA Ops:
  5.1 5.2 %shard_map.68 = (f32[3,40,8,128]{3,2,1,0:T(8,128)S(1)}, f32[3,40,8,128]{3,2,1,0:T(8,128)}, f32[3,40,8,128]{3,2,1,0:T(8,128)}, f32[3,40,8,128]{3,2,1,0:T(8,128)S(...) custom-call(s32[2]{0:T(128)S(1)} %pad_add_fusion.1.where_ref, ...), custom_call_target="tpu_custom_call" | custom-call | flops 1000000 | tf_op jit(solution)/shard_map/pallas_call | solution.py:577
  10.4 3.1 %collective-permute-start.3 = (f32[3,10,8,128]{3,2,1,0:T(8,128)S(1)}, f32[3,10,8,128]{3,2,1,0:T(8,128)S(1)}, u32[]{:S(2)}, u32[]{:S(2)}) collective-permute-start(f32[3,10,8,128]{3,2,1,0:T(8,128)S(1)} %get-tuple-element.42), channel_id=1, source_target_pairs={{0,1},{1,2},{2,3},{3,0},{4,5},{5,6},{6,7},{7,4},{8,9},{9,10},{10,1... | collective-permute-start | bytes 368648 | tf_op jit(solution)/shard_map/ppermute | solution.py:630
  13.5 2.1 %collective-permute-start.4 = (f32[3,10,8,128]{3,2,1,0:T(8,128)S(1)}, f32[3,10,8,128]{3,2,1,0:T(8,128)S(1)}, u32[]{:S(2)}, u32[]{:S(2)}) collective-permute-start(f32[3,10,8,128]{3,2,1,0:T(8,128)S(1)} %get-tuple-element.43), channel_id=1, source_target_pairs={{0,3},{1,0},{2,1},{3,2},{4,7},{5,4},{6,5},{7,6},{8,11},{9,8},{10,9... | collective-permute-start | bytes 368648 | tf_op jit(solution)/shard_map/ppermute | solution.py:631
  15.7 4.0 %collective-permute-done.3.low_ref = f32[3,10,8,128]{3,2,1,0:T(8,128)S(1)} collective-permute-done((f32[3,10,8,128]{3,2,1,0:T(8,128)S(1)}, f32[3,10,8,128]{3,2,1,0:T(8,128)S(1)}, u32[]{:S(2)}, u32[]{:S(2)}) %collective-permute-start.3) | collective-permute-done | bytes 122912 | tf_op jit(solution)/shard_map/ppermute | solution.py:630
  20.9 1.8 %shard_map.69 = (f32[3,20,8,128]{3,2,1,0:T(8,128)S(1)}, f32[3,20,8,128]{3,2,1,0:T(8,128)S(1)}, f32[3,20,8,128]{3,2,1,0:T(8,128)}, f32[3,20,8,128]{3,2,1,0:T(8,128)}) custom-call(s32[1]{0:T(128)} %bitcast.1.place_ref, f32[2]{0:T(128)S(1)} %add_convert_fusion.edge_ref, f32[3,10,8,128]{3,2,1,0:T(8,128)S(1)} %collective-permute-done.3.low_ref, ...), custom_call_target="tpu_custom_call" | custom-call | flops 1000000 | tf_op jit(solution)/shard_map/pallas_call | solution.py:577
  24.7 1.5 %collective-permute-start.1 = (f32[3,40,8,128]{3,2,1,0:T(8,128)}, f32[3,40,8,128]{3,2,1,0:T(8,128)S(1)}, u32[]{:S(2)}, u32[]{:S(2)}) collective-permute-start(f32[3,40,8,128]{3,2,1,0:T(8,128)} %get-tuple-element.40), channel_id=1, source_target_pairs={{0,8},{4,12},{8,0},{12,4},{1,9},{5,13},{9,1},{13,5},{2,10},{6,14},... | collective-permute-start | bytes 1474568 | tf_op jit(solution)/shard_map/ppermute | solution.py:595
  27.7 1.5 %collective-permute-start.6 = (f32[3,20,8,128]{3,2,1,0:T(8,128)}, f32[3,20,8,128]{3,2,1,0:T(8,128)S(1)}, u32[]{:S(2)}, u32[]{:S(2)}) collective-permute-start(f32[3,20,8,128]{3,2,1,0:T(8,128)} %get-tuple-element.50), channel_id=1, source_target_pairs={{0,8},{4,12},{8,0},{12,4},{1,9},{5,13},{9,1},{13,5},{2,10},{6,14},... | collective-permute-start | bytes 737288 | tf_op jit(solution)/shard_map/ppermute | solution.py:595
  29.2 2.3 %collective-permute-done.5.refs_5_ = f32[3,20,8,128]{3,2,1,0:T(8,128)S(1)} collective-permute-done((f32[3,20,8,128]{3,2,1,0:T(8,128)S(1)}, f32[3,20,8,128]{3,2,1,0:T(8,128)S(1)}, u32[]{:S(2)}, u32[]{:S(2)}) %collective-permute-start.5) | collective-permute-done | bytes 245792 | tf_op jit(solution)/shard_map/ppermute | solution.py:595
  31.5 2.4 %collective-permute-start.7 = (f32[3,20,8,128]{3,2,1,0:T(8,128)}, f32[3,20,8,128]{3,2,1,0:T(8,128)S(1)}, u32[]{:S(2)}, u32[]{:S(2)}) collective-permute-start(f32[3,20,8,128]{3,2,1,0:T(8,128)} %get-tuple-element.51), channel_id=1, source_target_pairs={{0,12},{4,8},{8,4},{12,0},{1,13},{5,9},{9,5},{13,1},{2,14},{6,10},... | collective-permute-start | bytes 737288 | tf_op jit(solution)/shard_map/ppermute | solution.py:595
  34.0 24.0 %collective-permute-done.6.refs_6_ = f32[3,20,8,128]{3,2,1,0:T(8,128)S(1)} collective-permute-done((f32[3,20,8,128]{3,2,1,0:T(8,128)}, f32[3,20,8,128]{3,2,1,0:T(8,128)S(1)}, u32[]{:S(2)}, u32[]{:S(2)}) %collective-permute-start.6) | collective-permute-done | bytes 245792 | tf_op jit(solution)/shard_map/ppermute | solution.py:595
  58.0 2.5 %shard_map.70 = (f32[3,80,32,128]{3,2,1,0:T(8,128)S(1)}, f32[2,32,128]{2,1,0:T(8,128)S(1)}) custom-call(s32[2]{0:T(128)S(1)} %pad_add_fusion.where_ref, f32[3,40,8,128]{3,2,1,0:T(8,128)S(1)} %get-tuple-element.38.refs_0_, f32[3,40,8,128]{3,2,1,0:T(8,128)S(1)} %collective-permute-done.refs_1_, f32[3,40,8,128]{3,2,1,0:T(8,128)S(1)} %collective-permute-done.1.refs_2_, ...), custom_call_target="tpu_custom_call" | custom-call | flops 1000000 | tf_op jit(solution)/shard_map/pallas_call | solution.py:577
  60.6 3.1 %shard_map.71 = (f32[2,80,32,128]{3,2,1,0:T(8,128)S(1)}, f32[80,32,128]{2,1,0:T(8,128)S(1)}) custom-call(f32[3,80,32,128]{3,2,1,0:T(8,128)S(1)} %get-tuple-element.52.fields_ref), custom_call_target="tpu_custom_call" | custom-call | flops 40000000 | tf_op jit(solution)/shard_map/pallas_call | solution.py:577
  63.7 22.4 %shard_map.72 = (f32[80,32,128]{2,1,0:T(8,128)S(1)}, f32[80,32,128]{2,1,0:T(8,128)S(1)}, f32[80,32,128]{2,1,0:T(8,128)S(1)}, f32[80,32,128]{2,1,0:T(8,128)S(1)},...) custom-call(s32[1]{0:T(128)} %bitcast.edge_ref, ...), custom_call_target="tpu_custom_call" | custom-call | flops 1000000 | tf_op jit(solution)/shard_map/pallas_call | solution.py:577
  86.1 12.5 %all_to_all.5.sums_ref = f32[16,8,128]{2,1,0:T(8,128)S(1)} all-to-all(f32[16,8,128]{2,1,0:T(8,128)S(1)} %get-tuple-element.56), channel_id=1, replica_groups=mesh['group'=2,'gx'=4,'gy'=4] {'gx','gy'}, dimensions={0} | all-to-all | bytes 131072 | tf_op jit(solution)/shard_map/all_to_all | solution.py:644
  98.7 1.5 %shard_map.73.coefs_ref = f32[13,8,128]{2,1,0:T(8,128)S(1)} custom-call(f32[16,8,128]{2,1,0:T(8,128)S(1)} %all_to_all.5.sums_ref), custom_call_target="tpu_custom_call" | custom-call | flops 1000000 | tf_op jit(solution)/shard_map/pallas_call | solution.py:577
  100.2 1.7 %shard_map.75 = (f32[40,8,128]{2,1,0:T(8,128)S(1)}, f32[40,8,128]{2,1,0:T(8,128)S(1)}, f32[40,8,128]{2,1,0:T(8,128)S(1)}, f32[40,8,128]{2,1,0:T(8,128)S(1)}) custom-call(s32[2]{0:T(128)S(1)} %pad_add_fusion.where_ref, f32[13,8,128]{2,1,0:T(8,128)S(1)} %shard_map.73.coefs_ref, f32[80,32,128]{2,1,0:T(8,128)S(1)} %get-tuple-element.57.refs_0_, ...), custom_call_target="tpu_custom_call" | custom-call | flops 1000000 | tf_op jit(solution)/shard_map/pallas_call | solution.py:577
  103.3 2.1 %collective-permute-start.14 = (f32[40,8,128]{2,1,0:T(8,128)S(1)}, f32[40,8,128]{2,1,0:T(8,128)S(1)}, u32[]{:S(2)}, u32[]{:S(2)}) collective-permute-start(f32[40,8,128]{2,1,0:T(8,128)S(1)} %get-tuple-element.71), channel_id=1, source_target_pairs={{0,12},{4,8},{8,4},{12,0},{1,13},{5,9},{9,5},{13,1},{2,14},{6,10},... | collective-permute-start | bytes 491528 | tf_op jit(solution)/shard_map/ppermute | solution.py:595
  105.4 1.7 %shard_map.74 = (f32[40,8,128]{2,1,0:T(8,128)S(1)}, f32[40,8,128]{2,1,0:T(8,128)S(1)}, f32[40,8,128]{2,1,0:T(8,128)S(1)}, f32[40,8,128]{2,1,0:T(8,128)S(1)}) custom-call(s32[2]{0:T(128)S(1)} %pad_add_fusion.where_ref, f32[13,8,128]{2,1,0:T(8,128)S(1)} %shard_map.73.coefs_ref, f32[80,32,128]{2,1,0:T(8,128)S(1)} %get-tuple-element.57.refs_0_, ...), custom_call_target="tpu_custom_call" | custom-call | flops 1000000 | tf_op jit(solution)/shard_map/pallas_call | solution.py:577
  109.0 1.6 %collective-permute-start.11 = (f32[40,8,128]{2,1,0:T(8,128)S(1)}, f32[40,8,128]{2,1,0:T(8,128)S(1)}, u32[]{:S(2)}, u32[]{:S(2)}) collective-permute-start(f32[40,8,128]{2,1,0:T(8,128)S(1)} %get-tuple-element.67), channel_id=1, source_target_pairs={{0,12},{4,8},{8,4},{12,0},{1,13},{5,9},{9,5},{13,1},{2,14},{6,10},... | collective-permute-start | bytes 491528 | tf_op jit(solution)/shard_map/ppermute | solution.py:595
  110.9 1.7 %collective-permute-done.14.refs_3_ = f32[40,8,128]{2,1,0:T(8,128)S(1)} collective-permute-done((f32[40,8,128]{2,1,0:T(8,128)S(1)}, f32[40,8,128]{2,1,0:T(8,128)S(1)}, u32[]{:S(2)}, u32[]{:S(2)}) %collective-permute-start.14) | collective-permute-done | bytes 163872 | tf_op jit(solution)/shard_map/ppermute | solution.py:595
  112.7 1.6 %shard_map.76 = (f32[1,80,8,256]{3,2,1,0:T(8,128)}, f32[1,80,8,256]{3,2,1,0:T(8,128)}) custom-call(s32[2]{0:T(128)S(1)} %pad_add_fusion.where_ref, f32[40,8,128]{2,1,0:T(8,128)S(1)} %get-tuple-element.68.refs_0_, f32[40,8,128]{2,1,0:T(8,128)S(1)} %collective-permute-done.12.refs_1_, f32[40,8,128]{2,1,0:T(8,128)S(1)} %collective-permute-done.13.refs_2_, ...), custom_call_target="tpu_custom_call" | custom-call | flops 1000000 | tf_op jit(solution)/shard_map/pallas_call | solution.py:577
  114.3 1.7 %collective-permute-done.9.refs_1_ = f32[40,8,128]{2,1,0:T(8,128)S(1)} collective-permute-done((f32[40,8,128]{2,1,0:T(8,128)S(1)}, f32[40,8,128]{2,1,0:T(8,128)S(1)}, u32[]{:S(2)}, u32[]{:S(2)}) %collective-permute-start.9) | collective-permute-done | bytes 163872 | tf_op jit(solution)/shard_map/ppermute | solution.py:595
  116.0 2.2 %collective-permute-done.10.refs_2_ = f32[40,8,128]{2,1,0:T(8,128)S(1)} collective-permute-done((f32[40,8,128]{2,1,0:T(8,128)S(1)}, f32[40,8,128]{2,1,0:T(8,128)S(1)}, u32[]{:S(2)}, u32[]{:S(2)}) %collective-permute-start.10) | collective-permute-done | bytes 163872 | tf_op jit(solution)/shard_map/ppermute | solution.py:595
  118.2 1.6 %shard_map.77 = (f32[1,80,8,256]{3,2,1,0:T(8,128)}, f32[1,80,8,256]{3,2,1,0:T(8,128)}) custom-call(s32[2]{0:T(128)S(1)} %pad_add_fusion.where_ref, f32[40,8,128]{2,1,0:T(8,128)S(1)} %get-tuple-element.64.refs_0_, f32[40,8,128]{2,1,0:T(8,128)S(1)} %collective-permute-done.9.refs_1_, ...), custom_call_target="tpu_custom_call", output_to_operand_aliasing={{0}: (5, {}), {1}: (6, {})} | custom-call | flops 1000000 | tf_op jit(solution)/shard_map/pallas_call | solution.py:577
  (30 shorter events, 13.1 us)
Async XLA Ops:
  0.7 1.1 copy-start
  1.8 1.0 copy-start.1
  2.8 1.0 copy-start.2
  3.7 0.7 copy-start.3
  4.4 0.7 copy-start.4
  10.4 9.3 %collective-permute-start.3 = (f32[3,10,8,128]{3,2,1,0:T(8,128)S(1)}, f32[3,10,8,128]{3,2,1,0:T(8,128)S(1)}, u32[]{:S(2)}, u32[]{:S(2)}) collective-permute-start(f32[3,10,8,128]{3,2,1,0:T(8,128)S(1)} %get-tuple-element.42), channel_id=1, source_target_pairs={{0,1},{1,2},{2,3},{3,0},{4,5},{5,6},{6,7},{7,4},{8,9},{9,10},{10,1... | collective-permute-start | bytes 368648 | tf_op jit(solution)/shard_map/ppermute | solution.py:630
  13.5 7.4 %collective-permute-start.4 = (f32[3,10,8,128]{3,2,1,0:T(8,128)S(1)}, f32[3,10,8,128]{3,2,1,0:T(8,128)S(1)}, u32[]{:S(2)}, u32[]{:S(2)}) collective-permute-start(f32[3,10,8,128]{3,2,1,0:T(8,128)S(1)} %get-tuple-element.43), channel_id=1, source_target_pairs={{0,3},{1,0},{2,1},{3,2},{4,7},{5,4},{6,5},{7,6},{8,11},{9,8},{10,9... | collective-permute-start | bytes 368648 | tf_op jit(solution)/shard_map/ppermute | solution.py:631
  22.7 8.8 %collective-permute-start.5 = (f32[3,20,8,128]{3,2,1,0:T(8,128)S(1)}, f32[3,20,8,128]{3,2,1,0:T(8,128)S(1)}, u32[]{:S(2)}, u32[]{:S(2)}) collective-permute-start(f32[3,20,8,128]{3,2,1,0:T(8,128)S(1)} %get-tuple-element.49), channel_id=1, source_target_pairs={{0,4},{4,0},{8,12},{12,8},{1,5},{5,1},{9,13},{13,9},{2,6},{6,2},{1... | collective-permute-start | bytes 737288 | tf_op jit(solution)/shard_map/ppermute | solution.py:595
  24.2 33.8 %collective-permute-start = (f32[3,40,8,128]{3,2,1,0:T(8,128)}, f32[3,40,8,128]{3,2,1,0:T(8,128)S(1)}, u32[]{:S(2)}, u32[]{:S(2)}) collective-permute-start(f32[3,40,8,128]{3,2,1,0:T(8,128)} %get-tuple-element.39), channel_id=1, source_target_pairs={{0,4},{4,0},{8,12},{12,8},{1,5},{5,1},{9,13},{13,9},{2,6},{6,2},{1... | collective-permute-start | bytes 1474568 | tf_op jit(solution)/shard_map/ppermute | solution.py:595
  24.7 33.3 %collective-permute-start.1 = (f32[3,40,8,128]{3,2,1,0:T(8,128)}, f32[3,40,8,128]{3,2,1,0:T(8,128)S(1)}, u32[]{:S(2)}, u32[]{:S(2)}) collective-permute-start(f32[3,40,8,128]{3,2,1,0:T(8,128)} %get-tuple-element.40), channel_id=1, source_target_pairs={{0,8},{4,12},{8,0},{12,4},{1,9},{5,13},{9,1},{13,5},{2,10},{6,14},... | collective-permute-start | bytes 1474568 | tf_op jit(solution)/shard_map/ppermute | solution.py:595
  26.2 31.8 %collective-permute-start.2 = (f32[3,40,8,128]{3,2,1,0:T(8,128)S(1)}, f32[3,40,8,128]{3,2,1,0:T(8,128)S(1)}, u32[]{:S(2)}, u32[]{:S(2)}) collective-permute-start(f32[3,40,8,128]{3,2,1,0:T(8,128)S(1)} %get-tuple-element.41), channel_id=1, source_target_pairs={{0,12},{4,8},{8,4},{12,0},{1,13},{5,9},{9,5},{13,1},{2,14},{6,10},... | collective-permute-start | bytes 1474568 | tf_op jit(solution)/shard_map/ppermute | solution.py:595
  27.7 30.3 %collective-permute-start.6 = (f32[3,20,8,128]{3,2,1,0:T(8,128)}, f32[3,20,8,128]{3,2,1,0:T(8,128)S(1)}, u32[]{:S(2)}, u32[]{:S(2)}) collective-permute-start(f32[3,20,8,128]{3,2,1,0:T(8,128)} %get-tuple-element.50), channel_id=1, source_target_pairs={{0,8},{4,12},{8,0},{12,4},{1,9},{5,13},{9,1},{13,5},{2,10},{6,14},... | collective-permute-start | bytes 737288 | tf_op jit(solution)/shard_map/ppermute | solution.py:595
  31.5 26.5 %collective-permute-start.7 = (f32[3,20,8,128]{3,2,1,0:T(8,128)}, f32[3,20,8,128]{3,2,1,0:T(8,128)S(1)}, u32[]{:S(2)}, u32[]{:S(2)}) collective-permute-start(f32[3,20,8,128]{3,2,1,0:T(8,128)} %get-tuple-element.51), channel_id=1, source_target_pairs={{0,12},{4,8},{8,4},{12,0},{1,13},{5,9},{9,5},{13,1},{2,14},{6,10},... | collective-permute-start | bytes 737288 | tf_op jit(solution)/shard_map/ppermute | solution.py:595
  60.6 3.2 %collective-permute-start.8 = (f32[2,32,128]{2,1,0:T(8,128)S(1)}, f32[2,32,128]{2,1,0:T(8,128)S(1)}, u32[]{:S(2)}, u32[]{:S(2)}) collective-permute-start(f32[2,32,128]{2,1,0:T(8,128)S(1)} %get-tuple-element.53), channel_id=1, source_target_pairs={{0,16},{16,0},{1,17},{17,1},{2,18},{18,2},{3,19},{19,3},{4,20},{20... | collective-permute-start | bytes 98312 | tf_op jit(solution)/shard_map/ppermute | solution.py:59
  101.9 7.1 %collective-permute-start.12 = (f32[40,8,128]{2,1,0:T(8,128)S(1)}, f32[40,8,128]{2,1,0:T(8,128)S(1)}, u32[]{:S(2)}, u32[]{:S(2)}) collective-permute-start(f32[40,8,128]{2,1,0:T(8,128)S(1)} %get-tuple-element.69), channel_id=1, source_target_pairs={{0,4},{4,0},{8,12},{12,8},{1,5},{5,1},{9,13},{13,9},{2,6},{6,2},{1... | collective-permute-start | bytes 491528 | tf_op jit(solution)/shard_map/ppermute | solution.py:595
  102.7 8.3 %collective-permute-start.13 = (f32[40,8,128]{2,1,0:T(8,128)S(1)}, f32[40,8,128]{2,1,0:T(8,128)S(1)}, u32[]{:S(2)}, u32[]{:S(2)}) collective-permute-start(f32[40,8,128]{2,1,0:T(8,128)S(1)} %get-tuple-element.70), channel_id=1, source_target_pairs={{0,8},{4,12},{8,0},{12,4},{1,9},{5,13},{9,1},{13,5},{2,10},{6,14},... | collective-permute-start | bytes 491528 | tf_op jit(solution)/shard_map/ppermute | solution.py:595
  103.3 9.4 %collective-permute-start.14 = (f32[40,8,128]{2,1,0:T(8,128)S(1)}, f32[40,8,128]{2,1,0:T(8,128)S(1)}, u32[]{:S(2)}, u32[]{:S(2)}) collective-permute-start(f32[40,8,128]{2,1,0:T(8,128)S(1)} %get-tuple-element.71), channel_id=1, source_target_pairs={{0,12},{4,8},{8,4},{12,0},{1,13},{5,9},{9,5},{13,1},{2,14},{6,10},... | collective-permute-start | bytes 491528 | tf_op jit(solution)/shard_map/ppermute | solution.py:595
  107.1 8.9 %collective-permute-start.9 = (f32[40,8,128]{2,1,0:T(8,128)S(1)}, f32[40,8,128]{2,1,0:T(8,128)S(1)}, u32[]{:S(2)}, u32[]{:S(2)}) collective-permute-start(f32[40,8,128]{2,1,0:T(8,128)S(1)} %get-tuple-element.65), channel_id=1, source_target_pairs={{0,4},{4,0},{8,12},{12,8},{1,5},{5,1},{9,13},{13,9},{2,6},{6,2},{1... | collective-permute-start | bytes 491528 | tf_op jit(solution)/shard_map/ppermute | solution.py:595
  107.9 10.3 %collective-permute-start.10 = (f32[40,8,128]{2,1,0:T(8,128)S(1)}, f32[40,8,128]{2,1,0:T(8,128)S(1)}, u32[]{:S(2)}, u32[]{:S(2)}) collective-permute-start(f32[40,8,128]{2,1,0:T(8,128)S(1)} %get-tuple-element.66), channel_id=1, source_target_pairs={{0,8},{4,12},{8,0},{12,4},{1,9},{5,13},{9,1},{13,5},{2,10},{6,14},... | collective-permute-start | bytes 491528 | tf_op jit(solution)/shard_map/ppermute | solution.py:595
  109.0 9.2 %collective-permute-start.11 = (f32[40,8,128]{2,1,0:T(8,128)S(1)}, f32[40,8,128]{2,1,0:T(8,128)S(1)}, u32[]{:S(2)}, u32[]{:S(2)}) collective-permute-start(f32[40,8,128]{2,1,0:T(8,128)S(1)} %get-tuple-element.67), channel_id=1, source_target_pairs={{0,12},{4,8},{8,4},{12,0},{1,13},{5,9},{9,5},{13,1},{2,14},{6,10},... | collective-permute-start | bytes 491528 | tf_op jit(solution)/shard_map/ppermute | solution.py:595

commit v4 on v3

--- a/solution.py
+++ b/solution.py
@@ -362,11 +362,10 @@
     here = at(0)
     near = at(1) + at(-1)
     mixed = here + cross_weight * near
-    wide = turned(mixed, 1) + far_weight * (here + turned(here, 2))
-    far = at(2) + at(-2) - 2.0 * here
+    far = at(2) + at(-2) + turned(here, 2) + turned(here, -2)
+    beside = near + turned(mixed, 1) + turned(mixed, -1) + far_weight * far
     above = held_ref[layer + 2, pl.ds(SUBLANES, rows)] + held_ref[layer, pl.ds(SUBLANES, rows)]
-    flat = near + far_weight * far + vertical_weight * above
-    return (flat + wide) + turned(wide, -2)
+    return beside + vertical_weight * above
 
 
 def scale_kernel(fields_ref, scale_ref, factor_ref, held_ref):
@@ -611,6 +610,10 @@
     block = (layers, block_x, block_y)
     chunks = 5 if layers % 40 == 0 else 1
     where = jnp.stack([edge, place_x])
+    forcing, conduct, diag_add, ice_mask, grounded = [
+        pltpu.with_memory_space_constraint(x, pltpu.HBM)
+        for x in (forcing, conduct, diag_add, ice_mask, grounded)
+    ]
     *made, low, high = call(
         prepare_kernel, [own] * count_x + [rim] * count_x + [side] * 2,
         (jnp.stack([group, place_x]), forcing, conduct, diag_add, ice_mask, grounded),

time: 120 us -> 105 us (0.88)
  Pallas kernels: 43.1 us -> 33 us
  local copies, waits for them, and re-layouts: 4.42 us -> 0 us
    pallas_call x10, Pallas kernels: 43.1 us -> 33 us  [call(): pl.pallas_call(kernel, out_shape=[jax.ShapeDtypeStruct(shape, jnp.float32...]
    unnamed x10 -> x0, local copies, waits for them, and re-layouts: 4.42 us -> none
where the time goes in v4:
time: 105 us
  waiting for transfers between devices  37.9 us (36%)
  Pallas kernels  33 us (31%)
  starting transfers between devices  20.9 us (20%)
  blocking collectives  12.5 us (12%)
    pallas_call x10, Pallas kernels, call(): pl.pallas_call(kernel, out_shape=[jax.ShapeDtypeStruct(shape, jnp.float32...  33 us
    ppermute x12, waiting for transfers between devices, exchanged(): lax.ppermute(parts[k], 'gx', [(i, i ^ k) for i in range(count)])  32.7 us
    ppermute x12, starting transfers between devices, exchanged(): lax.ppermute(parts[k], 'gx', [(i, i ^ k) for i in range(count)])  15.6 us
    all_to_all x1, blocking collectives, in_windows(): sums = lax.all_to_all(sums, ('gx', 'gy'), 0, 0, tiled=True)  12.5 us
    ppermute x1, waiting for transfers between devices, in_windows(): before = lax.ppermute(high, 'gy', ring(count_y, 1))  4.03 us
    ppermute x1, starting transfers between devices, in_windows(): before = lax.ppermute(high, 'gy', ring(count_y, 1))  3.1 us
  transfers between devices with their start and end apart: 15, of which 9 were waited for; matrix products, arithmetic and copies ran while one was open for 0% of the time, Pallas kernels for 5%

profile of v4, /device:TPU:0, one launch (start us, length us, event | category | flops | bytes accessed | tf_op | source)
XLA Modules:
  0.0 105.3 jit_solution(7596952650784899)
XLA Ops:
  0.7 4.7 %shard_map.68 = (f32[3,40,8,128]{3,2,1,0:T(8,128)S(1)}, f32[3,40,8,128]{3,2,1,0:T(8,128)}, f32[3,40,8,128]{3,2,1,0:T(8,128)}, f32[3,40,8,128]{3,2,1,0:T(8,128)S(...) custom-call(s32[2]{0:T(128)S(1)} %pad_add_fusion.1.where_ref, ...), custom_call_target="tpu_custom_call" | custom-call | flops 1000000 | tf_op jit(solution)/shard_map/pallas_call | solution.py:576
  5.4 3.1 %collective-permute-start.3 = (f32[3,10,8,128]{3,2,1,0:T(8,128)S(1)}, f32[3,10,8,128]{3,2,1,0:T(8,128)S(1)}, u32[]{:S(2)}, u32[]{:S(2)}) collective-permute-start(f32[3,10,8,128]{3,2,1,0:T(8,128)S(1)} %get-tuple-element.42), channel_id=1, source_target_pairs={{0,1},{1,2},{2,3},{3,0},{4,5},{5,6},{6,7},{7,4},{8,9},{9,10},{10,1... | collective-permute-start | bytes 368648 | tf_op jit(solution)/shard_map/ppermute | solution.py:633
  8.5 2.1 %collective-permute-start.4 = (f32[3,10,8,128]{3,2,1,0:T(8,128)S(1)}, f32[3,10,8,128]{3,2,1,0:T(8,128)S(1)}, u32[]{:S(2)}, u32[]{:S(2)}) collective-permute-start(f32[3,10,8,128]{3,2,1,0:T(8,128)S(1)} %get-tuple-element.43), channel_id=1, source_target_pairs={{0,3},{1,0},{2,1},{3,2},{4,7},{5,4},{6,5},{7,6},{8,11},{9,8},{10,9... | collective-permute-start | bytes 368648 | tf_op jit(solution)/shard_map/ppermute | solution.py:634
  10.7 4.0 %collective-permute-done.3.low_ref = f32[3,10,8,128]{3,2,1,0:T(8,128)S(1)} collective-permute-done((f32[3,10,8,128]{3,2,1,0:T(8,128)S(1)}, f32[3,10,8,128]{3,2,1,0:T(8,128)S(1)}, u32[]{:S(2)}, u32[]{:S(2)}) %collective-permute-start.3) | collective-permute-done | bytes 122912 | tf_op jit(solution)/shard_map/ppermute | solution.py:633
  15.9 1.8 %shard_map.69 = (f32[3,20,8,128]{3,2,1,0:T(8,128)S(1)}, f32[3,20,8,128]{3,2,1,0:T(8,128)S(1)}, f32[3,20,8,128]{3,2,1,0:T(8,128)}, f32[3,20,8,128]{3,2,1,0:T(8,128)}) custom-call(s32[1]{0:T(128)} %bitcast.1.place_ref, f32[2]{0:T(128)S(1)} %add_convert_fusion.edge_ref, f32[3,10,8,128]{3,2,1,0:T(8,128)S(1)} %collective-permute-done.3.low_ref, ...), custom_call_target="tpu_custom_call" | custom-call | flops 1000000 | tf_op jit(solution)/shard_map/pallas_call | solution.py:576
  19.7 1.5 %collective-permute-start.1 = (f32[3,40,8,128]{3,2,1,0:T(8,128)}, f32[3,40,8,128]{3,2,1,0:T(8,128)S(1)}, u32[]{:S(2)}, u32[]{:S(2)}) collective-permute-start(f32[3,40,8,128]{3,2,1,0:T(8,128)} %get-tuple-element.40), channel_id=1, source_target_pairs={{0,8},{4,12},{8,0},{12,4},{1,9},{5,13},{9,1},{13,5},{2,10},{6,14},... | collective-permute-start | bytes 1474568 | tf_op jit(solution)/shard_map/ppermute | solution.py:594
  22.7 1.5 %collective-permute-start.6 = (f32[3,20,8,128]{3,2,1,0:T(8,128)}, f32[3,20,8,128]{3,2,1,0:T(8,128)S(1)}, u32[]{:S(2)}, u32[]{:S(2)}) collective-permute-start(f32[3,20,8,128]{3,2,1,0:T(8,128)} %get-tuple-element.50), channel_id=1, source_target_pairs={{0,8},{4,12},{8,0},{12,4},{1,9},{5,13},{9,1},{13,5},{2,10},{6,14},... | collective-permute-start | bytes 737288 | tf_op jit(solution)/shard_map/ppermute | solution.py:594
  24.2 2.3 %collective-permute-done.5.refs_5_ = f32[3,20,8,128]{3,2,1,0:T(8,128)S(1)} collective-permute-done((f32[3,20,8,128]{3,2,1,0:T(8,128)S(1)}, f32[3,20,8,128]{3,2,1,0:T(8,128)S(1)}, u32[]{:S(2)}, u32[]{:S(2)}) %collective-permute-start.5) | collective-permute-done | bytes 245792 | tf_op jit(solution)/shard_map/ppermute | solution.py:594
  26.5 2.4 %collective-permute-start.7 = (f32[3,20,8,128]{3,2,1,0:T(8,128)}, f32[3,20,8,128]{3,2,1,0:T(8,128)S(1)}, u32[]{:S(2)}, u32[]{:S(2)}) collective-permute-start(f32[3,20,8,128]{3,2,1,0:T(8,128)} %get-tuple-element.51), channel_id=1, source_target_pairs={{0,12},{4,8},{8,4},{12,0},{1,13},{5,9},{9,5},{13,1},{2,14},{6,10},... | collective-permute-start | bytes 737288 | tf_op jit(solution)/shard_map/ppermute | solution.py:594
  29.0 24.0 %collective-permute-done.6.refs_6_ = f32[3,20,8,128]{3,2,1,0:T(8,128)S(1)} collective-permute-done((f32[3,20,8,128]{3,2,1,0:T(8,128)}, f32[3,20,8,128]{3,2,1,0:T(8,128)S(1)}, u32[]{:S(2)}, u32[]{:S(2)}) %collective-permute-start.6) | collective-permute-done | bytes 245792 | tf_op jit(solution)/shard_map/ppermute | solution.py:594
  53.0 2.5 %shard_map.70 = (f32[3,80,32,128]{3,2,1,0:T(8,128)S(1)}, f32[2,32,128]{2,1,0:T(8,128)S(1)}) custom-call(s32[2]{0:T(128)S(1)} %pad_add_fusion.where_ref, f32[3,40,8,128]{3,2,1,0:T(8,128)S(1)} %get-tuple-element.38.refs_0_, f32[3,40,8,128]{3,2,1,0:T(8,128)S(1)} %collective-permute-done.refs_1_, f32[3,40,8,128]{3,2,1,0:T(8,128)S(1)} %collective-permute-done.1.refs_2_, ...), custom_call_target="tpu_custom_call" | custom-call | flops 1000000 | tf_op jit(solution)/shard_map/pallas_call | solution.py:576
  55.6 2.0 %shard_map.71 = (f32[2,80,32,128]{3,2,1,0:T(8,128)S(1)}, f32[80,32,128]{2,1,0:T(8,128)S(1)}) custom-call(f32[3,80,32,128]{3,2,1,0:T(8,128)S(1)} %get-tuple-element.52.fields_ref), custom_call_target="tpu_custom_call" | custom-call | flops 40000000 | tf_op jit(solution)/shard_map/pallas_call | solution.py:576
  57.7 13.9 %shard_map.72 = (f32[80,32,128]{2,1,0:T(8,128)S(1)}, f32[80,32,128]{2,1,0:T(8,128)S(1)}, f32[80,32,128]{2,1,0:T(8,128)S(1)}, f32[80,32,128]{2,1,0:T(8,128)S(1)},...) custom-call(s32[1]{0:T(128)} %bitcast.edge_ref, ...), custom_call_target="tpu_custom_call" | custom-call | flops 1000000 | tf_op jit(solution)/shard_map/pallas_call | solution.py:576
  71.6 12.5 %all_to_all.5.sums_ref = f32[16,8,128]{2,1,0:T(8,128)S(1)} all-to-all(f32[16,8,128]{2,1,0:T(8,128)S(1)} %get-tuple-element.56), channel_id=1, replica_groups=mesh['group'=2,'gx'=4,'gy'=4] {'gx','gy'}, dimensions={0} | all-to-all | bytes 131072 | tf_op jit(solution)/shard_map/all_to_all | solution.py:647
  84.1 1.5 %shard_map.73.coefs_ref = f32[13,8,128]{2,1,0:T(8,128)S(1)} custom-call(f32[16,8,128]{2,1,0:T(8,128)S(1)} %all_to_all.5.sums_ref), custom_call_target="tpu_custom_call" | custom-call | flops 1000000 | tf_op jit(solution)/shard_map/pallas_call | solution.py:576
  85.6 1.7 %shard_map.75 = (f32[40,8,128]{2,1,0:T(8,128)S(1)}, f32[40,8,128]{2,1,0:T(8,128)S(1)}, f32[40,8,128]{2,1,0:T(8,128)S(1)}, f32[40,8,128]{2,1,0:T(8,128)S(1)}) custom-call(s32[2]{0:T(128)S(1)} %pad_add_fusion.where_ref, f32[13,8,128]{2,1,0:T(8,128)S(1)} %shard_map.73.coefs_ref, f32[80,32,128]{2,1,0:T(8,128)S(1)} %get-tuple-element.57.refs_0_, ...), custom_call_target="tpu_custom_call" | custom-call | flops 1000000 | tf_op jit(solution)/shard_map/pallas_call | solution.py:576
  88.8 2.1 %collective-permute-start.14 = (f32[40,8,128]{2,1,0:T(8,128)S(1)}, f32[40,8,128]{2,1,0:T(8,128)S(1)}, u32[]{:S(2)}, u32[]{:S(2)}) collective-permute-start(f32[40,8,128]{2,1,0:T(8,128)S(1)} %get-tuple-element.71), channel_id=1, source_target_pairs={{0,12},{4,8},{8,4},{12,0},{1,13},{5,9},{9,5},{13,1},{2,14},{6,10},... | collective-permute-start | bytes 491528 | tf_op jit(solution)/shard_map/ppermute | solution.py:594
  90.9 1.7 %shard_map.74 = (f32[40,8,128]{2,1,0:T(8,128)S(1)}, f32[40,8,128]{2,1,0:T(8,128)S(1)}, f32[40,8,128]{2,1,0:T(8,128)S(1)}, f32[40,8,128]{2,1,0:T(8,128)S(1)}) custom-call(s32[2]{0:T(128)S(1)} %pad_add_fusion.where_ref, f32[13,8,128]{2,1,0:T(8,128)S(1)} %shard_map.73.coefs_ref, f32[80,32,128]{2,1,0:T(8,128)S(1)} %get-tuple-element.57.refs_0_, ...), custom_call_target="tpu_custom_call" | custom-call | flops 1000000 | tf_op jit(solution)/shard_map/pallas_call | solution.py:576
  94.5 1.6 %collective-permute-start.11 = (f32[40,8,128]{2,1,0:T(8,128)S(1)}, f32[40,8,128]{2,1,0:T(8,128)S(1)}, u32[]{:S(2)}, u32[]{:S(2)}) collective-permute-start(f32[40,8,128]{2,1,0:T(8,128)S(1)} %get-tuple-element.67), channel_id=1, source_target_pairs={{0,12},{4,8},{8,4},{12,0},{1,13},{5,9},{9,5},{13,1},{2,14},{6,10},... | collective-permute-start | bytes 491528 | tf_op jit(solution)/shard_map/ppermute | solution.py:594
  96.4 1.7 %collective-permute-done.14.refs_3_ = f32[40,8,128]{2,1,0:T(8,128)S(1)} collective-permute-done((f32[40,8,128]{2,1,0:T(8,128)S(1)}, f32[40,8,128]{2,1,0:T(8,128)S(1)}, u32[]{:S(2)}, u32[]{:S(2)}) %collective-permute-start.14) | collective-permute-done | bytes 163872 | tf_op jit(solution)/shard_map/ppermute | solution.py:594
  98.1 1.6 %shard_map.76 = (f32[1,80,8,256]{3,2,1,0:T(8,128)}, f32[1,80,8,256]{3,2,1,0:T(8,128)}) custom-call(s32[2]{0:T(128)S(1)} %pad_add_fusion.where_ref, f32[40,8,128]{2,1,0:T(8,128)S(1)} %get-tuple-element.68.refs_0_, f32[40,8,128]{2,1,0:T(8,128)S(1)} %collective-permute-done.12.refs_1_, f32[40,8,128]{2,1,0:T(8,128)S(1)} %collective-permute-done.13.refs_2_, ...), custom_call_target="tpu_custom_call" | custom-call | flops 1000000 | tf_op jit(solution)/shard_map/pallas_call | solution.py:576
  99.8 1.7 %collective-permute-done.9.refs_1_ = f32[40,8,128]{2,1,0:T(8,128)S(1)} collective-permute-done((f32[40,8,128]{2,1,0:T(8,128)S(1)}, f32[40,8,128]{2,1,0:T(8,128)S(1)}, u32[]{:S(2)}, u32[]{:S(2)}) %collective-permute-start.9) | collective-permute-done | bytes 163872 | tf_op jit(solution)/shard_map/ppermute | solution.py:594
  101.4 2.2 %collective-permute-done.10.refs_2_ = f32[40,8,128]{2,1,0:T(8,128)S(1)} collective-permute-done((f32[40,8,128]{2,1,0:T(8,128)S(1)}, f32[40,8,128]{2,1,0:T(8,128)S(1)}, u32[]{:S(2)}, u32[]{:S(2)}) %collective-permute-start.10) | collective-permute-done | bytes 163872 | tf_op jit(solution)/shard_map/ppermute | solution.py:594
  103.6 1.6 %shard_map.77 = (f32[1,80,8,256]{3,2,1,0:T(8,128)}, f32[1,80,8,256]{3,2,1,0:T(8,128)}) custom-call(s32[2]{0:T(128)S(1)} %pad_add_fusion.where_ref, f32[40,8,128]{2,1,0:T(8,128)S(1)} %get-tuple-element.64.refs_0_, f32[40,8,128]{2,1,0:T(8,128)S(1)} %collective-permute-done.9.refs_1_, ...), custom_call_target="tpu_custom_call", output_to_operand_aliasing={{0}: (5, {}), {1}: (6, {})} | custom-call | flops 1000000 | tf_op jit(solution)/shard_map/pallas_call | solution.py:576
  (20 shorter events, 8.7 us)
Async XLA Ops:
  5.4 9.3 %collective-permute-start.3 = (f32[3,10,8,128]{3,2,1,0:T(8,128)S(1)}, f32[3,10,8,128]{3,2,1,0:T(8,128)S(1)}, u32[]{:S(2)}, u32[]{:S(2)}) collective-permute-start(f32[3,10,8,128]{3,2,1,0:T(8,128)S(1)} %get-tuple-element.42), channel_id=1, source_target_pairs={{0,1},{1,2},{2,3},{3,0},{4,5},{5,6},{6,7},{7,4},{8,9},{9,10},{10,1... | collective-permute-start | bytes 368648 | tf_op jit(solution)/shard_map/ppermute | solution.py:633
  8.5 7.4 %collective-permute-start.4 = (f32[3,10,8,128]{3,2,1,0:T(8,128)S(1)}, f32[3,10,8,128]{3,2,1,0:T(8,128)S(1)}, u32[]{:S(2)}, u32[]{:S(2)}) collective-permute-start(f32[3,10,8,128]{3,2,1,0:T(8,128)S(1)} %get-tuple-element.43), channel_id=1, source_target_pairs={{0,3},{1,0},{2,1},{3,2},{4,7},{5,4},{6,5},{7,6},{8,11},{9,8},{10,9... | collective-permute-start | bytes 368648 | tf_op jit(solution)/shard_map/ppermute | solution.py:634
  17.7 8.8 %collective-permute-start.5 = (f32[3,20,8,128]{3,2,1,0:T(8,128)S(1)}, f32[3,20,8,128]{3,2,1,0:T(8,128)S(1)}, u32[]{:S(2)}, u32[]{:S(2)}) collective-permute-start(f32[3,20,8,128]{3,2,1,0:T(8,128)S(1)} %get-tuple-element.49), channel_id=1, source_target_pairs={{0,4},{4,0},{8,12},{12,8},{1,5},{5,1},{9,13},{13,9},{2,6},{6,2},{1... | collective-permute-start | bytes 737288 | tf_op jit(solution)/shard_map/ppermute | solution.py:594
  19.2 33.8 %collective-permute-start = (f32[3,40,8,128]{3,2,1,0:T(8,128)}, f32[3,40,8,128]{3,2,1,0:T(8,128)S(1)}, u32[]{:S(2)}, u32[]{:S(2)}) collective-permute-start(f32[3,40,8,128]{3,2,1,0:T(8,128)} %get-tuple-element.39), channel_id=1, source_target_pairs={{0,4},{4,0},{8,12},{12,8},{1,5},{5,1},{9,13},{13,9},{2,6},{6,2},{1... | collective-permute-start | bytes 1474568 | tf_op jit(solution)/shard_map/ppermute | solution.py:594
  19.7 33.3 %collective-permute-start.1 = (f32[3,40,8,128]{3,2,1,0:T(8,128)}, f32[3,40,8,128]{3,2,1,0:T(8,128)S(1)}, u32[]{:S(2)}, u32[]{:S(2)}) collective-permute-start(f32[3,40,8,128]{3,2,1,0:T(8,128)} %get-tuple-element.40), channel_id=1, source_target_pairs={{0,8},{4,12},{8,0},{12,4},{1,9},{5,13},{9,1},{13,5},{2,10},{6,14},... | collective-permute-start | bytes 1474568 | tf_op jit(solution)/shard_map/ppermute | solution.py:594
  21.2 31.8 %collective-permute-start.2 = (f32[3,40,8,128]{3,2,1,0:T(8,128)S(1)}, f32[3,40,8,128]{3,2,1,0:T(8,128)S(1)}, u32[]{:S(2)}, u32[]{:S(2)}) collective-permute-start(f32[3,40,8,128]{3,2,1,0:T(8,128)S(1)} %get-tuple-element.41), channel_id=1, source_target_pairs={{0,12},{4,8},{8,4},{12,0},{1,13},{5,9},{9,5},{13,1},{2,14},{6,10},... | collective-permute-start | bytes 1474568 | tf_op jit(solution)/shard_map/ppermute | solution.py:594
  22.7 30.3 %collective-permute-start.6 = (f32[3,20,8,128]{3,2,1,0:T(8,128)}, f32[3,20,8,128]{3,2,1,0:T(8,128)S(1)}, u32[]{:S(2)}, u32[]{:S(2)}) collective-permute-start(f32[3,20,8,128]{3,2,1,0:T(8,128)} %get-tuple-element.50), channel_id=1, source_target_pairs={{0,8},{4,12},{8,0},{12,4},{1,9},{5,13},{9,1},{13,5},{2,10},{6,14},... | collective-permute-start | bytes 737288 | tf_op jit(solution)/shard_map/ppermute | solution.py:594
  26.5 26.5 %collective-permute-start.7 = (f32[3,20,8,128]{3,2,1,0:T(8,128)}, f32[3,20,8,128]{3,2,1,0:T(8,128)S(1)}, u32[]{:S(2)}, u32[]{:S(2)}) collective-permute-start(f32[3,20,8,128]{3,2,1,0:T(8,128)} %get-tuple-element.51), channel_id=1, source_target_pairs={{0,12},{4,8},{8,4},{12,0},{1,13},{5,9},{9,5},{13,1},{2,14},{6,10},... | collective-permute-start | bytes 737288 | tf_op jit(solution)/shard_map/ppermute | solution.py:594
  55.6 2.1 %collective-permute-start.8 = (f32[2,32,128]{2,1,0:T(8,128)S(1)}, f32[2,32,128]{2,1,0:T(8,128)S(1)}, u32[]{:S(2)}, u32[]{:S(2)}) collective-permute-start(f32[2,32,128]{2,1,0:T(8,128)S(1)} %get-tuple-element.53), channel_id=1, source_target_pairs={{0,16},{16,0},{1,17},{17,1},{2,18},{18,2},{3,19},{19,3},{4,20},{20... | collective-permute-start | bytes 98312 | tf_op jit(solution)/shard_map/ppermute | solution.py:59
  87.3 7.1 %collective-permute-start.12 = (f32[40,8,128]{2,1,0:T(8,128)S(1)}, f32[40,8,128]{2,1,0:T(8,128)S(1)}, u32[]{:S(2)}, u32[]{:S(2)}) collective-permute-start(f32[40,8,128]{2,1,0:T(8,128)S(1)} %get-tuple-element.69), channel_id=1, source_target_pairs={{0,4},{4,0},{8,12},{12,8},{1,5},{5,1},{9,13},{13,9},{2,6},{6,2},{1... | collective-permute-start | bytes 491528 | tf_op jit(solution)/shard_map/ppermute | solution.py:594
  88.1 8.3 %collective-permute-start.13 = (f32[40,8,128]{2,1,0:T(8,128)S(1)}, f32[40,8,128]{2,1,0:T(8,128)S(1)}, u32[]{:S(2)}, u32[]{:S(2)}) collective-permute-start(f32[40,8,128]{2,1,0:T(8,128)S(1)} %get-tuple-element.70), channel_id=1, source_target_pairs={{0,8},{4,12},{8,0},{12,4},{1,9},{5,13},{9,1},{13,5},{2,10},{6,14},... | collective-permute-start | bytes 491528 | tf_op jit(solution)/shard_map/ppermute | solution.py:594
  88.8 9.4 %collective-permute-start.14 = (f32[40,8,128]{2,1,0:T(8,128)S(1)}, f32[40,8,128]{2,1,0:T(8,128)S(1)}, u32[]{:S(2)}, u32[]{:S(2)}) collective-permute-start(f32[40,8,128]{2,1,0:T(8,128)S(1)} %get-tuple-element.71), channel_id=1, source_target_pairs={{0,12},{4,8},{8,4},{12,0},{1,13},{5,9},{9,5},{13,1},{2,14},{6,10},... | collective-permute-start | bytes 491528 | tf_op jit(solution)/shard_map/ppermute | solution.py:594
  92.5 8.9 %collective-permute-start.9 = (f32[40,8,128]{2,1,0:T(8,128)S(1)}, f32[40,8,128]{2,1,0:T(8,128)S(1)}, u32[]{:S(2)}, u32[]{:S(2)}) collective-permute-start(f32[40,8,128]{2,1,0:T(8,128)S(1)} %get-tuple-element.65), channel_id=1, source_target_pairs={{0,4},{4,0},{8,12},{12,8},{1,5},{5,1},{9,13},{13,9},{2,6},{6,2},{1... | collective-permute-start | bytes 491528 | tf_op jit(solution)/shard_map/ppermute | solution.py:594
  93.3 10.3 %collective-permute-start.10 = (f32[40,8,128]{2,1,0:T(8,128)S(1)}, f32[40,8,128]{2,1,0:T(8,128)S(1)}, u32[]{:S(2)}, u32[]{:S(2)}) collective-permute-start(f32[40,8,128]{2,1,0:T(8,128)S(1)} %get-tuple-element.66), channel_id=1, source_target_pairs={{0,8},{4,12},{8,0},{12,4},{1,9},{5,13},{9,1},{13,5},{2,10},{6,14},... | collective-permute-start | bytes 491528 | tf_op jit(solution)/shard_map/ppermute | solution.py:594
  94.5 9.2 %collective-permute-start.11 = (f32[40,8,128]{2,1,0:T(8,128)S(1)}, f32[40,8,128]{2,1,0:T(8,128)S(1)}, u32[]{:S(2)}, u32[]{:S(2)}) collective-permute-start(f32[40,8,128]{2,1,0:T(8,128)S(1)} %get-tuple-element.67), channel_id=1, source_target_pairs={{0,12},{4,8},{8,4},{12,0},{1,13},{5,9},{9,5},{13,1},{2,14},{6,10},... | collective-permute-start | bytes 491528 | tf_op jit(solution)/shard_map/ppermute | solution.py:594

commit v5 on v4

--- a/solution.py
+++ b/solution.py
@@ -182,14 +182,14 @@
     return values
 
 
-def partner_rows(place, count):
-    return [pl.ds(pl.multiple_of(SUBLANES * (place ^ n), SUBLANES), SUBLANES) for n in range(count)]
+def partner_rows(place, count, skip=0):
+    return [pl.ds(pl.multiple_of(SUBLANES * (place ^ n) + skip, SUBLANES), SUBLANES) for n in range(count)]
 
 
 def prepare_kernel(where_ref, force_ref, conduct_ref, diag_ref, ice_ref, ground_ref, *refs):
-    count = (len(refs) - 10) // 2
-    own_refs, rim_refs = refs[:count], refs[count : 2 * count]
-    low_ref, high_ref, force, conduct, diag, ice, ground, sems, small_sems, _ = refs[2 * count :]
+    count = (len(refs) - 11) // 4
+    own_refs, rim_refs, force_own_refs, force_rim_refs = [refs[count * n : count * (n + 1)] for n in range(4)]
+    low_ref, high_ref, active_ref, shared_ref, force, conduct, diag, ice, ground, sems, small_sems = refs[4 * count :]
     layers = force.shape[0]
     chunks = sems.shape[0]
     depth = layers // chunks
@@ -216,12 +216,15 @@
     ground_cells = ground[...].astype(jnp.float32)
     active = ice_cells * (1.0 - (1.0 - is_ice) * ground_cells)
     friction = is_ice * friction_gain * ground_cells * ice_cells
+    active_ref[...] = active
     lane = lanes_of(SUBLANES)
     slot = slots_of(SUBLANES)
     half = LANES // 2
 
-    def step(q, carry):
+    def step(q, total):
         for k in range(3):
+            owns, rims_out = (force_own_refs, force_rim_refs) if k == 2 else (own_refs, rim_refs)
+            lead = () if k == 2 else (k,)
             low = high = None
             for group in range(2):
                 rims = [None] * count
@@ -236,6 +239,7 @@
                             value = value + friction * jnp.where(q == 0, 1.0, 0.0)
                     else:
                         value = active * force[layer]
+                        total = total + value
                     pieces = [value[:, LANES * p : LANES * (p + 1)] for p in range(count // 2)]
                     halves = [turned(piece, half) for piece in pieces]
                     pair.append((pieces, halves))
@@ -270,22 +274,26 @@
                                 packed.append(jnp.where(lane < half, even_pieces[p], odd_halves[p]))
                             else:
                                 packed.append(jnp.where(lane < half, even_halves[p], odd_pieces[p]))
-                        for ref, packed_value in zip(own_refs, by_partner(place, packed)):
-                            ref[k, q * 4 + group * 2 + j // 2] = packed_value
-                for ref, rim in zip(rim_refs, by_partner(place, rims)):
-                    ref[k, q * 2 + group] = rim
+                        for ref, packed_value in zip(owns, by_partner(place, packed)):
+                            ref[(*lead, q * 4 + group * 2 + j // 2)] = packed_value
+                for ref, rim in zip(rims_out, by_partner(place, rims)):
+                    ref[(*lead, q * 2 + group)] = rim
             low_ref[k, q] = low
             high_ref[k, q] = high
-        return carry
-
+        return total
+
+    total = jnp.zeros_like(active)
     for c in range(chunks):
         for copy in copies[c]:
             copy.wait()
-        lax.fori_loop(c * depth // 8, (c + 1) * depth // 8, step, 0)
-
-
-def rims_kernel(place_ref, edge_ref, low_ref, high_ref, *refs):
-    count = len(refs) // 2
+        total = lax.fori_loop(c * depth // 8, (c + 1) * depth // 8, step, total)
+    weight = jnp.sqrt(conduct[where_ref[2]].astype(jnp.float32)) * active
+    shared_ref[...] = weight * (total / layers)
+
+
+def merge_kernel(place_ref, edge_ref, low_ref, high_ref, term_ref, before_ref, after_ref, *refs):
+    count = len(refs) // 5
+    rims, owns, force_rims, rims_out, force_out = [refs[count * n : count * (n + 1)] for n in range(5)]
     groups = low_ref.shape[1]
     odd = slots_of(SUBLANES) % 2 == 1
     first = [jnp.where(odd, place_ref[0], -1) == k for k in range(count)]
@@ -299,49 +307,44 @@
             befores, afters = (before, turned(before, 48)), (after, turned(after, 80))
             for n in range(count):
                 for group in range(2):
-                    rim = refs[n][k, 2 * q + group]
-                    rim = jnp.where(first[n], befores[group], rim)
-                    refs[count + n][k, 2 * q + group] = jnp.where(last[n], afters[group], rim)
+                    g = 2 * q + group
+                    rim = force_rims[n][g] if k == 2 else rims[n][k, g]
+                    rim = jnp.where(last[n], afters[group], jnp.where(first[n], befores[group], rim))
+                    if k == 2:
+                        force_out[n][4 * groups + g] = rim
+                    else:
+                        rims_out[n][k, g] = rim
+        for n in range(count):
+            for m in range(4):
+                force_out[n][4 * q + m] = owns[n][4 * q + m]
 
     def pair(start):
         step(start)
         step(start + 1)
 
     blocks(groups, 2, pair)
-
-
-def assemble_kernel(where_ref, *refs):
-    count = (len(refs) - 2) // 2
-    own_refs, rim_refs = refs[:count], refs[count : 2 * count]
-    fields_ref, shared_ref = refs[2 * count :]
-    groups = rim_refs[0].shape[1]
+    lane = lanes_of(SUBLANES)
+    half = LANES // 2
+    pieces = [term_ref[:, LANES * p : LANES * (p + 1)] for p in range(count // 2)]
+    halves = [turned(piece, half) for piece in pieces] + [turned(after_ref[...], half)]
+    windows = []
+    for d in range(count):
+        p = d // 2
+        if d % 2 == 0:
+            own, right, left = pieces[p], pieces[p], pieces[p - 1] if p else before_ref[...]
+        else:
+            own, right, left = halves[p], halves[p + 1], halves[p]
+        outer = jnp.where(lane >= LANES - HALO, left, 0.0)
+        windows.append(jnp.where(lane < half, own, jnp.where(lane < half + HALO, right, outer)))
+    for ref, value in zip(force_out, by_partner(place_ref[0], windows)):
+        ref[6 * groups] = value
+
+
+def window_of(own, rim, j, fill):
     lane = lanes_of(SUBLANES)
     half = LANES // 2
     inside = (lane < half + HALO) | (lane >= LANES - HALO)
-    rows = partner_rows(where_ref[1], count)
-
-    def step(i, totals):
-        totals = list(totals)
-        for u in range(2):
-            g = 2 * i + u
-            for k in range(3):
-                fill = 1.0 if k == 1 else 0.0
-                for n in range(count):
-                    rim = rim_refs[n][k, g]
-                    for pair in range(2):
-                        packed = own_refs[n][k, 2 * g + pair]
-                        for own, j in ((packed, 2 * pair), (turned(packed, half), 2 * pair + 1)):
-                            value = jnp.where(lane < half, own, jnp.where(inside, turned(rim, -32 * j), fill))
-                            fields_ref[k, 4 * g + j, rows[n]] = value
-                            if k == 2:
-                                totals[n] = totals[n] + value
-        return tuple(totals)
-
-    zero = jnp.zeros((SUBLANES, LANES), jnp.float32)
-    totals = lax.fori_loop(0, groups // 2, step, (zero,) * count)
-    for n in range(count):
-        shared_ref[0, rows[n]] = totals[n] / (4 * groups)
-        shared_ref[1, rows[n]] = fields_ref[0, where_ref[0], rows[n]]
+    return jnp.where(lane < half, turned(own, half * (j % 2)), jnp.where(inside, turned(rim, -32 * j), fill))
 
 
 def two_sum(a, b):
@@ -368,22 +371,35 @@
     return beside + vertical_weight * above
 
 
-def scale_kernel(fields_ref, scale_ref, factor_ref, held_ref):
-    layers, rows = fields_ref.shape[1:3]
-    inner = pl.ds(SUBLANES, rows)
+def scale_kernel(place_ref, *refs):
+    count = (len(refs) - 4) // 2
+    own_refs, rim_refs = refs[:count], refs[count : 2 * count]
+    scale_ref, factor_ref, held_ref, base_ref = refs[2 * count :]
+    layers, rows = base_ref.shape[:2]
     clear_edges(held_ref, rows)
-
-    def fill(first):
-        for layer in range(UNROLL):
-            held_ref[first + layer + 1, inner] = fields_ref[0, first + layer]
-
-    blocks(layers, UNROLL, fill)
+    places = partner_rows(place_ref[0], count)
+    padded = partner_rows(place_ref[0], count, SUBLANES)
+
+    def gather(first):
+        for u in range(2):
+            g = first + u
+            for n in range(count):
+                for j in range(4):
+                    layer = 4 * g + j
+                    coupling, base = [
+                        window_of(own_refs[n][k, 2 * g + j // 2], rim_refs[n][k, g], j, 1.0 if k else 0.0)
+                        for k in range(2)
+                    ]
+                    held_ref[layer + 1, padded[n]] = coupling
+                    base_ref[layer, places[n]] = base
+
+    blocks(layers // 4, 2, gather)
 
     def begin(first):
         for layer in range(UNROLL):
             layer = first + layer
-            coupling = fields_ref[0, layer]
-            diagonal = fields_ref[1, layer] + coupling * stencil(held_ref, layer, rows)
+            coupling = held_ref[layer + 1, pl.ds(SUBLANES, rows)]
+            diagonal = base_ref[layer] + coupling * stencil(held_ref, layer, rows)
             root = jnp.sqrt(diagonal)
             inverse = 1.0 / root
             scale_ref[0, layer] = inverse
@@ -402,26 +418,33 @@
     ref[layers - 1] = jnp.zeros((rows + 2 * SUBLANES, LANES), jnp.float32)
 
 
-def krylov_kernel(edge_ref, fields_ref, got_ref, scale_ref, factor_ref, *refs):
-    basis = refs[: ITERS + 1]
-    sums_ref, even_ref, odd_ref, gram_ref = refs[ITERS + 1 :]
+def krylov_kernel(where_ref, scale_ref, factor_ref, *refs):
+    count = len(refs) - ITERS - 1 - 4
+    force_refs = refs[:count]
+    basis = refs[count : count + ITERS + 1]
+    sums_ref, even_ref, odd_ref, gram_ref = refs[count + ITERS + 1 :]
     held = (even_ref, odd_ref)
-    layers, rows = fields_ref.shape[1:3]
+    layers, rows = factor_ref.shape[:2]
     inner = pl.ds(SUBLANES, rows)
     for ref in held:
         clear_edges(ref, rows)
-    active = jnp.where(fields_ref[0, 0] > 0.0, 1.0, 0.0)
-    term = active * got_ref[1] * got_ref[0]
+    places = partner_rows(where_ref[1], count)
+    padded = partner_rows(where_ref[1], count, SUBLANES)
 
     def begin(first):
-        for layer in range(UNROLL):
-            layer = first + layer
-            source = fields_ref[2, layer] + term * jnp.where(layer == edge_ref[0], 1.0, 0.0)
-            vector = source * scale_ref[0, layer]
-            basis[0][layer] = vector
-            odd_ref[layer + 1, inner] = factor_ref[layer] * vector
-
-    blocks(layers, UNROLL, begin)
+        for u in range(4):
+            g = first + u
+            for n in range(count):
+                term = force_refs[n][3 * layers // 4]
+                for j in range(4):
+                    layer = 4 * g + j
+                    source = window_of(force_refs[n][2 * g + j // 2], force_refs[n][layers // 2 + g], j, 0.0)
+                    source = source + term * jnp.where(layer == where_ref[0], 1.0, 0.0)
+                    vector = source * scale_ref[0, layer, places[n]]
+                    basis[0][layer, places[n]] = vector
+                    odd_ref[layer + 1, padded[n]] = factor_ref[layer, places[n]] * vector
+
+    blocks(layers // 4, 4, begin)
     for k in range(ITERS):
         source_ref, target_ref = held[(k + 1) % 2], held[k % 2]
 
@@ -604,8 +627,8 @@
     place_y = lax.axis_index("gy")
     edge = jnp.where(group == 0, 0, layers - 1).astype(jnp.int32)
     inside = jnp.stack([place_y > 0, place_y < count_y - 1]).astype(jnp.float32)
-    own = (3, layers // 2, block_x, LANES)
-    rim = (3, layers // 4, block_x, LANES)
+    own = (layers // 2, block_x, LANES)
+    rim = (layers // 4, block_x, LANES)
     side = (3, layers // 8, block_x, LANES)
     block = (layers, block_x, block_y)
     chunks = 5 if layers % 40 == 0 else 1
@@ -614,9 +637,11 @@
         pltpu.with_memory_space_constraint(x, pltpu.HBM)
         for x in (forcing, conduct, diag_add, ice_mask, grounded)
     ]
-    *made, low, high = call(
-        prepare_kernel, [own] * count_x + [rim] * count_x + [side] * 2,
-        (jnp.stack([group, place_x]), forcing, conduct, diag_add, ice_mask, grounded),
+    *made, low, high, active, shared = call(
+        prepare_kernel,
+        [(2, *own)] * count_x + [(2, *rim)] * count_x + [own] * count_x + [rim] * count_x
+        + [side] * 2 + [ice_mask.shape] * 2,
+        (jnp.stack([group, place_x, edge]), forcing, conduct, diag_add, ice_mask, grounded),
         smem=1, hbm=5,
         scratch=[
             block,
@@ -626,22 +651,32 @@
             pltpu.VMEM(grounded.shape, grounded.dtype),
             pltpu.SemaphoreType.DMA((chunks, 3)),
             pltpu.SemaphoreType.DMA((2,)),
-            (SUBLANES, LANES),
         ],
     )
-    owns = exchanged(made[:count_x])
-    before = lax.ppermute(high, "gy", ring(count_y, 1))
-    after = lax.ppermute(low, "gy", ring(count_y, -1))
-    rims = call(rims_kernel, [rim] * count_x, (place_x[None], inside, before, after, *made[count_x:]), smem=2)
-    rims = exchanged(rims)
-    windows, shared = call(assemble_kernel, [(3, layers, rows, LANES), (2, rows, LANES)], (where, *owns, *rims), smem=1)
+    owns, *left = [made[count_x * n : count_x * (n + 1)] for n in range(4)]
+    owns = exchanged(owns)
     received = from_partner(shared, "group", 0)
+    up, down = ring(count_y, 1), ring(count_y, -1)
+    before, after = lax.ppermute(high, "gy", up), lax.ppermute(low, "gy", down)
+    term = active * received
+    term_before = lax.ppermute(term[:, -LANES:], "gy", up)
+    term_after = lax.ppermute(term[:, :LANES], "gy", down)
+    force = (own[0] + rim[0] + 1, block_x, LANES)
+    merged = call(
+        merge_kernel, [(2, *rim)] * count_x + [force] * count_x,
+        (place_x[None], inside, before, after, term, term_before, term_after, *left[0], *left[1], *left[2]), smem=2,
+    )
+    rims = exchanged(merged[:count_x])
+    forces = exchanged(merged[count_x:])
     padded = (layers + 2, rows + 2 * SUBLANES, LANES)
     window = (layers, rows, LANES)
-    scale, factor = call(scale_kernel, [(2,) + window, window], (windows,), scratch=[padded], flops=4 * 10**7)
+    scale, factor = call(
+        scale_kernel, [(2,) + window, window], (place_x[None], *owns, *rims), smem=1,
+        scratch=[padded, window],
+    )
     *basis, sums = call(
         krylov_kernel, [window] * (ITERS + 1) + [(count_x * count_y, SUBLANES, LANES)],
-        (edge[None], windows, received, scale, factor), smem=1,
+        (where, scale, factor, *forces), smem=1,
         scratch=[padded] * 2 + [(2, 32, SUBLANES, LANES)], limit=32,
     )
     sums = lax.all_to_all(sums, ("gx", "gy"), 0, 0, tiled=True)

time: 105 us -> 99.9 us (0.951)
  waiting for transfers between devices: 37.9 us -> 28.6 us
  starting transfers between devices: 20.9 us -> 27 us
  blocking collectives: 12.5 us -> 10.8 us
    ppermute x12 -> x15, waiting for transfers between devices: 32.7 us -> 23.5 us  [exchanged(): lax.ppermute(parts[k], 'gx', [(i, i ^ k) for i in range(count)])]
    ppermute x12 -> x15, starting transfers between devices: 15.6 us -> 19.7 us  [exchanged(): lax.ppermute(parts[k], 'gx', [(i, i ^ k) for i in range(count)])]
    all_to_all x1, blocking collectives: 12.5 us -> 10.8 us  [in_windows(): sums = lax.all_to_all(sums, ('gx', 'gy'), 0, 0, tiled=True)]
    ppermute x2 -> x4, starting transfers between devices: 5.2 us -> 6.79 us  [the longest x1 2.63 us: in_windows(): lax.ppermute(high, 'gy', up)]
    pallas_call x10 -> x9, Pallas kernels: 33 us -> 32.2 us  [call(): pl.pallas_call(kernel, out_shape=[jax.ShapeDtypeStruct(shape, jnp.float32...]
    ppermute x2 -> x4, waiting for transfers between devices: 5.25 us -> 5.11 us  [the longest x1 2.69 us: in_windows(): term_before = lax.ppermute(term[:, -LANES:], 'gy', up)]
  transfers between devices with their start and end apart: 15 -> 20, of which waited for: 9 -> 7; matrix products, arithmetic and copies ran while one was open for 0% -> 0% of each run, Pallas kernels for 5% -> 8%
where the time goes in v5:
time: 99.9 us; the launch traced here: 99.6 us
  Pallas kernels  32.2 us (32%)
  waiting for transfers between devices  28.6 us (29%)
  starting transfers between devices  27 us (27%)
  blocking collectives  10.8 us (11%)
    pallas_call x9, Pallas kernels, call(): pl.pallas_call(kernel, out_shape=[jax.ShapeDtypeStruct(shape, jnp.float32...  32.2 us
    ppermute x15, waiting for transfers between devices, exchanged(): lax.ppermute(parts[k], 'gx', [(i, i ^ k) for i in range(count)])  23.5 us
    ppermute x15, starting transfers between devices, exchanged(): lax.ppermute(parts[k], 'gx', [(i, i ^ k) for i in range(count)])  19.7 us
    all_to_all x1, blocking collectives, in_windows(): sums = lax.all_to_all(sums, ('gx', 'gy'), 0, 0, tiled=True)  10.8 us
    ppermute x1, waiting for transfers between devices, in_windows(): term_before = lax.ppermute(term[:, -LANES:], 'gy', up)  2.69 us
    ppermute x1, starting transfers between devices, in_windows(): lax.ppermute(high, 'gy', up)  2.63 us
    ppermute x1, waiting for transfers between devices, in_windows(): term_after = lax.ppermute(term[:, :LANES], 'gy', down)  2.42 us
    ppermute x1, starting transfers between devices, in_windows(): lax.ppermute(low, 'gy', down)  2.09 us
  transfers between devices with their start and end apart: 20, of which 7 were waited for; matrix products, arithmetic and copies ran while one was open for 0% of the time, Pallas kernels for 8%

profile of v5, /device:TPU:0, one launch (start us, length us, event | category | flops | bytes accessed | tf_op | source)
XLA Modules:
  0.0 99.6 jit_solution(13756127498401369668)
XLA Ops:
  0.7 4.5 %shard_map.68 = (f32[2,40,8,128]{3,2,1,0:T(8,128)S(1)}, f32[2,40,8,128]{3,2,1,0:T(8,128)S(1)}, f32[2,40,8,128]{3,2,1,0:T(8,128)S(1)}, f32[2,40,8,128]{3,2,1,0:T(...) custom-call(s32[3]{0:T(128)S(1)} %pad_add_fusion.1.where_ref, ...), custom_call_target="tpu_custom_call" | custom-call | flops 1000000 | tf_op jit(solution)/shard_map/pallas_call | solution.py:599
  5.7 2.6 %collective-permute-start.3 = (f32[3,10,8,128]{3,2,1,0:T(8,128)}, f32[3,10,8,128]{3,2,1,0:T(8,128)S(1)}, u32[]{:S(2)}, u32[]{:S(2)}) collective-permute-start(f32[3,10,8,128]{3,2,1,0:T(8,128)} %get-tuple-element.54), channel_id=1, source_target_pairs={{0,1},{1,2},{2,3},{3,0},{4,5},{5,6},{6,7},{7,4},{8,9},{9,10},{10,1... | collective-permute-start | bytes 368648 | tf_op jit(solution)/shard_map/ppermute | solution.py:660
  8.4 2.1 %collective-permute-start.4 = (f32[3,10,8,128]{3,2,1,0:T(8,128)}, f32[3,10,8,128]{3,2,1,0:T(8,128)S(1)}, u32[]{:S(2)}, u32[]{:S(2)}) collective-permute-start(f32[3,10,8,128]{3,2,1,0:T(8,128)} %get-tuple-element.55), channel_id=1, source_target_pairs={{0,3},{1,0},{2,1},{3,2},{4,7},{5,4},{6,5},{7,6},{8,11},{9,8},{10,9... | collective-permute-start | bytes 368648 | tf_op jit(solution)/shard_map/ppermute | solution.py:660
  10.4 1.6 %collective-permute-start = (f32[2,40,8,128]{3,2,1,0:T(8,128)S(1)}, f32[2,40,8,128]{3,2,1,0:T(8,128)S(1)}, u32[]{:S(2)}, u32[]{:S(2)}) collective-permute-start(f32[2,40,8,128]{3,2,1,0:T(8,128)S(1)} %get-tuple-element.51), channel_id=1, source_target_pairs={{0,4},{4,0},{8,12},{12,8},{1,5},{5,1},{9,13},{13,9},{2,6},{6,2},{1... | collective-permute-start | bytes 983048 | tf_op jit(solution)/shard_map/ppermute | solution.py:617
  12.1 1.9 %collective-permute-start.7 = (f32[8,128]{1,0:T(8,128)S(1)}, f32[8,128]{1,0:T(8,128)S(1)}, u32[]{:S(2)}, u32[]{:S(2)}) collective-permute-start(f32[8,128]{1,0:T(8,128)S(1)} %get-tuple-element.98), channel_id=1, source_target_pairs={{0,3},{1,0},{2,1},{3,2},{4,7},{5,4},{6,5},{7,6},{8,11},{9,8},{10,9... | collective-permute-start | bytes 12296 | tf_op jit(solution)/shard_map/ppermute | solution.py:663
  14.3 2.4 %collective-permute-done.7.after_ref = f32[8,128]{1,0:T(8,128)S(1)} collective-permute-done((f32[8,128]{1,0:T(8,128)S(1)}, f32[8,128]{1,0:T(8,128)S(1)}, u32[]{:S(2)}, u32[]{:S(2)}) %collective-permute-start.7) | collective-permute-done | bytes 4128 | tf_op jit(solution)/shard_map/ppermute | solution.py:663
  16.7 2.7 %collective-permute-done.6.before_ref = f32[8,128]{1,0:T(8,128)S(1)} collective-permute-done((f32[8,128]{1,0:T(8,128)S(1)}, f32[8,128]{1,0:T(8,128)S(1)}, u32[]{:S(2)}, u32[]{:S(2)}) %collective-permute-start.6) | collective-permute-done | bytes 4128 | tf_op jit(solution)/shard_map/ppermute | solution.py:662
  21.0 1.5 %collective-permute-start.9 = (f32[2,20,8,128]{3,2,1,0:T(8,128)S(1)}, f32[2,20,8,128]{3,2,1,0:T(8,128)S(1)}, u32[]{:S(2)}, u32[]{:S(2)}) collective-permute-start(f32[2,20,8,128]{3,2,1,0:T(8,128)S(1)} %get-tuple-element.72), channel_id=1, source_target_pairs={{0,8},{4,12},{8,0},{12,4},{1,9},{5,13},{9,1},{13,5},{2,10},{6,14},... | collective-permute-start | bytes 491528 | tf_op jit(solution)/shard_map/ppermute | solution.py:617
  24.0 1.5 %collective-permute-start.1 = (f32[2,40,8,128]{3,2,1,0:T(8,128)S(1)}, f32[2,40,8,128]{3,2,1,0:T(8,128)S(1)}, u32[]{:S(2)}, u32[]{:S(2)}) collective-permute-start(f32[2,40,8,128]{3,2,1,0:T(8,128)S(1)} %get-tuple-element.52), channel_id=1, source_target_pairs={{0,8},{4,12},{8,0},{12,4},{1,9},{5,13},{9,1},{13,5},{2,10},{6,14},... | collective-permute-start | bytes 983048 | tf_op jit(solution)/shard_map/ppermute | solution.py:617
  26.7 2.3 %collective-permute-start.2 = (f32[2,40,8,128]{3,2,1,0:T(8,128)S(1)}, f32[2,40,8,128]{3,2,1,0:T(8,128)S(1)}, u32[]{:S(2)}, u32[]{:S(2)}) collective-permute-start(f32[2,40,8,128]{3,2,1,0:T(8,128)S(1)} %get-tuple-element.53), channel_id=1, source_target_pairs={{0,12},{4,8},{8,4},{12,0},{1,13},{5,9},{9,5},{13,1},{2,14},{6,10},... | collective-permute-start | bytes 983048 | tf_op jit(solution)/shard_map/ppermute | solution.py:617
  29.0 8.1 %collective-permute-done.9.refs_6_ = f32[2,20,8,128]{3,2,1,0:T(8,128)S(1)} collective-permute-done((f32[2,20,8,128]{3,2,1,0:T(8,128)S(1)}, f32[2,20,8,128]{3,2,1,0:T(8,128)S(1)}, u32[]{:S(2)}, u32[]{:S(2)}) %collective-permute-start.9) | collective-permute-done | bytes 163872 | tf_op jit(solution)/shard_map/ppermute | solution.py:617
  37.1 2.1 %collective-permute-start.11 = (f32[61,8,128]{2,1,0:T(8,128)S(1)}, f32[61,8,128]{2,1,0:T(8,128)S(1)}, u32[]{:S(2)}, u32[]{:S(2)}) collective-permute-start(f32[61,8,128]{2,1,0:T(8,128)S(1)} %get-tuple-element.77), channel_id=1, source_target_pairs={{0,4},{4,0},{8,12},{12,8},{1,5},{5,1},{9,13},{13,9},{2,6},{6,2},{1... | collective-permute-start | bytes 749576 | tf_op jit(solution)/shard_map/ppermute | solution.py:617
  40.8 9.6 %collective-permute-done.1.refs_2_ = f32[2,40,8,128]{3,2,1,0:T(8,128)S(1)} collective-permute-done((f32[2,40,8,128]{3,2,1,0:T(8,128)S(1)}, f32[2,40,8,128]{3,2,1,0:T(8,128)S(1)}, u32[]{:S(2)}, u32[]{:S(2)}) %collective-permute-start.1) | collective-permute-done | bytes 327712 | tf_op jit(solution)/shard_map/ppermute | solution.py:617
  50.5 3.5 %shard_map.70 = (f32[2,80,32,128]{3,2,1,0:T(8,128)S(1)}, f32[80,32,128]{2,1,0:T(8,128)S(1)}) custom-call(s32[1]{0:T(128)} %bitcast.1.place_ref, f32[2,40,8,128]{3,2,1,0:T(8,128)S(1)} %get-tuple-element.50.refs_0_, f32[2,40,8,128]{3,2,1,0:T(8,128)S(1)} %collective-permute-done.refs_1_, f32[2,40,8,128]{3,2,1,0:T(8,128)S(1)} %collective-permute-done.1.refs_2_, ...), custom_call_target="tpu_custom_call" | custom-call | flops 1000000 | tf_op jit(solution)/shard_map/pallas_call | solution.py:599
  54.0 15.1 %shard_map.71 = (f32[80,32,128]{2,1,0:T(8,128)S(1)}, f32[80,32,128]{2,1,0:T(8,128)S(1)}, f32[80,32,128]{2,1,0:T(8,128)S(1)}, f32[80,32,128]{2,1,0:T(8,128)S(1)},...) custom-call(s32[2]{0:T(128)S(1)} %pad_add_fusion.where_ref, ...), custom_call_target="tpu_custom_call" | custom-call | flops 1000000 | tf_op jit(solution)/shard_map/pallas_call | solution.py:599
  69.1 10.8 %all_to_all.5.sums_ref = f32[16,8,128]{2,1,0:T(8,128)S(1)} all-to-all(f32[16,8,128]{2,1,0:T(8,128)S(1)} %get-tuple-element.80), channel_id=1, replica_groups=mesh['group'=2,'gx'=4,'gy'=4] {'gx','gy'}, dimensions={0} | all-to-all | bytes 131072 | tf_op jit(solution)/shard_map/all_to_all | solution.py:682
  81.4 1.7 %shard_map.74 = (f32[40,8,128]{2,1,0:T(8,128)S(1)}, f32[40,8,128]{2,1,0:T(8,128)S(1)}, f32[40,8,128]{2,1,0:T(8,128)S(1)}, f32[40,8,128]{2,1,0:T(8,128)S(1)}) custom-call(s32[2]{0:T(128)S(1)} %pad_add_fusion.where_ref, f32[13,8,128]{2,1,0:T(8,128)S(1)} %shard_map.72.coefs_ref, f32[80,32,128]{2,1,0:T(8,128)S(1)} %get-tuple-element.81.refs_0_, ...), custom_call_target="tpu_custom_call" | custom-call | flops 1000000 | tf_op jit(solution)/shard_map/pallas_call | solution.py:599
  84.6 2.1 %collective-permute-start.19 = (f32[40,8,128]{2,1,0:T(8,128)S(1)}, f32[40,8,128]{2,1,0:T(8,128)S(1)}, u32[]{:S(2)}, u32[]{:S(2)}) collective-permute-start(f32[40,8,128]{2,1,0:T(8,128)S(1)} %get-tuple-element.95), channel_id=1, source_target_pairs={{0,12},{4,8},{8,4},{12,0},{1,13},{5,9},{9,5},{13,1},{2,14},{6,10},... | collective-permute-start | bytes 491528 | tf_op jit(solution)/shard_map/ppermute | solution.py:617
  86.7 1.7 %shard_map.73 = (f32[40,8,128]{2,1,0:T(8,128)S(1)}, f32[40,8,128]{2,1,0:T(8,128)S(1)}, f32[40,8,128]{2,1,0:T(8,128)S(1)}, f32[40,8,128]{2,1,0:T(8,128)S(1)}) custom-call(s32[2]{0:T(128)S(1)} %pad_add_fusion.where_ref, f32[13,8,128]{2,1,0:T(8,128)S(1)} %shard_map.72.coefs_ref, f32[80,32,128]{2,1,0:T(8,128)S(1)} %get-tuple-element.81.refs_0_, ...), custom_call_target="tpu_custom_call" | custom-call | flops 1000000 | tf_op jit(solution)/shard_map/pallas_call | solution.py:599
  89.8 2.1 %collective-permute-start.16 = (f32[40,8,128]{2,1,0:T(8,128)S(1)}, f32[40,8,128]{2,1,0:T(8,128)S(1)}, u32[]{:S(2)}, u32[]{:S(2)}) collective-permute-start(f32[40,8,128]{2,1,0:T(8,128)S(1)} %get-tuple-element.91), channel_id=1, source_target_pairs={{0,12},{4,8},{8,4},{12,0},{1,13},{5,9},{9,5},{13,1},{2,14},{6,10},... | collective-permute-start | bytes 491528 | tf_op jit(solution)/shard_map/ppermute | solution.py:617
  91.9 2.2 %collective-permute-done.18.refs_2_ = f32[40,8,128]{2,1,0:T(8,128)S(1)} collective-permute-done((f32[40,8,128]{2,1,0:T(8,128)S(1)}, f32[40,8,128]{2,1,0:T(8,128)S(1)}, u32[]{:S(2)}, u32[]{:S(2)}) %collective-permute-start.18) | collective-permute-done | bytes 163872 | tf_op jit(solution)/shard_map/ppermute | solution.py:617
  94.1 1.6 %shard_map.75 = (f32[1,80,8,256]{3,2,1,0:T(8,128)}, f32[1,80,8,256]{3,2,1,0:T(8,128)}) custom-call(s32[2]{0:T(128)S(1)} %pad_add_fusion.where_ref, f32[40,8,128]{2,1,0:T(8,128)S(1)} %get-tuple-element.92.refs_0_, f32[40,8,128]{2,1,0:T(8,128)S(1)} %collective-permute-done.17.refs_1_, f32[40,8,128]{2,1,0:T(8,128)S(1)} %collective-permute-done.18.refs_2_, ...), custom_call_target="tpu_custom_call" | custom-call | flops 1000000 | tf_op jit(solution)/shard_map/pallas_call | solution.py:599
  95.7 2.3 %collective-permute-done.15.refs_2_ = f32[40,8,128]{2,1,0:T(8,128)S(1)} collective-permute-done((f32[40,8,128]{2,1,0:T(8,128)S(1)}, f32[40,8,128]{2,1,0:T(8,128)S(1)}, u32[]{:S(2)}, u32[]{:S(2)}) %collective-permute-start.15) | collective-permute-done | bytes 163872 | tf_op jit(solution)/shard_map/ppermute | solution.py:617
  98.0 1.6 %shard_map.76 = (f32[1,80,8,256]{3,2,1,0:T(8,128)}, f32[1,80,8,256]{3,2,1,0:T(8,128)}) custom-call(s32[2]{0:T(128)S(1)} %pad_add_fusion.where_ref, f32[40,8,128]{2,1,0:T(8,128)S(1)} %get-tuple-element.88.refs_0_, f32[40,8,128]{2,1,0:T(8,128)S(1)} %collective-permute-done.14.refs_1_, ...), custom_call_target="tpu_custom_call", output_to_operand_aliasing={{0}: (5, {}), {1}: (6, {})} | custom-call | flops 1000000 | tf_op jit(solution)/shard_map/pallas_call | solution.py:599
  (31 shorter events, 11.2 us)
Async XLA Ops:
  5.2 6.9 %collective-permute-start.5 = (f32[8,256]{1,0:T(8,128)S(1)}, f32[8,256]{1,0:T(8,128)S(1)}, u32[]{:S(2)}, u32[]{:S(2)}) collective-permute-start(f32[8,256]{1,0:T(8,128)S(1)} %get-tuple-element.57), channel_id=1, source_target_pairs={{0,16},{16,0},{1,17},{17,1},{2,18},{18,2},{3,19},{19,3},{4,20},{20... | collective-permute-start | bytes 24584 | tf_op jit(solution)/shard_map/ppermute | solution.py:59
  5.7 13.6 %collective-permute-start.3 = (f32[3,10,8,128]{3,2,1,0:T(8,128)}, f32[3,10,8,128]{3,2,1,0:T(8,128)S(1)}, u32[]{:S(2)}, u32[]{:S(2)}) collective-permute-start(f32[3,10,8,128]{3,2,1,0:T(8,128)} %get-tuple-element.54), channel_id=1, source_target_pairs={{0,1},{1,2},{2,3},{3,0},{4,5},{5,6},{6,7},{7,4},{8,9},{9,10},{10,1... | collective-permute-start | bytes 368648 | tf_op jit(solution)/shard_map/ppermute | solution.py:660
  8.4 11.0 %collective-permute-start.4 = (f32[3,10,8,128]{3,2,1,0:T(8,128)}, f32[3,10,8,128]{3,2,1,0:T(8,128)S(1)}, u32[]{:S(2)}, u32[]{:S(2)}) collective-permute-start(f32[3,10,8,128]{3,2,1,0:T(8,128)} %get-tuple-element.55), channel_id=1, source_target_pairs={{0,3},{1,0},{2,1},{3,2},{4,7},{5,4},{6,5},{7,6},{8,11},{9,8},{10,9... | collective-permute-start | bytes 368648 | tf_op jit(solution)/shard_map/ppermute | solution.py:660
  10.4 29.4 %collective-permute-start = (f32[2,40,8,128]{3,2,1,0:T(8,128)S(1)}, f32[2,40,8,128]{3,2,1,0:T(8,128)S(1)}, u32[]{:S(2)}, u32[]{:S(2)}) collective-permute-start(f32[2,40,8,128]{3,2,1,0:T(8,128)S(1)} %get-tuple-element.51), channel_id=1, source_target_pairs={{0,4},{4,0},{8,12},{12,8},{1,5},{5,1},{9,13},{13,9},{2,6},{6,2},{1... | collective-permute-start | bytes 983048 | tf_op jit(solution)/shard_map/ppermute | solution.py:617
  12.1 4.6 %collective-permute-start.7 = (f32[8,128]{1,0:T(8,128)S(1)}, f32[8,128]{1,0:T(8,128)S(1)}, u32[]{:S(2)}, u32[]{:S(2)}) collective-permute-start(f32[8,128]{1,0:T(8,128)S(1)} %get-tuple-element.98), channel_id=1, source_target_pairs={{0,3},{1,0},{2,1},{3,2},{4,7},{5,4},{6,5},{7,6},{8,11},{9,8},{10,9... | collective-permute-start | bytes 12296 | tf_op jit(solution)/shard_map/ppermute | solution.py:663
  14.0 5.4 %collective-permute-start.6 = (f32[8,128]{1,0:T(8,128)S(1)}, f32[8,128]{1,0:T(8,128)S(1)}, u32[]{:S(2)}, u32[]{:S(2)}) collective-permute-start(f32[8,128]{1,0:T(8,128)S(1)} %get-tuple-element.99), channel_id=1, source_target_pairs={{0,1},{1,2},{2,3},{3,0},{4,5},{5,6},{6,7},{7,4},{8,9},{9,10},{10,1... | collective-permute-start | bytes 12296 | tf_op jit(solution)/shard_map/ppermute | solution.py:662
  20.5 6.3 %collective-permute-start.8 = (f32[2,20,8,128]{3,2,1,0:T(8,128)S(1)}, f32[2,20,8,128]{3,2,1,0:T(8,128)S(1)}, u32[]{:S(2)}, u32[]{:S(2)}) collective-permute-start(f32[2,20,8,128]{3,2,1,0:T(8,128)S(1)} %get-tuple-element.71), channel_id=1, source_target_pairs={{0,4},{4,0},{8,12},{12,8},{1,5},{5,1},{9,13},{13,9},{2,6},{6,2},{1... | collective-permute-start | bytes 491528 | tf_op jit(solution)/shard_map/ppermute | solution.py:617
  21.0 16.1 %collective-permute-start.9 = (f32[2,20,8,128]{3,2,1,0:T(8,128)S(1)}, f32[2,20,8,128]{3,2,1,0:T(8,128)S(1)}, u32[]{:S(2)}, u32[]{:S(2)}) collective-permute-start(f32[2,20,8,128]{3,2,1,0:T(8,128)S(1)} %get-tuple-element.72), channel_id=1, source_target_pairs={{0,8},{4,12},{8,0},{12,4},{1,9},{5,13},{9,1},{13,5},{2,10},{6,14},... | collective-permute-start | bytes 491528 | tf_op jit(solution)/shard_map/ppermute | solution.py:617
  22.5 16.8 %collective-permute-start.10 = (f32[2,20,8,128]{3,2,1,0:T(8,128)S(1)}, f32[2,20,8,128]{3,2,1,0:T(8,128)S(1)}, u32[]{:S(2)}, u32[]{:S(2)}) collective-permute-start(f32[2,20,8,128]{3,2,1,0:T(8,128)S(1)} %get-tuple-element.73), channel_id=1, source_target_pairs={{0,12},{4,8},{8,4},{12,0},{1,13},{5,9},{9,5},{13,1},{2,14},{6,10},... | collective-permute-start | bytes 491528 | tf_op jit(solution)/shard_map/ppermute | solution.py:617
  24.0 26.5 %collective-permute-start.1 = (f32[2,40,8,128]{3,2,1,0:T(8,128)S(1)}, f32[2,40,8,128]{3,2,1,0:T(8,128)S(1)}, u32[]{:S(2)}, u32[]{:S(2)}) collective-permute-start(f32[2,40,8,128]{3,2,1,0:T(8,128)S(1)} %get-tuple-element.52), channel_id=1, source_target_pairs={{0,8},{4,12},{8,0},{12,4},{1,9},{5,13},{9,1},{13,5},{2,10},{6,14},... | collective-permute-start | bytes 983048 | tf_op jit(solution)/shard_map/ppermute | solution.py:617
  26.7 23.7 %collective-permute-start.2 = (f32[2,40,8,128]{3,2,1,0:T(8,128)S(1)}, f32[2,40,8,128]{3,2,1,0:T(8,128)S(1)}, u32[]{:S(2)}, u32[]{:S(2)}) collective-permute-start(f32[2,40,8,128]{3,2,1,0:T(8,128)S(1)} %get-tuple-element.53), channel_id=1, source_target_pairs={{0,12},{4,8},{8,4},{12,0},{1,13},{5,9},{9,5},{13,1},{2,14},{6,10},... | collective-permute-start | bytes 983048 | tf_op jit(solution)/shard_map/ppermute | solution.py:617
  37.1 16.8 %collective-permute-start.11 = (f32[61,8,128]{2,1,0:T(8,128)S(1)}, f32[61,8,128]{2,1,0:T(8,128)S(1)}, u32[]{:S(2)}, u32[]{:S(2)}) collective-permute-start(f32[61,8,128]{2,1,0:T(8,128)S(1)} %get-tuple-element.77), channel_id=1, source_target_pairs={{0,4},{4,0},{8,12},{12,8},{1,5},{5,1},{9,13},{13,9},{2,6},{6,2},{1... | collective-permute-start | bytes 749576 | tf_op jit(solution)/shard_map/ppermute | solution.py:617
  39.3 14.7 %collective-permute-start.12 = (f32[61,8,128]{2,1,0:T(8,128)S(1)}, f32[61,8,128]{2,1,0:T(8,128)S(1)}, u32[]{:S(2)}, u32[]{:S(2)}) collective-permute-start(f32[61,8,128]{2,1,0:T(8,128)S(1)} %get-tuple-element.78), channel_id=1, source_target_pairs={{0,8},{4,12},{8,0},{12,4},{1,9},{5,13},{9,1},{13,5},{2,10},{6,14},... | collective-permute-start | bytes 749576 | tf_op jit(solution)/shard_map/ppermute | solution.py:617
  39.8 14.2 %collective-permute-start.13 = (f32[61,8,128]{2,1,0:T(8,128)S(1)}, f32[61,8,128]{2,1,0:T(8,128)S(1)}, u32[]{:S(2)}, u32[]{:S(2)}) collective-permute-start(f32[61,8,128]{2,1,0:T(8,128)S(1)} %get-tuple-element.79), channel_id=1, source_target_pairs={{0,12},{4,8},{8,4},{12,0},{1,13},{5,9},{9,5},{13,1},{2,14},{6,10},... | collective-permute-start | bytes 749576 | tf_op jit(solution)/shard_map/ppermute | solution.py:617
  83.1 6.7 %collective-permute-start.17 = (f32[40,8,128]{2,1,0:T(8,128)S(1)}, f32[40,8,128]{2,1,0:T(8,128)S(1)}, u32[]{:S(2)}, u32[]{:S(2)}) collective-permute-start(f32[40,8,128]{2,1,0:T(8,128)S(1)} %get-tuple-element.93), channel_id=1, source_target_pairs={{0,4},{4,0},{8,12},{12,8},{1,5},{5,1},{9,13},{13,9},{2,6},{6,2},{1... | collective-permute-start | bytes 491528 | tf_op jit(solution)/shard_map/ppermute | solution.py:617
  83.9 10.2 %collective-permute-start.18 = (f32[40,8,128]{2,1,0:T(8,128)S(1)}, f32[40,8,128]{2,1,0:T(8,128)S(1)}, u32[]{:S(2)}, u32[]{:S(2)}) collective-permute-start(f32[40,8,128]{2,1,0:T(8,128)S(1)} %get-tuple-element.94), channel_id=1, source_target_pairs={{0,8},{4,12},{8,0},{12,4},{1,9},{5,13},{9,1},{13,5},{2,10},{6,14},... | collective-permute-start | bytes 491528 | tf_op jit(solution)/shard_map/ppermute | solution.py:617
  84.6 9.5 %collective-permute-start.19 = (f32[40,8,128]{2,1,0:T(8,128)S(1)}, f32[40,8,128]{2,1,0:T(8,128)S(1)}, u32[]{:S(2)}, u32[]{:S(2)}) collective-permute-start(f32[40,8,128]{2,1,0:T(8,128)S(1)} %get-tuple-element.95), channel_id=1, source_target_pairs={{0,12},{4,8},{8,4},{12,0},{1,13},{5,9},{9,5},{13,1},{2,14},{6,10},... | collective-permute-start | bytes 491528 | tf_op jit(solution)/shard_map/ppermute | solution.py:617
  88.3 7.4 %collective-permute-start.14 = (f32[40,8,128]{2,1,0:T(8,128)S(1)}, f32[40,8,128]{2,1,0:T(8,128)S(1)}, u32[]{:S(2)}, u32[]{:S(2)}) collective-permute-start(f32[40,8,128]{2,1,0:T(8,128)S(1)} %get-tuple-element.89), channel_id=1, source_target_pairs={{0,4},{4,0},{8,12},{12,8},{1,5},{5,1},{9,13},{13,9},{2,6},{6,2},{1... | collective-permute-start | bytes 491528 | tf_op jit(solution)/shard_map/ppermute | solution.py:617
  89.1 8.9 %collective-permute-start.15 = (f32[40,8,128]{2,1,0:T(8,128)S(1)}, f32[40,8,128]{2,1,0:T(8,128)S(1)}, u32[]{:S(2)}, u32[]{:S(2)}) collective-permute-start(f32[40,8,128]{2,1,0:T(8,128)S(1)} %get-tuple-element.90), channel_id=1, source_target_pairs={{0,8},{4,12},{8,0},{12,4},{1,9},{5,13},{9,1},{13,5},{2,10},{6,14},... | collective-permute-start | bytes 491528 | tf_op jit(solution)/shard_map/ppermute | solution.py:617
  89.8 8.2 %collective-permute-start.16 = (f32[40,8,128]{2,1,0:T(8,128)S(1)}, f32[40,8,128]{2,1,0:T(8,128)S(1)}, u32[]{:S(2)}, u32[]{:S(2)}) collective-permute-start(f32[40,8,128]{2,1,0:T(8,128)S(1)} %get-tuple-element.91), channel_id=1, source_target_pairs={{0,12},{4,8},{8,4},{12,0},{1,13},{5,9},{9,5},{13,1},{2,14},{6,10},... | collective-permute-start | bytes 491528 | tf_op jit(solution)/shard_map/ppermute | solution.py:617

commit v6 on v5

--- a/solution.py
+++ b/solution.py
@@ -15,7 +15,6 @@
 HALO = 16
 SHIFTS = (0.0, 0.75, 1.5, 0.25, 1.75, 1.0)
 UNROLL = 16
-PARTS = 2
 PAIRS = tuple((i, j) for i in range(ITERS + 1) for j in range(i + 1) if j < ITERS)
 
 
@@ -159,6 +158,18 @@
         return carry
 
     lax.fori_loop(0, total // size, step, 0)
+
+
+def spans(start, stop, size, body):
+    def step(g, carry):
+        body(start + g * size, size)
+        return carry
+
+    whole = (stop - start) // size
+    if whole:
+        lax.fori_loop(0, whole, step, 0)
+    if (stop - start) % size:
+        body(start + whole * size, (stop - start) % size)
 
 
 def slots_of(rows):
@@ -292,14 +303,17 @@
 
 
 def merge_kernel(place_ref, edge_ref, low_ref, high_ref, term_ref, before_ref, after_ref, *refs):
-    count = len(refs) // 5
-    rims, owns, force_rims, rims_out, force_out = [refs[count * n : count * (n + 1)] for n in range(5)]
+    count = len(refs) // 6
+    rims, owns, force_rims, rims_out, *force_out = [refs[count * n : count * (n + 1)] for n in range(6)]
     groups = low_ref.shape[1]
+    half_groups = groups // 2
     odd = slots_of(SUBLANES) % 2 == 1
     first = [jnp.where(odd, place_ref[0], -1) == k for k in range(count)]
     last = [jnp.where(odd, -1, place_ref[0] ^ (count - 1)) == k for k in range(count)]
 
-    def step(q):
+    def step(side, i):
+        q = side * half_groups + i
+        out = force_out[side]
         for k in range(3):
             before, after = low_ref[k, q], high_ref[k, q]
             if k == 0:
@@ -311,18 +325,16 @@
                     rim = force_rims[n][g] if k == 2 else rims[n][k, g]
                     rim = jnp.where(last[n], afters[group], jnp.where(first[n], befores[group], rim))
                     if k == 2:
-                        force_out[n][4 * groups + g] = rim
+                        out[n][4 * half_groups + 2 * i + group] = rim
                     else:
                         rims_out[n][k, g] = rim
         for n in range(count):
             for m in range(4):
-                force_out[n][4 * q + m] = owns[n][4 * q + m]
-
-    def pair(start):
-        step(start)
-        step(start + 1)
-
-    blocks(groups, 2, pair)
+                out[n][4 * i + m] = owns[n][4 * q + m]
+
+    for i in range(half_groups):
+        step(0, i)
+        step(1, i)
     lane = lanes_of(SUBLANES)
     half = LANES // 2
     pieces = [term_ref[:, LANES * p : LANES * (p + 1)] for p in range(count // 2)]
@@ -336,8 +348,9 @@
             own, right, left = halves[p], halves[p + 1], halves[p]
         outer = jnp.where(lane >= LANES - HALO, left, 0.0)
         windows.append(jnp.where(lane < half, own, jnp.where(lane < half + HALO, right, outer)))
-    for ref, value in zip(force_out, by_partner(place_ref[0], windows)):
-        ref[6 * groups] = value
+    for n, value in enumerate(by_partner(place_ref[0], windows)):
+        force_out[0][n][6 * half_groups] = value
+        force_out[1][n][6 * half_groups] = value
 
 
 def window_of(own, rim, j, fill):
@@ -418,53 +431,51 @@
     ref[layers - 1] = jnp.zeros((rows + 2 * SUBLANES, LANES), jnp.float32)
 
 
-def krylov_kernel(where_ref, scale_ref, factor_ref, *refs):
-    count = len(refs) - ITERS - 1 - 4
-    force_refs = refs[:count]
-    basis = refs[count : count + ITERS + 1]
-    sums_ref, even_ref, odd_ref, gram_ref = refs[count + ITERS + 1 :]
-    held = (even_ref, odd_ref)
-    layers, rows = factor_ref.shape[:2]
-    inner = pl.ds(SUBLANES, rows)
-    for ref in held:
-        clear_edges(ref, rows)
+def begin_part(where_ref, scale_ref, factor_ref, force_refs, vector_ref, held_ref, start, origin):
+    count = len(force_refs)
+    groups = (force_refs[0].shape[0] - 1) // 3
     places = partner_rows(where_ref[1], count)
     padded = partner_rows(where_ref[1], count, SUBLANES)
 
-    def begin(first):
-        for u in range(4):
+    def begin(first, number):
+        for u in range(number):
             g = first + u
             for n in range(count):
-                term = force_refs[n][3 * layers // 4]
+                term = force_refs[n][3 * groups]
                 for j in range(4):
-                    layer = 4 * g + j
-                    source = window_of(force_refs[n][2 * g + j // 2], force_refs[n][layers // 2 + g], j, 0.0)
+                    layer = start + 4 * g + j
+                    source = window_of(force_refs[n][2 * g + j // 2], force_refs[n][2 * groups + g], j, 0.0)
                     source = source + term * jnp.where(layer == where_ref[0], 1.0, 0.0)
                     vector = source * scale_ref[0, layer, places[n]]
-                    basis[0][layer, places[n]] = vector
-                    odd_ref[layer + 1, padded[n]] = factor_ref[layer, places[n]] * vector
-
-    blocks(layers // 4, 4, begin)
-    for k in range(ITERS):
-        source_ref, target_ref = held[(k + 1) % 2], held[k % 2]
-
-        def apply(first):
-            for layer in range(UNROLL):
-                layer = first + layer
-                factor = factor_ref[layer]
-                spread = stencil(source_ref, layer, rows)
-                before = basis[k][layer]
-                before = (1.0 - SHIFTS[k]) * before if SHIFTS[k] else before
-                vector = before - factor * spread
-                basis[k + 1][layer] = vector
-                if k + 1 < ITERS:
-                    target_ref[layer + 1, inner] = factor * vector
-
-        blocks(layers, UNROLL, apply)
-
+                    vector_ref[layer - origin, places[n]] = vector
+                    held_ref[layer - origin + 1, padded[n]] = factor_ref[layer, places[n]] * vector
+
+    spans(0, groups, 4, begin)
+
+
+def apply_part(k, factor_ref, basis, held, start, stop, origin):
+    rows = factor_ref.shape[1]
+    source_ref, target_ref = held[k % 2], held[(k + 1) % 2]
+
+    def apply(first, number):
+        for layer in range(number):
+            layer = first + layer
+            factor = factor_ref[layer]
+            spread = stencil(source_ref, layer - origin, rows)
+            before = basis[k][layer - origin]
+            before = (1.0 - SHIFTS[k]) * before if SHIFTS[k] else before
+            vector = before - factor * spread
+            basis[k + 1][layer - origin] = vector
+            if k + 1 < ITERS:
+                target_ref[layer - origin + 1, pl.ds(SUBLANES, rows)] = factor * vector
+
+    spans(start, stop, UNROLL, apply)
+
+
+def products_part(basis, gram_ref, layers):
+    rows = basis[0].shape[1]
     lane = lanes_of(SUBLANES)
     half = LANES // 2
-    gram_ref[...] = jnp.zeros(gram_ref.shape, jnp.float32)
 
     def products(first):
         sums = [None] * len(PAIRS)
@@ -484,6 +495,44 @@
             gram_ref[1, p] = low
 
     blocks(layers, 8, products)
+
+
+def lower_kernel(where_ref, scale_ref, factor_ref, *refs):
+    count = len(refs) - ITERS - 1 - 3
+    basis = refs[count : count + ITERS + 1]
+    gram_ref, *held = refs[count + ITERS + 1 :]
+    half, rows = basis[0].shape[:2]
+    for ref in held:
+        clear_edges(ref, rows)
+    begin_part(where_ref, scale_ref, factor_ref, refs[:count], basis[0], held[0], 0, 0)
+    for k in range(ITERS):
+        apply_part(k, factor_ref, basis, held, 0, half - 1 - k, 0)
+    gram_ref[...] = jnp.zeros(gram_ref.shape, jnp.float32)
+    products_part(basis, gram_ref, half - 8)
+
+
+def upper_kernel(where_ref, scale_ref, factor_ref, *refs):
+    count = len(refs) - 2 * (ITERS + 1) - 5
+    below = refs[count : count + ITERS + 1]
+    part_ref = refs[count + ITERS + 1]
+    basis = refs[count + ITERS + 2 : count + 2 * ITERS + 3]
+    sums_ref, gram_ref, *held = refs[count + 2 * ITERS + 3 :]
+    half, rows = below[0].shape[:2]
+    layers = factor_ref.shape[0]
+    origin = half - 8
+    lane = lanes_of(SUBLANES)
+    for ref in held:
+        clear_edges(ref, rows)
+    for k in range(ITERS + 1):
+        for layer in range(origin, half - k):
+            basis[k][layer - origin] = below[k][layer]
+    begin_part(where_ref, scale_ref, factor_ref, refs[:count], basis[0], held[0], half, origin)
+    for k in range(ITERS):
+        for layer in (half - k - 2, half - k - 1):
+            held[k % 2][layer - origin + 1, pl.ds(SUBLANES, rows)] = factor_ref[layer] * below[k][layer]
+        apply_part(k, factor_ref, basis, held, half - 1 - k, layers, origin)
+    gram_ref[...] = part_ref[...]
+    products_part(basis, gram_ref, layers - origin)
     high, low = gram_ref[0, :, 0], gram_ref[1, :, 0]
     for row in range(1, SUBLANES):
         high, low = add_pairs(high, low, gram_ref[0, :, row], gram_ref[1, :, row])
@@ -564,7 +613,7 @@
         for layer in range(8):
             layer = first + layer
             for ref, part in zip(out_refs, rows):
-                vectors = [basis_ref[start + layer, part] for basis_ref in basis]
+                vectors = [basis_ref[layer, part] for basis_ref in basis]
                 answered = tree_sum([c * v for c, v in zip(answer, vectors)]) * scale_ref[0, start + layer, part]
                 left = tree_sum([c * v for c, v in zip(residual, vectors)]) * scale_ref[1, start + layer, part]
                 ref[layer] = jnp.where(lane < half, answered, turned(left, half))
@@ -586,10 +635,12 @@
                 low, high = got[2 * p : 2 * p + 2]
                 solved[layer, :, place] = jnp.where(lane < half, low, turned(high, half))
                 left[layer, :, place] = jnp.where(lane < half, turned(low, half), high)
-    for n, (held, target) in enumerate(((solved, solution_ref), (left, residual_ref))):
-        copy = pltpu.make_async_copy(held, target.at[0, pl.ds(start, depth)], sems.at[n])
-        copy.start()
-        copies.append(copy)
+        for n, (held, target) in enumerate(((solved, solution_ref), (left, residual_ref))):
+            copy = pltpu.make_async_copy(
+                held.at[pl.ds(first, 8)], target.at[0, pl.ds(start + first, 8)], sems.at[n, first // 8]
+            )
+            copy.start()
+            copies.append(copy)
     for copy in copies:
         copy.wait()
 
@@ -661,41 +712,51 @@
     term = active * received
     term_before = lax.ppermute(term[:, -LANES:], "gy", up)
     term_after = lax.ppermute(term[:, :LANES], "gy", down)
-    force = (own[0] + rim[0] + 1, block_x, LANES)
+    force = ((own[0] + rim[0]) // 2 + 1, block_x, LANES)
     merged = call(
-        merge_kernel, [(2, *rim)] * count_x + [force] * count_x,
+        merge_kernel, [(2, *rim)] * count_x + [force] * 2 * count_x,
         (place_x[None], inside, before, after, term, term_before, term_after, *left[0], *left[1], *left[2]), smem=2,
     )
     rims = exchanged(merged[:count_x])
-    forces = exchanged(merged[count_x:])
+    forces = []
+    for n in range(2):
+        forces.append(exchanged(merged[count_x * (n + 1) : count_x * (n + 2)]))
     padded = (layers + 2, rows + 2 * SUBLANES, LANES)
     window = (layers, rows, LANES)
     scale, factor = call(
         scale_kernel, [(2,) + window, window], (place_x[None], *owns, *rims), smem=1,
         scratch=[padded, window],
     )
-    *basis, sums = call(
-        krylov_kernel, [window] * (ITERS + 1) + [(count_x * count_y, SUBLANES, LANES)],
-        (where, scale, factor, *forces), smem=1,
-        scratch=[padded] * 2 + [(2, 32, SUBLANES, LANES)], limit=32,
+    half = layers // 2
+    depths = (half - 8, layers - half + 8)
+    gram = (2, 32, SUBLANES, LANES)
+    *below, part = call(
+        lower_kernel, [(half, rows, LANES)] * (ITERS + 1) + [gram],
+        (where, scale, factor, *forces[0]), smem=1, scratch=[(half + 2,) + padded[1:]] * 2, limit=32,
+    )
+    *beyond, sums = call(
+        upper_kernel,
+        [(depths[1], rows, LANES)] * (ITERS + 1) + [(count_x * count_y, SUBLANES, LANES)],
+        (where, scale, factor, *forces[1], *below, part), smem=1,
+        scratch=[gram] + [(depths[1] + 2,) + padded[1:]] * 2, limit=32,
     )
     sums = lax.all_to_all(sums, ("gx", "gy"), 0, 0, tiled=True)
     (coefs,) = call(solve_kernel, [(2 * ITERS + 1, SUBLANES, LANES)], (sums,), scratch=[(SUBLANES, LANES)])
-    depth = layers // PARTS
+    starts = (0, depths[0])
     arrived = []
-    for n in range(PARTS):
+    for start, depth, basis in zip(starts, depths, (below, beyond)):
         mixed = call(
-            functools.partial(combine_kernel, n * depth, depth),
+            functools.partial(combine_kernel, start, depth),
             [(depth, block_x, LANES)] * count_x, (where, coefs, *basis, scale), smem=1,
         )
         arrived.append(exchanged(mixed))
     outs = ()
-    for n in range(PARTS):
+    for n, (start, depth) in enumerate(zip(starts, depths)):
         outs = tuple(
             call(
-                functools.partial(finish_kernel, n * depth, depth, count_x),
+                functools.partial(finish_kernel, start, depth, count_x),
                 [forcing.shape] * 2, (where, *arrived[n], *outs), smem=1, tail=len(outs), hbm_outs=True,
-                scratch=[(depth, block_x, block_y)] * 2 + [pltpu.SemaphoreType.DMA((2,))],
+                scratch=[(depth, block_x, block_y)] * 2 + [pltpu.SemaphoreType.DMA((2, depth // 8))],
                 aliases={1 + count_x + i: i for i in range(len(outs))},
             )
         )
@@ -705,7 +766,8 @@
 def fits_windows(layers, block_x, block_y, count_x):
     width = block_y // count_x
     return (
-        layers % (LANES // HALO) == 0
+        layers % 16 == 0
+        and layers >= 32
         and block_x == SUBLANES
         and block_y % LANES == 0
         and 2 * width == LANES

time: 99.9 us -> 108 us (1.081)
  waiting for transfers between devices: 28.6 us -> 32.1 us
  starting transfers between devices: 27 us -> 30 us
  blocking collectives: 10.8 us -> 12.4 us
    ppermute x15 -> x18, waiting for transfers between devices: 23.5 us -> 26.8 us  [exchanged(): lax.ppermute(parts[k], 'gx', [(i, i ^ k) for i in range(count)])]
    ppermute x15 -> x18, starting transfers between devices: 19.7 us -> 22.7 us  [exchanged(): lax.ppermute(parts[k], 'gx', [(i, i ^ k) for i in range(count)])]
    all_to_all x1, blocking collectives: 10.8 us -> 12.4 us  [in_windows(): sums = lax.all_to_all(sums, ('gx', 'gy'), 0, 0, tiled=True)]
    ppermute x1, waiting for transfers between devices: 2.42 us -> 3.85 us  [in_windows(): term_after = lax.ppermute(term[:, :LANES], 'gy', down)]
    ppermute x1, waiting for transfers between devices: 2.69 us -> 1.41 us  [in_windows(): term_before = lax.ppermute(term[:, -LANES:], 'gy', up)]
    pallas_call x9 -> x10, Pallas kernels: 32.2 us -> 32.2 us  [call(): pl.pallas_call(kernel, out_shape=[jax.ShapeDtypeStruct(shape, jnp.float32...]
  transfers between devices with their start and end apart: 20 -> 23, of which waited for: 7 -> 5; matrix products, arithmetic and copies ran while one was open for 0% -> 0% of each run, Pallas kernels for 8% -> 13%
where the time goes in v6:
time: 108 us
  Pallas kernels  32.2 us (30%)
  waiting for transfers between devices  32.1 us (30%)
  starting transfers between devices  30 us (28%)
  blocking collectives  12.4 us (11%)
    pallas_call x10, Pallas kernels, call(): pl.pallas_call(kernel, out_shape=[jax.ShapeDtypeStruct(shape, jnp.float32...  32.2 us
    ppermute x18, waiting for transfers between devices, exchanged(): lax.ppermute(parts[k], 'gx', [(i, i ^ k) for i in range(count)])  26.8 us
    ppermute x18, starting transfers between devices, exchanged(): lax.ppermute(parts[k], 'gx', [(i, i ^ k) for i in range(count)])  22.7 us
    all_to_all x1, blocking collectives, in_windows(): sums = lax.all_to_all(sums, ('gx', 'gy'), 0, 0, tiled=True)  12.4 us
    ppermute x1, waiting for transfers between devices, in_windows(): term_after = lax.ppermute(term[:, :LANES], 'gy', down)  3.85 us
    ppermute x1, starting transfers between devices, in_windows(): lax.ppermute(high, 'gy', up)  2.63 us
  transfers between devices with their start and end apart: 23, of which 5 were waited for; matrix products, arithmetic and copies ran while one was open for 0% of the time, Pallas kernels for 13%

profile of v6, /device:TPU:0, one launch (start us, length us, event | category | flops | bytes accessed | tf_op | source)
XLA Modules:
  0.0 107.7 jit_solution(4586165920646336222)
XLA Ops:
  0.7 3.8 %shard_map.68 = (f32[2,40,8,128]{3,2,1,0:T(8,128)S(1)}, f32[2,40,8,128]{3,2,1,0:T(8,128)S(1)}, f32[2,40,8,128]{3,2,1,0:T(8,128)S(1)}, f32[2,40,8,128]{3,2,1,0:T(...) custom-call(s32[3]{0:T(128)S(1)} %pad_add_fusion.1.where_ref, ...), custom_call_target="tpu_custom_call" | custom-call | flops 1000000 | tf_op jit(solution)/shard_map/pallas_call | solution.py:650
  5.1 2.6 %collective-permute-start.3 = (f32[3,10,8,128]{3,2,1,0:T(8,128)S(1)}, f32[3,10,8,128]{3,2,1,0:T(8,128)S(1)}, u32[]{:S(2)}, u32[]{:S(2)}) collective-permute-start(f32[3,10,8,128]{3,2,1,0:T(8,128)S(1)} %get-tuple-element.66), channel_id=1, source_target_pairs={{0,1},{1,2},{2,3},{3,0},{4,5},{5,6},{6,7},{7,4},{8,9},{9,10},{10,1... | collective-permute-start | bytes 368648 | tf_op jit(solution)/shard_map/ppermute | solution.py:711
  7.7 2.1 %collective-permute-start.4 = (f32[3,10,8,128]{3,2,1,0:T(8,128)S(1)}, f32[3,10,8,128]{3,2,1,0:T(8,128)S(1)}, u32[]{:S(2)}, u32[]{:S(2)}) collective-permute-start(f32[3,10,8,128]{3,2,1,0:T(8,128)S(1)} %get-tuple-element.67), channel_id=1, source_target_pairs={{0,3},{1,0},{2,1},{3,2},{4,7},{5,4},{6,5},{7,6},{8,11},{9,8},{10,9... | collective-permute-start | bytes 368648 | tf_op jit(solution)/shard_map/ppermute | solution.py:711
  9.8 2.0 %collective-permute-start.7 = (f32[8,128]{1,0:T(8,128)S(1)}, f32[8,128]{1,0:T(8,128)S(1)}, u32[]{:S(2)}, u32[]{:S(2)}) collective-permute-start(f32[8,128]{1,0:T(8,128)S(1)} %get-tuple-element.122), channel_id=1, source_target_pairs={{0,3},{1,0},{2,1},{3,2},{4,7},{5,4},{6,5},{7,6},{8,11},{9,8},{10,9... | collective-permute-start | bytes 12296 | tf_op jit(solution)/shard_map/ppermute | solution.py:714
  11.9 3.9 %collective-permute-done.7.after_ref = f32[8,128]{1,0:T(8,128)S(1)} collective-permute-done((f32[8,128]{1,0:T(8,128)S(1)}, f32[8,128]{1,0:T(8,128)S(1)}, u32[]{:S(2)}, u32[]{:S(2)}) %collective-permute-start.7) | collective-permute-done | bytes 4128 | tf_op jit(solution)/shard_map/ppermute | solution.py:714
  17.9 1.6 %collective-permute-start.8 = (f32[2,20,8,128]{3,2,1,0:T(8,128)S(1)}, f32[2,20,8,128]{3,2,1,0:T(8,128)S(1)}, u32[]{:S(2)}, u32[]{:S(2)}) collective-permute-start(f32[2,20,8,128]{3,2,1,0:T(8,128)S(1)} %get-tuple-element.83), channel_id=1, source_target_pairs={{0,4},{4,0},{8,12},{12,8},{1,5},{5,1},{9,13},{13,9},{2,6},{6,2},{1... | collective-permute-start | bytes 491528 | tf_op jit(solution)/shard_map/ppermute | solution.py:668
  20.0 1.5 %collective-permute-start.1 = (f32[2,40,8,128]{3,2,1,0:T(8,128)S(1)}, f32[2,40,8,128]{3,2,1,0:T(8,128)S(1)}, u32[]{:S(2)}, u32[]{:S(2)}) collective-permute-start(f32[2,40,8,128]{3,2,1,0:T(8,128)S(1)} %get-tuple-element.64), channel_id=1, source_target_pairs={{0,8},{4,12},{8,0},{12,4},{1,9},{5,13},{9,1},{13,5},{2,10},{6,14},... | collective-permute-start | bytes 983048 | tf_op jit(solution)/shard_map/ppermute | solution.py:668
  23.5 16.2 %collective-permute-done.14.refs_1_ = f32[31,8,128]{2,1,0:T(8,128)S(1)} collective-permute-done((f32[31,8,128]{2,1,0:T(8,128)S(1)}, f32[31,8,128]{2,1,0:T(8,128)S(1)}, u32[]{:S(2)}, u32[]{:S(2)}) %collective-permute-start.14) | collective-permute-done | bytes 127008 | tf_op jit(solution)/shard_map/ppermute | solution.py:668
  41.0 1.4 %collective-permute-start.10 = (f32[2,20,8,128]{3,2,1,0:T(8,128)S(1)}, f32[2,20,8,128]{3,2,1,0:T(8,128)S(1)}, u32[]{:S(2)}, u32[]{:S(2)}) collective-permute-start(f32[2,20,8,128]{3,2,1,0:T(8,128)S(1)} %get-tuple-element.85), channel_id=1, source_target_pairs={{0,12},{4,8},{8,4},{12,0},{1,13},{5,9},{9,5},{13,1},{2,14},{6,10},... | collective-permute-start | bytes 491528 | tf_op jit(solution)/shard_map/ppermute | solution.py:668
  42.4 3.6 %collective-permute-done.9.refs_6_ = f32[2,20,8,128]{3,2,1,0:T(8,128)S(1)} collective-permute-done((f32[2,20,8,128]{3,2,1,0:T(8,128)S(1)}, f32[2,20,8,128]{3,2,1,0:T(8,128)S(1)}, u32[]{:S(2)}, u32[]{:S(2)}) %collective-permute-start.9) | collective-permute-done | bytes 163872 | tf_op jit(solution)/shard_map/ppermute | solution.py:668
  46.1 2.6 %collective-permute-start.15 = (f32[31,8,128]{2,1,0:T(8,128)S(1)}, f32[31,8,128]{2,1,0:T(8,128)S(1)}, u32[]{:S(2)}, u32[]{:S(2)}) collective-permute-start(f32[31,8,128]{2,1,0:T(8,128)S(1)} %get-tuple-element.94), channel_id=1, source_target_pairs={{0,8},{4,12},{8,0},{12,4},{1,9},{5,13},{9,1},{13,5},{2,10},{6,14},... | collective-permute-start | bytes 380936 | tf_op jit(solution)/shard_map/ppermute | solution.py:668
  50.5 1.7 %collective-permute-start.12 = (f32[31,8,128]{2,1,0:T(8,128)S(1)}, f32[31,8,128]{2,1,0:T(8,128)S(1)}, u32[]{:S(2)}, u32[]{:S(2)}) collective-permute-start(f32[31,8,128]{2,1,0:T(8,128)S(1)} %get-tuple-element.90), channel_id=1, source_target_pairs={{0,8},{4,12},{8,0},{12,4},{1,9},{5,13},{9,1},{13,5},{2,10},{6,14},... | collective-permute-start | bytes 380936 | tf_op jit(solution)/shard_map/ppermute | solution.py:668
  53.5 3.5 %shard_map.70 = (f32[2,80,32,128]{3,2,1,0:T(8,128)S(1)}, f32[80,32,128]{2,1,0:T(8,128)S(1)}) custom-call(s32[1]{0:T(128)} %bitcast.1.place_ref, f32[2,40,8,128]{3,2,1,0:T(8,128)S(1)} %get-tuple-element.62.refs_0_, f32[2,40,8,128]{3,2,1,0:T(8,128)S(1)} %collective-permute-done.refs_1_, f32[2,40,8,128]{3,2,1,0:T(8,128)S(1)} %collective-permute-done.1.refs_2_, ...), custom_call_target="tpu_custom_call" | custom-call | flops 1000000 | tf_op jit(solution)/shard_map/pallas_call | solution.py:650
  57.0 7.1 %shard_map.71 = (f32[40,32,128]{2,1,0:T(8,128)S(1)}, f32[40,32,128]{2,1,0:T(8,128)S(1)}, f32[40,32,128]{2,1,0:T(8,128)S(1)}, f32[40,32,128]{2,1,0:T(8,128)S(1)},...) custom-call(s32[2]{0:T(128)S(1)} %pad_add_fusion.where_ref, ...), custom_call_target="tpu_custom_call" | custom-call | flops 1000000 | tf_op jit(solution)/shard_map/pallas_call | solution.py:650
  64.1 9.1 %shard_map.72 = (f32[48,32,128]{2,1,0:T(8,128)S(1)}, f32[48,32,128]{2,1,0:T(8,128)S(1)}, f32[48,32,128]{2,1,0:T(8,128)S(1)}, f32[48,32,128]{2,1,0:T(8,128)S(1)},...) custom-call(s32[2]{0:T(128)S(1)} %pad_add_fusion.where_ref, ...), custom_call_target="tpu_custom_call" | custom-call | flops 1000000 | tf_op jit(solution)/shard_map/pallas_call | solution.py:650
  73.3 12.4 %all_to_all.5.sums_ref = f32[16,8,128]{2,1,0:T(8,128)S(1)} all-to-all(f32[16,8,128]{2,1,0:T(8,128)S(1)} %get-tuple-element.104), channel_id=1, replica_groups=mesh['group'=2,'gx'=4,'gy'=4] {'gx','gy'}, dimensions={0} | all-to-all | bytes 131072 | tf_op jit(solution)/shard_map/all_to_all | solution.py:743
  85.6 1.5 %shard_map.73.coefs_ref = f32[13,8,128]{2,1,0:T(8,128)S(1)} custom-call(f32[16,8,128]{2,1,0:T(8,128)S(1)} %all_to_all.5.sums_ref), custom_call_target="tpu_custom_call" | custom-call | flops 1000000 | tf_op jit(solution)/shard_map/pallas_call | solution.py:650
  87.1 1.5 %shard_map.75 = (f32[32,8,128]{2,1,0:T(8,128)S(1)}, f32[32,8,128]{2,1,0:T(8,128)S(1)}, f32[32,8,128]{2,1,0:T(8,128)S(1)}, f32[32,8,128]{2,1,0:T(8,128)S(1)}) custom-call(s32[2]{0:T(128)S(1)} %pad_add_fusion.where_ref, f32[13,8,128]{2,1,0:T(8,128)S(1)} %shard_map.73.coefs_ref, f32[40,32,128]{2,1,0:T(8,128)S(1)} %get-tuple-element.96.refs_4_.refs_0_, ...), custom_call_target="tpu_custom_call" | custom-call | flops 1000000 | tf_op jit(solution)/shard_map/pallas_call | solution.py:650
  89.4 1.9 %shard_map.74 = (f32[48,8,128]{2,1,0:T(8,128)S(1)}, f32[48,8,128]{2,1,0:T(8,128)S(1)}, f32[48,8,128]{2,1,0:T(8,128)S(1)}, f32[48,8,128]{2,1,0:T(8,128)S(1)}) custom-call(s32[2]{0:T(128)S(1)} %pad_add_fusion.where_ref, f32[13,8,128]{2,1,0:T(8,128)S(1)} %shard_map.73.coefs_ref, f32[48,32,128]{2,1,0:T(8,128)S(1)} %get-tuple-element.105.refs_0_, ...), custom_call_target="tpu_custom_call" | custom-call | flops 1000000 | tf_op jit(solution)/shard_map/pallas_call | solution.py:650
  93.4 1.5 %collective-permute-start.19 = (f32[48,8,128]{2,1,0:T(8,128)S(1)}, f32[48,8,128]{2,1,0:T(8,128)S(1)}, u32[]{:S(2)}, u32[]{:S(2)}) collective-permute-start(f32[48,8,128]{2,1,0:T(8,128)S(1)} %get-tuple-element.115), channel_id=1, source_target_pairs={{0,12},{4,8},{8,4},{12,0},{1,13},{5,9},{9,5},{13,1},{2,14},{6,10},... | collective-permute-start | bytes 589832 | tf_op jit(solution)/shard_map/ppermute | solution.py:668
  95.5 2.1 %collective-permute-start.22 = (f32[32,8,128]{2,1,0:T(8,128)S(1)}, f32[32,8,128]{2,1,0:T(8,128)S(1)}, u32[]{:S(2)}, u32[]{:S(2)}) collective-permute-start(f32[32,8,128]{2,1,0:T(8,128)S(1)} %get-tuple-element.119), channel_id=1, source_target_pairs={{0,12},{4,8},{8,4},{12,0},{1,13},{5,9},{9,5},{13,1},{2,14},{6,10},... | collective-permute-start | bytes 393224 | tf_op jit(solution)/shard_map/ppermute | solution.py:668
  97.6 7.0 %collective-permute-done.21.refs_2_ = f32[32,8,128]{2,1,0:T(8,128)S(1)} collective-permute-done((f32[32,8,128]{2,1,0:T(8,128)S(1)}, f32[32,8,128]{2,1,0:T(8,128)S(1)}, u32[]{:S(2)}, u32[]{:S(2)}) %collective-permute-start.21) | collective-permute-done | bytes 131104 | tf_op jit(solution)/shard_map/ppermute | solution.py:668
  104.5 1.5 %shard_map.76 = (f32[1,80,8,256]{3,2,1,0:T(8,128)}, f32[1,80,8,256]{3,2,1,0:T(8,128)}) custom-call(s32[2]{0:T(128)S(1)} %pad_add_fusion.where_ref, f32[32,8,128]{2,1,0:T(8,128)S(1)} %get-tuple-element.116.refs_0_, f32[32,8,128]{2,1,0:T(8,128)S(1)} %collective-permute-done.20.refs_1_, f32[32,8,128]{2,1,0:T(8,128)S(1)} %collective-permute-done.21.refs_2_, ...), custom_call_target="tpu_custom_call" | custom-call | flops 1000000 | tf_op jit(solution)/shard_map/pallas_call | solution.py:650
  106.1 1.6 %shard_map.77 = (f32[1,80,8,256]{3,2,1,0:T(8,128)}, f32[1,80,8,256]{3,2,1,0:T(8,128)}) custom-call(s32[2]{0:T(128)S(1)} %pad_add_fusion.where_ref, f32[48,8,128]{2,1,0:T(8,128)S(1)} %get-tuple-element.112.refs_0_, f32[48,8,128]{2,1,0:T(8,128)S(1)} %collective-permute-done.17.refs_1_, ...), custom_call_target="tpu_custom_call", output_to_operand_aliasing={{0}: (5, {}), {1}: (6, {})} | custom-call | flops 1000000 | tf_op jit(solution)/shard_map/pallas_call | solution.py:650
  (38 shorter events, 13.3 us)
Async XLA Ops:
  4.5 5.3 %collective-permute-start.5 = (f32[8,256]{1,0:T(8,128)S(1)}, f32[8,256]{1,0:T(8,128)S(1)}, u32[]{:S(2)}, u32[]{:S(2)}) collective-permute-start(f32[8,256]{1,0:T(8,128)S(1)} %get-tuple-element.69), channel_id=1, source_target_pairs={{0,16},{16,0},{1,17},{17,1},{2,18},{18,2},{3,19},{19,3},{4,20},{20... | collective-permute-start | bytes 24584 | tf_op jit(solution)/shard_map/ppermute | solution.py:58
  5.1 12.2 %collective-permute-start.3 = (f32[3,10,8,128]{3,2,1,0:T(8,128)S(1)}, f32[3,10,8,128]{3,2,1,0:T(8,128)S(1)}, u32[]{:S(2)}, u32[]{:S(2)}) collective-permute-start(f32[3,10,8,128]{3,2,1,0:T(8,128)S(1)} %get-tuple-element.66), channel_id=1, source_target_pairs={{0,1},{1,2},{2,3},{3,0},{4,5},{5,6},{6,7},{7,4},{8,9},{9,10},{10,1... | collective-permute-start | bytes 368648 | tf_op jit(solution)/shard_map/ppermute | solution.py:711
  7.7 9.5 %collective-permute-start.4 = (f32[3,10,8,128]{3,2,1,0:T(8,128)S(1)}, f32[3,10,8,128]{3,2,1,0:T(8,128)S(1)}, u32[]{:S(2)}, u32[]{:S(2)}) collective-permute-start(f32[3,10,8,128]{3,2,1,0:T(8,128)S(1)} %get-tuple-element.67), channel_id=1, source_target_pairs={{0,3},{1,0},{2,1},{3,2},{4,7},{5,4},{6,5},{7,6},{8,11},{9,8},{10,9... | collective-permute-start | bytes 368648 | tf_op jit(solution)/shard_map/ppermute | solution.py:711
  9.8 6.0 %collective-permute-start.7 = (f32[8,128]{1,0:T(8,128)S(1)}, f32[8,128]{1,0:T(8,128)S(1)}, u32[]{:S(2)}, u32[]{:S(2)}) collective-permute-start(f32[8,128]{1,0:T(8,128)S(1)} %get-tuple-element.122), channel_id=1, source_target_pairs={{0,3},{1,0},{2,1},{3,2},{4,7},{5,4},{6,5},{7,6},{8,11},{9,8},{10,9... | collective-permute-start | bytes 12296 | tf_op jit(solution)/shard_map/ppermute | solution.py:714
  11.8 5.4 %collective-permute-start.6 = (f32[8,128]{1,0:T(8,128)S(1)}, f32[8,128]{1,0:T(8,128)S(1)}, u32[]{:S(2)}, u32[]{:S(2)}) collective-permute-start(f32[8,128]{1,0:T(8,128)S(1)} %get-tuple-element.123), channel_id=1, source_target_pairs={{0,1},{1,2},{2,3},{3,0},{4,5},{5,6},{6,7},{7,4},{8,9},{9,10},{10,1... | collective-permute-start | bytes 12296 | tf_op jit(solution)/shard_map/ppermute | solution.py:713
  17.9 23.1 %collective-permute-start.8 = (f32[2,20,8,128]{3,2,1,0:T(8,128)S(1)}, f32[2,20,8,128]{3,2,1,0:T(8,128)S(1)}, u32[]{:S(2)}, u32[]{:S(2)}) collective-permute-start(f32[2,20,8,128]{3,2,1,0:T(8,128)S(1)} %get-tuple-element.83), channel_id=1, source_target_pairs={{0,4},{4,0},{8,12},{12,8},{1,5},{5,1},{9,13},{13,9},{2,6},{6,2},{1... | collective-permute-start | bytes 491528 | tf_op jit(solution)/shard_map/ppermute | solution.py:668
  19.5 30.3 %collective-permute-start = (f32[2,40,8,128]{3,2,1,0:T(8,128)S(1)}, f32[2,40,8,128]{3,2,1,0:T(8,128)S(1)}, u32[]{:S(2)}, u32[]{:S(2)}) collective-permute-start(f32[2,40,8,128]{3,2,1,0:T(8,128)S(1)} %get-tuple-element.63), channel_id=1, source_target_pairs={{0,4},{4,0},{8,12},{12,8},{1,5},{5,1},{9,13},{13,9},{2,6},{6,2},{1... | collective-permute-start | bytes 983048 | tf_op jit(solution)/shard_map/ppermute | solution.py:668
  20.0 30.4 %collective-permute-start.1 = (f32[2,40,8,128]{3,2,1,0:T(8,128)S(1)}, f32[2,40,8,128]{3,2,1,0:T(8,128)S(1)}, u32[]{:S(2)}, u32[]{:S(2)}) collective-permute-start(f32[2,40,8,128]{3,2,1,0:T(8,128)S(1)} %get-tuple-element.64), channel_id=1, source_target_pairs={{0,8},{4,12},{8,0},{12,4},{1,9},{5,13},{9,1},{13,5},{2,10},{6,14},... | collective-permute-start | bytes 983048 | tf_op jit(solution)/shard_map/ppermute | solution.py:668
  21.5 30.7 %collective-permute-start.2 = (f32[2,40,8,128]{3,2,1,0:T(8,128)S(1)}, f32[2,40,8,128]{3,2,1,0:T(8,128)S(1)}, u32[]{:S(2)}, u32[]{:S(2)}) collective-permute-start(f32[2,40,8,128]{3,2,1,0:T(8,128)S(1)} %get-tuple-element.65), channel_id=1, source_target_pairs={{0,12},{4,8},{8,4},{12,0},{1,13},{5,9},{9,5},{13,1},{2,14},{6,10},... | collective-permute-start | bytes 983048 | tf_op jit(solution)/shard_map/ppermute | solution.py:668
  23.0 16.7 %collective-permute-start.14 = (f32[31,8,128]{2,1,0:T(8,128)S(1)}, f32[31,8,128]{2,1,0:T(8,128)S(1)}, u32[]{:S(2)}, u32[]{:S(2)}) collective-permute-start(f32[31,8,128]{2,1,0:T(8,128)S(1)} %get-tuple-element.93), channel_id=1, source_target_pairs={{0,4},{4,0},{8,12},{12,8},{1,5},{5,1},{9,13},{13,9},{2,6},{6,2},{1... | collective-permute-start | bytes 380936 | tf_op jit(solution)/shard_map/ppermute | solution.py:668
  39.7 6.4 %collective-permute-start.9 = (f32[2,20,8,128]{3,2,1,0:T(8,128)S(1)}, f32[2,20,8,128]{3,2,1,0:T(8,128)S(1)}, u32[]{:S(2)}, u32[]{:S(2)}) collective-permute-start(f32[2,20,8,128]{3,2,1,0:T(8,128)S(1)} %get-tuple-element.84), channel_id=1, source_target_pairs={{0,8},{4,12},{8,0},{12,4},{1,9},{5,13},{9,1},{13,5},{2,10},{6,14},... | collective-permute-start | bytes 491528 | tf_op jit(solution)/shard_map/ppermute | solution.py:668
  41.0 7.7 %collective-permute-start.10 = (f32[2,20,8,128]{3,2,1,0:T(8,128)S(1)}, f32[2,20,8,128]{3,2,1,0:T(8,128)S(1)}, u32[]{:S(2)}, u32[]{:S(2)}) collective-permute-start(f32[2,20,8,128]{3,2,1,0:T(8,128)S(1)} %get-tuple-element.85), channel_id=1, source_target_pairs={{0,12},{4,8},{8,4},{12,0},{1,13},{5,9},{9,5},{13,1},{2,14},{6,10},... | collective-permute-start | bytes 491528 | tf_op jit(solution)/shard_map/ppermute | solution.py:668
  46.1 10.9 %collective-permute-start.15 = (f32[31,8,128]{2,1,0:T(8,128)S(1)}, f32[31,8,128]{2,1,0:T(8,128)S(1)}, u32[]{:S(2)}, u32[]{:S(2)}) collective-permute-start(f32[31,8,128]{2,1,0:T(8,128)S(1)} %get-tuple-element.94), channel_id=1, source_target_pairs={{0,8},{4,12},{8,0},{12,4},{1,9},{5,13},{9,1},{13,5},{2,10},{6,14},... | collective-permute-start | bytes 380936 | tf_op jit(solution)/shard_map/ppermute | solution.py:668
  48.7 8.2 %collective-permute-start.16 = (f32[31,8,128]{2,1,0:T(8,128)S(1)}, f32[31,8,128]{2,1,0:T(8,128)S(1)}, u32[]{:S(2)}, u32[]{:S(2)}) collective-permute-start(f32[31,8,128]{2,1,0:T(8,128)S(1)} %get-tuple-element.95), channel_id=1, source_target_pairs={{0,12},{4,8},{8,4},{12,0},{1,13},{5,9},{9,5},{13,1},{2,14},{6,10},... | collective-permute-start | bytes 380936 | tf_op jit(solution)/shard_map/ppermute | solution.py:668
  49.8 14.3 %collective-permute-start.11 = (f32[31,8,128]{2,1,0:T(8,128)S(1)}, f32[31,8,128]{2,1,0:T(8,128)S(1)}, u32[]{:S(2)}, u32[]{:S(2)}) collective-permute-start(f32[31,8,128]{2,1,0:T(8,128)S(1)} %get-tuple-element.89), channel_id=1, source_target_pairs={{0,4},{4,0},{8,12},{12,8},{1,5},{5,1},{9,13},{13,9},{2,6},{6,2},{1... | collective-permute-start | bytes 380936 | tf_op jit(solution)/shard_map/ppermute | solution.py:668
  50.5 13.6 %collective-permute-start.12 = (f32[31,8,128]{2,1,0:T(8,128)S(1)}, f32[31,8,128]{2,1,0:T(8,128)S(1)}, u32[]{:S(2)}, u32[]{:S(2)}) collective-permute-start(f32[31,8,128]{2,1,0:T(8,128)S(1)} %get-tuple-element.90), channel_id=1, source_target_pairs={{0,8},{4,12},{8,0},{12,4},{1,9},{5,13},{9,1},{13,5},{2,10},{6,14},... | collective-permute-start | bytes 380936 | tf_op jit(solution)/shard_map/ppermute | solution.py:668
  52.2 11.9 %collective-permute-start.13 = (f32[31,8,128]{2,1,0:T(8,128)S(1)}, f32[31,8,128]{2,1,0:T(8,128)S(1)}, u32[]{:S(2)}, u32[]{:S(2)}) collective-permute-start(f32[31,8,128]{2,1,0:T(8,128)S(1)} %get-tuple-element.91), channel_id=1, source_target_pairs={{0,12},{4,8},{8,4},{12,0},{1,13},{5,9},{9,5},{13,1},{2,14},{6,10},... | collective-permute-start | bytes 380936 | tf_op jit(solution)/shard_map/ppermute | solution.py:668
  88.6 6.9 %collective-permute-start.20 = (f32[32,8,128]{2,1,0:T(8,128)S(1)}, f32[32,8,128]{2,1,0:T(8,128)S(1)}, u32[]{:S(2)}, u32[]{:S(2)}) collective-permute-start(f32[32,8,128]{2,1,0:T(8,128)S(1)} %get-tuple-element.117), channel_id=1, source_target_pairs={{0,4},{4,0},{8,12},{12,8},{1,5},{5,1},{9,13},{13,9},{2,6},{6,2},{1... | collective-permute-start | bytes 393224 | tf_op jit(solution)/shard_map/ppermute | solution.py:668
  91.3 14.8 %collective-permute-start.17 = (f32[48,8,128]{2,1,0:T(8,128)S(1)}, f32[48,8,128]{2,1,0:T(8,128)S(1)}, u32[]{:S(2)}, u32[]{:S(2)}) collective-permute-start(f32[48,8,128]{2,1,0:T(8,128)S(1)} %get-tuple-element.113), channel_id=1, source_target_pairs={{0,4},{4,0},{8,12},{12,8},{1,5},{5,1},{9,13},{13,9},{2,6},{6,2},{1... | collective-permute-start | bytes 589832 | tf_op jit(solution)/shard_map/ppermute | solution.py:668
  92.6 13.4 %collective-permute-start.18 = (f32[48,8,128]{2,1,0:T(8,128)S(1)}, f32[48,8,128]{2,1,0:T(8,128)S(1)}, u32[]{:S(2)}, u32[]{:S(2)}) collective-permute-start(f32[48,8,128]{2,1,0:T(8,128)S(1)} %get-tuple-element.114), channel_id=1, source_target_pairs={{0,8},{4,12},{8,0},{12,4},{1,9},{5,13},{9,1},{13,5},{2,10},{6,14},... | collective-permute-start | bytes 589832 | tf_op jit(solution)/shard_map/ppermute | solution.py:668
  93.4 12.7 %collective-permute-start.19 = (f32[48,8,128]{2,1,0:T(8,128)S(1)}, f32[48,8,128]{2,1,0:T(8,128)S(1)}, u32[]{:S(2)}, u32[]{:S(2)}) collective-permute-start(f32[48,8,128]{2,1,0:T(8,128)S(1)} %get-tuple-element.115), channel_id=1, source_target_pairs={{0,12},{4,8},{8,4},{12,0},{1,13},{5,9},{9,5},{13,1},{2,14},{6,10},... | collective-permute-start | bytes 589832 | tf_op jit(solution)/shard_map/ppermute | solution.py:668
  94.8 9.7 %collective-permute-start.21 = (f32[32,8,128]{2,1,0:T(8,128)S(1)}, f32[32,8,128]{2,1,0:T(8,128)S(1)}, u32[]{:S(2)}, u32[]{:S(2)}) collective-permute-start(f32[32,8,128]{2,1,0:T(8,128)S(1)} %get-tuple-element.118), channel_id=1, source_target_pairs={{0,8},{4,12},{8,0},{12,4},{1,9},{5,13},{9,1},{13,5},{2,10},{6,14},... | collective-permute-start | bytes 393224 | tf_op jit(solution)/shard_map/ppermute | solution.py:668
  95.5 9.1 %collective-permute-start.22 = (f32[32,8,128]{2,1,0:T(8,128)S(1)}, f32[32,8,128]{2,1,0:T(8,128)S(1)}, u32[]{:S(2)}, u32[]{:S(2)}) collective-permute-start(f32[32,8,128]{2,1,0:T(8,128)S(1)} %get-tuple-element.119), channel_id=1, source_target_pairs={{0,12},{4,8},{8,4},{12,0},{1,13},{5,9},{9,5},{13,1},{2,14},{6,10},... | collective-permute-start | bytes 393224 | tf_op jit(solution)/shard_map/ppermute | solution.py:668

commit v7 on v6

--- a/solution.py
+++ b/solution.py
@@ -371,23 +371,53 @@
     return total, low + other_low + error
 
 
-def stencil(held_ref, layer, rows):
+def stencil_first(held_ref, layer, rows):
     def at(shift):
         return held_ref[layer + 1, pl.ds(SUBLANES + shift, rows)]
 
     here = at(0)
     near = at(1) + at(-1)
-    mixed = here + cross_weight * near
-    far = at(2) + at(-2) + turned(here, 2) + turned(here, -2)
-    beside = near + turned(mixed, 1) + turned(mixed, -1) + far_weight * far
+    wide = turned(here + cross_weight * near, 1) + far_weight * (here + turned(here, 2))
+    far = (at(2) - here) + (at(-2) - here)
     above = held_ref[layer + 2, pl.ds(SUBLANES, rows)] + held_ref[layer, pl.ds(SUBLANES, rows)]
-    return beside + vertical_weight * above
+    return near + far_weight * far + vertical_weight * above + wide, wide
+
+
+def spread_over(held_ref, flat_ref, wide_ref, start, stop, origin, use):
+    rows = flat_ref.shape[1]
+
+    def first_half(first, number):
+        for u in range(number):
+            flat, wide = stencil_first(held_ref, first + u - origin, rows)
+            flat_ref[first + u - origin] = flat
+            wide_ref[first + u - origin] = wide
+
+    def second_half(first, number):
+        for u in range(number):
+            spread = flat_ref[first + u - origin] + turned(wide_ref[first + u - origin], -2)
+            use(first + u, spread)
+
+    size = min(UNROLL, stop - start)
+
+    def step(b, carry):
+        second_half(start + (b - 1) * size, size)
+        first_half(start + b * size, size)
+        return carry
+
+    whole, rest = divmod(stop - start, size)
+    end = start + whole * size
+    first_half(start, size)
+    lax.fori_loop(1, whole, step, 0)
+    second_half(end - size, size)
+    if rest:
+        first_half(end, rest)
+        second_half(end, rest)
 
 
 def scale_kernel(place_ref, *refs):
-    count = (len(refs) - 4) // 2
+    count = (len(refs) - 6) // 2
     own_refs, rim_refs = refs[:count], refs[count : 2 * count]
-    scale_ref, factor_ref, held_ref, base_ref = refs[2 * count :]
+    scale_ref, factor_ref, held_ref, base_ref, *scratch = refs[2 * count :]
     layers, rows = base_ref.shape[:2]
     clear_edges(held_ref, rows)
     places = partner_rows(place_ref[0], count)
@@ -408,18 +438,15 @@
 
     blocks(layers // 4, 2, gather)
 
-    def begin(first):
-        for layer in range(UNROLL):
-            layer = first + layer
-            coupling = held_ref[layer + 1, pl.ds(SUBLANES, rows)]
-            diagonal = base_ref[layer] + coupling * stencil(held_ref, layer, rows)
-            root = jnp.sqrt(diagonal)
-            inverse = 1.0 / root
-            scale_ref[0, layer] = inverse
-            scale_ref[1, layer] = root
-            factor_ref[layer] = coupling * inverse
-
-    blocks(layers, UNROLL, begin)
+    def use(layer, spread):
+        coupling = held_ref[layer + 1, pl.ds(SUBLANES, rows)]
+        root = jnp.sqrt(base_ref[layer] + coupling * spread)
+        inverse = 1.0 / root
+        scale_ref[0, layer] = inverse
+        scale_ref[1, layer] = root
+        factor_ref[layer] = coupling * inverse
+
+    spread_over(held_ref, *scratch, 0, layers, 0, use)
 
 
 def clear_edges(ref, rows):
@@ -453,23 +480,20 @@
     spans(0, groups, 4, begin)
 
 
-def apply_part(k, factor_ref, basis, held, start, stop, origin):
+def apply_part(k, factor_ref, basis, held, scratch, start, stop, origin):
     rows = factor_ref.shape[1]
     source_ref, target_ref = held[k % 2], held[(k + 1) % 2]
 
-    def apply(first, number):
-        for layer in range(number):
-            layer = first + layer
-            factor = factor_ref[layer]
-            spread = stencil(source_ref, layer - origin, rows)
-            before = basis[k][layer - origin]
-            before = (1.0 - SHIFTS[k]) * before if SHIFTS[k] else before
-            vector = before - factor * spread
-            basis[k + 1][layer - origin] = vector
-            if k + 1 < ITERS:
-                target_ref[layer - origin + 1, pl.ds(SUBLANES, rows)] = factor * vector
-
-    spans(start, stop, UNROLL, apply)
+    def use(layer, spread):
+        factor = factor_ref[layer]
+        before = basis[k][layer - origin]
+        before = (1.0 - SHIFTS[k]) * before if SHIFTS[k] else before
+        vector = before - factor * spread
+        basis[k + 1][layer - origin] = vector
+        if k + 1 < ITERS:
+            target_ref[layer - origin + 1, pl.ds(SUBLANES, rows)] = factor * vector
+
+    spread_over(source_ref, *scratch, start, stop, origin, use)
 
 
 def products_part(basis, gram_ref, layers):
@@ -498,25 +522,27 @@
 
 
 def lower_kernel(where_ref, scale_ref, factor_ref, *refs):
-    count = len(refs) - ITERS - 1 - 3
+    count = len(refs) - ITERS - 1 - 5
     basis = refs[count : count + ITERS + 1]
-    gram_ref, *held = refs[count + ITERS + 1 :]
+    gram_ref, *held, flat_ref, wide_ref = refs[count + ITERS + 1 :]
+    scratch = flat_ref, wide_ref
     half, rows = basis[0].shape[:2]
     for ref in held:
         clear_edges(ref, rows)
     begin_part(where_ref, scale_ref, factor_ref, refs[:count], basis[0], held[0], 0, 0)
     for k in range(ITERS):
-        apply_part(k, factor_ref, basis, held, 0, half - 1 - k, 0)
+        apply_part(k, factor_ref, basis, held, scratch, 0, half - 1 - k, 0)
     gram_ref[...] = jnp.zeros(gram_ref.shape, jnp.float32)
     products_part(basis, gram_ref, half - 8)
 
 
 def upper_kernel(where_ref, scale_ref, factor_ref, *refs):
-    count = len(refs) - 2 * (ITERS + 1) - 5
+    count = len(refs) - 2 * (ITERS + 1) - 7
     below = refs[count : count + ITERS + 1]
     part_ref = refs[count + ITERS + 1]
     basis = refs[count + ITERS + 2 : count + 2 * ITERS + 3]
-    sums_ref, gram_ref, *held = refs[count + 2 * ITERS + 3 :]
+    sums_ref, gram_ref, *held, flat_ref, wide_ref = refs[count + 2 * ITERS + 3 :]
+    scratch = flat_ref, wide_ref
     half, rows = below[0].shape[:2]
     layers = factor_ref.shape[0]
     origin = half - 8
@@ -530,7 +556,7 @@
     for k in range(ITERS):
         for layer in (half - k - 2, half - k - 1):
             held[k % 2][layer - origin + 1, pl.ds(SUBLANES, rows)] = factor_ref[layer] * below[k][layer]
-        apply_part(k, factor_ref, basis, held, half - 1 - k, layers, origin)
+        apply_part(k, factor_ref, basis, held, scratch, half - 1 - k, layers, origin)
     gram_ref[...] = part_ref[...]
     products_part(basis, gram_ref, layers - origin)
     high, low = gram_ref[0, :, 0], gram_ref[1, :, 0]
@@ -725,20 +751,20 @@
     window = (layers, rows, LANES)
     scale, factor = call(
         scale_kernel, [(2,) + window, window], (place_x[None], *owns, *rims), smem=1,
-        scratch=[padded, window],
+        scratch=[padded] + [window] * 3,
     )
     half = layers // 2
     depths = (half - 8, layers - half + 8)
     gram = (2, 32, SUBLANES, LANES)
     *below, part = call(
         lower_kernel, [(half, rows, LANES)] * (ITERS + 1) + [gram],
-        (where, scale, factor, *forces[0]), smem=1, scratch=[(half + 2,) + padded[1:]] * 2, limit=32,
+        (where, scale, factor, *forces[0]), smem=1, scratch=[(half + 2,) + padded[1:]] * 2 + [(half, rows, LANES)] * 2, limit=32,
     )
     *beyond, sums = call(
         upper_kernel,
         [(depths[1], rows, LANES)] * (ITERS + 1) + [(count_x * count_y, SUBLANES, LANES)],
         (where, scale, factor, *forces[1], *below, part), smem=1,
-        scratch=[gram] + [(depths[1] + 2,) + padded[1:]] * 2, limit=32,
+        scratch=[gram] + [(depths[1] + 2,) + padded[1:]] * 2 + [(depths[1], rows, LANES)] * 2, limit=32,
     )
     sums = lax.all_to_all(sums, ("gx", "gy"), 0, 0, tiled=True)
     (coefs,) = call(solve_kernel, [(2 * ITERS + 1, SUBLANES, LANES)], (sums,), scratch=[(SUBLANES, LANES)])

time: 108 us -> 105 us (0.972)
  Pallas kernels: 32.2 us -> 29.2 us
    pallas_call x10, Pallas kernels: 32.2 us -> 29.2 us  [call(): pl.pallas_call(kernel, out_shape=[jax.ShapeDtypeStruct(shape, jnp.float32...]
  transfers between devices with their start and end apart: 23 -> 23, of which waited for: 5 -> 5; matrix products, arithmetic and copies ran while one was open for 0% -> 0% of each run, Pallas kernels for 13% -> 12%
where the time goes in v7:
time: 105 us
  waiting for transfers between devices  31.9 us (30%)
  starting transfers between devices  30 us (29%)
  Pallas kernels  29.2 us (28%)
  blocking collectives  12.6 us (12%)
    pallas_call x10, Pallas kernels, call(): pl.pallas_call(kernel, out_shape=[jax.ShapeDtypeStruct(shape, jnp.float32...  29.2 us
    ppermute x18, waiting for transfers between devices, exchanged(): lax.ppermute(parts[k], 'gx', [(i, i ^ k) for i in range(count)])  26.6 us
    ppermute x18, starting transfers between devices, exchanged(): lax.ppermute(parts[k], 'gx', [(i, i ^ k) for i in range(count)])  22.7 us
    all_to_all x1, blocking collectives, in_windows(): sums = lax.all_to_all(sums, ('gx', 'gy'), 0, 0, tiled=True)  12.6 us
    ppermute x1, waiting for transfers between devices, in_windows(): term_after = lax.ppermute(term[:, :LANES], 'gy', down)  3.85 us
    ppermute x1, starting transfers between devices, in_windows(): lax.ppermute(high, 'gy', up)  2.63 us
  transfers between devices with their start and end apart: 23, of which 5 were waited for; matrix products, arithmetic and copies ran while one was open for 0% of the time, Pallas kernels for 12%

profile of v7, /device:TPU:0, one launch (start us, length us, event | category | flops | bytes accessed | tf_op | source)
XLA Modules:
  0.0 104.7 jit_solution(62003501790774490)
XLA Ops:
  0.7 3.8 %shard_map.68 = (f32[2,40,8,128]{3,2,1,0:T(8,128)S(1)}, f32[2,40,8,128]{3,2,1,0:T(8,128)S(1)}, f32[2,40,8,128]{3,2,1,0:T(8,128)S(1)}, f32[2,40,8,128]{3,2,1,0:T(...) custom-call(s32[3]{0:T(128)S(1)} %pad_add_fusion.1.where_ref, ...), custom_call_target="tpu_custom_call" | custom-call | flops 1000000 | tf_op jit(solution)/shard_map/pallas_call | solution.py:676
  5.1 2.6 %collective-permute-start.3 = (f32[3,10,8,128]{3,2,1,0:T(8,128)S(1)}, f32[3,10,8,128]{3,2,1,0:T(8,128)S(1)}, u32[]{:S(2)}, u32[]{:S(2)}) collective-permute-start(f32[3,10,8,128]{3,2,1,0:T(8,128)S(1)} %get-tuple-element.66), channel_id=1, source_target_pairs={{0,1},{1,2},{2,3},{3,0},{4,5},{5,6},{6,7},{7,4},{8,9},{9,10},{10,1... | collective-permute-start | bytes 368648 | tf_op jit(solution)/shard_map/ppermute | solution.py:737
  7.7 2.1 %collective-permute-start.4 = (f32[3,10,8,128]{3,2,1,0:T(8,128)S(1)}, f32[3,10,8,128]{3,2,1,0:T(8,128)S(1)}, u32[]{:S(2)}, u32[]{:S(2)}) collective-permute-start(f32[3,10,8,128]{3,2,1,0:T(8,128)S(1)} %get-tuple-element.67), channel_id=1, source_target_pairs={{0,3},{1,0},{2,1},{3,2},{4,7},{5,4},{6,5},{7,6},{8,11},{9,8},{10,9... | collective-permute-start | bytes 368648 | tf_op jit(solution)/shard_map/ppermute | solution.py:737
  9.8 2.0 %collective-permute-start.7 = (f32[8,128]{1,0:T(8,128)S(1)}, f32[8,128]{1,0:T(8,128)S(1)}, u32[]{:S(2)}, u32[]{:S(2)}) collective-permute-start(f32[8,128]{1,0:T(8,128)S(1)} %get-tuple-element.122), channel_id=1, source_target_pairs={{0,3},{1,0},{2,1},{3,2},{4,7},{5,4},{6,5},{7,6},{8,11},{9,8},{10,9... | collective-permute-start | bytes 12296 | tf_op jit(solution)/shard_map/ppermute | solution.py:740
  11.9 3.9 %collective-permute-done.7.after_ref = f32[8,128]{1,0:T(8,128)S(1)} collective-permute-done((f32[8,128]{1,0:T(8,128)S(1)}, f32[8,128]{1,0:T(8,128)S(1)}, u32[]{:S(2)}, u32[]{:S(2)}) %collective-permute-start.7) | collective-permute-done | bytes 4128 | tf_op jit(solution)/shard_map/ppermute | solution.py:740
  17.9 1.6 %collective-permute-start.8 = (f32[2,20,8,128]{3,2,1,0:T(8,128)S(1)}, f32[2,20,8,128]{3,2,1,0:T(8,128)S(1)}, u32[]{:S(2)}, u32[]{:S(2)}) collective-permute-start(f32[2,20,8,128]{3,2,1,0:T(8,128)S(1)} %get-tuple-element.83), channel_id=1, source_target_pairs={{0,4},{4,0},{8,12},{12,8},{1,5},{5,1},{9,13},{13,9},{2,6},{6,2},{1... | collective-permute-start | bytes 491528 | tf_op jit(solution)/shard_map/ppermute | solution.py:694
  20.0 1.5 %collective-permute-start.1 = (f32[2,40,8,128]{3,2,1,0:T(8,128)S(1)}, f32[2,40,8,128]{3,2,1,0:T(8,128)S(1)}, u32[]{:S(2)}, u32[]{:S(2)}) collective-permute-start(f32[2,40,8,128]{3,2,1,0:T(8,128)S(1)} %get-tuple-element.64), channel_id=1, source_target_pairs={{0,8},{4,12},{8,0},{12,4},{1,9},{5,13},{9,1},{13,5},{2,10},{6,14},... | collective-permute-start | bytes 983048 | tf_op jit(solution)/shard_map/ppermute | solution.py:694
  23.5 16.2 %collective-permute-done.14.refs_1_ = f32[31,8,128]{2,1,0:T(8,128)S(1)} collective-permute-done((f32[31,8,128]{2,1,0:T(8,128)S(1)}, f32[31,8,128]{2,1,0:T(8,128)S(1)}, u32[]{:S(2)}, u32[]{:S(2)}) %collective-permute-start.14) | collective-permute-done | bytes 127008 | tf_op jit(solution)/shard_map/ppermute | solution.py:694
  41.0 1.4 %collective-permute-start.10 = (f32[2,20,8,128]{3,2,1,0:T(8,128)S(1)}, f32[2,20,8,128]{3,2,1,0:T(8,128)S(1)}, u32[]{:S(2)}, u32[]{:S(2)}) collective-permute-start(f32[2,20,8,128]{3,2,1,0:T(8,128)S(1)} %get-tuple-element.85), channel_id=1, source_target_pairs={{0,12},{4,8},{8,4},{12,0},{1,13},{5,9},{9,5},{13,1},{2,14},{6,10},... | collective-permute-start | bytes 491528 | tf_op jit(solution)/shard_map/ppermute | solution.py:694
  42.4 3.6 %collective-permute-done.9.refs_6_ = f32[2,20,8,128]{3,2,1,0:T(8,128)S(1)} collective-permute-done((f32[2,20,8,128]{3,2,1,0:T(8,128)S(1)}, f32[2,20,8,128]{3,2,1,0:T(8,128)S(1)}, u32[]{:S(2)}, u32[]{:S(2)}) %collective-permute-start.9) | collective-permute-done | bytes 163872 | tf_op jit(solution)/shard_map/ppermute | solution.py:694
  46.1 2.6 %collective-permute-start.15 = (f32[31,8,128]{2,1,0:T(8,128)S(1)}, f32[31,8,128]{2,1,0:T(8,128)S(1)}, u32[]{:S(2)}, u32[]{:S(2)}) collective-permute-start(f32[31,8,128]{2,1,0:T(8,128)S(1)} %get-tuple-element.94), channel_id=1, source_target_pairs={{0,8},{4,12},{8,0},{12,4},{1,9},{5,13},{9,1},{13,5},{2,10},{6,14},... | collective-permute-start | bytes 380936 | tf_op jit(solution)/shard_map/ppermute | solution.py:694
  50.5 1.7 %collective-permute-start.12 = (f32[31,8,128]{2,1,0:T(8,128)S(1)}, f32[31,8,128]{2,1,0:T(8,128)S(1)}, u32[]{:S(2)}, u32[]{:S(2)}) collective-permute-start(f32[31,8,128]{2,1,0:T(8,128)S(1)} %get-tuple-element.90), channel_id=1, source_target_pairs={{0,8},{4,12},{8,0},{12,4},{1,9},{5,13},{9,1},{13,5},{2,10},{6,14},... | collective-permute-start | bytes 380936 | tf_op jit(solution)/shard_map/ppermute | solution.py:694
  53.5 3.3 %shard_map.70 = (f32[2,80,32,128]{3,2,1,0:T(8,128)S(1)}, f32[80,32,128]{2,1,0:T(8,128)S(1)}) custom-call(s32[1]{0:T(128)} %bitcast.1.place_ref, f32[2,40,8,128]{3,2,1,0:T(8,128)S(1)} %get-tuple-element.62.refs_0_, f32[2,40,8,128]{3,2,1,0:T(8,128)S(1)} %collective-permute-done.refs_1_, f32[2,40,8,128]{3,2,1,0:T(8,128)S(1)} %collective-permute-done.1.refs_2_, ...), custom_call_target="tpu_custom_call" | custom-call | flops 1000000 | tf_op jit(solution)/shard_map/pallas_call | solution.py:676
  56.7 5.8 %shard_map.71 = (f32[40,32,128]{2,1,0:T(8,128)S(1)}, f32[40,32,128]{2,1,0:T(8,128)S(1)}, f32[40,32,128]{2,1,0:T(8,128)S(1)}, f32[40,32,128]{2,1,0:T(8,128)S(1)},...) custom-call(s32[2]{0:T(128)S(1)} %pad_add_fusion.where_ref, ...), custom_call_target="tpu_custom_call" | custom-call | flops 1000000 | tf_op jit(solution)/shard_map/pallas_call | solution.py:676
  62.6 7.7 %shard_map.72 = (f32[48,32,128]{2,1,0:T(8,128)S(1)}, f32[48,32,128]{2,1,0:T(8,128)S(1)}, f32[48,32,128]{2,1,0:T(8,128)S(1)}, f32[48,32,128]{2,1,0:T(8,128)S(1)},...) custom-call(s32[2]{0:T(128)S(1)} %pad_add_fusion.where_ref, ...), custom_call_target="tpu_custom_call" | custom-call | flops 1000000 | tf_op jit(solution)/shard_map/pallas_call | solution.py:676
  70.3 12.6 %all_to_all.5.sums_ref = f32[16,8,128]{2,1,0:T(8,128)S(1)} all-to-all(f32[16,8,128]{2,1,0:T(8,128)S(1)} %get-tuple-element.104), channel_id=1, replica_groups=mesh['group'=2,'gx'=4,'gy'=4] {'gx','gy'}, dimensions={0} | all-to-all | bytes 131072 | tf_op jit(solution)/shard_map/all_to_all | solution.py:769
  82.8 1.5 %shard_map.73.coefs_ref = f32[13,8,128]{2,1,0:T(8,128)S(1)} custom-call(f32[16,8,128]{2,1,0:T(8,128)S(1)} %all_to_all.5.sums_ref), custom_call_target="tpu_custom_call" | custom-call | flops 1000000 | tf_op jit(solution)/shard_map/pallas_call | solution.py:676
  84.4 1.5 %shard_map.75 = (f32[32,8,128]{2,1,0:T(8,128)S(1)}, f32[32,8,128]{2,1,0:T(8,128)S(1)}, f32[32,8,128]{2,1,0:T(8,128)S(1)}, f32[32,8,128]{2,1,0:T(8,128)S(1)}) custom-call(s32[2]{0:T(128)S(1)} %pad_add_fusion.where_ref, f32[13,8,128]{2,1,0:T(8,128)S(1)} %shard_map.73.coefs_ref, f32[40,32,128]{2,1,0:T(8,128)S(1)} %get-tuple-element.96.refs_4_.refs_0_, ...), custom_call_target="tpu_custom_call" | custom-call | flops 1000000 | tf_op jit(solution)/shard_map/pallas_call | solution.py:676
  86.6 1.9 %shard_map.74 = (f32[48,8,128]{2,1,0:T(8,128)S(1)}, f32[48,8,128]{2,1,0:T(8,128)S(1)}, f32[48,8,128]{2,1,0:T(8,128)S(1)}, f32[48,8,128]{2,1,0:T(8,128)S(1)}) custom-call(s32[2]{0:T(128)S(1)} %pad_add_fusion.where_ref, f32[13,8,128]{2,1,0:T(8,128)S(1)} %shard_map.73.coefs_ref, f32[48,32,128]{2,1,0:T(8,128)S(1)} %get-tuple-element.105.refs_0_, ...), custom_call_target="tpu_custom_call" | custom-call | flops 1000000 | tf_op jit(solution)/shard_map/pallas_call | solution.py:676
  90.6 1.5 %collective-permute-start.19 = (f32[48,8,128]{2,1,0:T(8,128)S(1)}, f32[48,8,128]{2,1,0:T(8,128)S(1)}, u32[]{:S(2)}, u32[]{:S(2)}) collective-permute-start(f32[48,8,128]{2,1,0:T(8,128)S(1)} %get-tuple-element.115), channel_id=1, source_target_pairs={{0,12},{4,8},{8,4},{12,0},{1,13},{5,9},{9,5},{13,1},{2,14},{6,10},... | collective-permute-start | bytes 589832 | tf_op jit(solution)/shard_map/ppermute | solution.py:694
  92.7 2.1 %collective-permute-start.22 = (f32[32,8,128]{2,1,0:T(8,128)S(1)}, f32[32,8,128]{2,1,0:T(8,128)S(1)}, u32[]{:S(2)}, u32[]{:S(2)}) collective-permute-start(f32[32,8,128]{2,1,0:T(8,128)S(1)} %get-tuple-element.119), channel_id=1, source_target_pairs={{0,12},{4,8},{8,4},{12,0},{1,13},{5,9},{9,5},{13,1},{2,14},{6,10},... | collective-permute-start | bytes 393224 | tf_op jit(solution)/shard_map/ppermute | solution.py:694
  94.8 6.7 %collective-permute-done.21.refs_2_ = f32[32,8,128]{2,1,0:T(8,128)S(1)} collective-permute-done((f32[32,8,128]{2,1,0:T(8,128)S(1)}, f32[32,8,128]{2,1,0:T(8,128)S(1)}, u32[]{:S(2)}, u32[]{:S(2)}) %collective-permute-start.21) | collective-permute-done | bytes 131104 | tf_op jit(solution)/shard_map/ppermute | solution.py:694
  101.6 1.5 %shard_map.76 = (f32[1,80,8,256]{3,2,1,0:T(8,128)}, f32[1,80,8,256]{3,2,1,0:T(8,128)}) custom-call(s32[2]{0:T(128)S(1)} %pad_add_fusion.where_ref, f32[32,8,128]{2,1,0:T(8,128)S(1)} %get-tuple-element.116.refs_0_, f32[32,8,128]{2,1,0:T(8,128)S(1)} %collective-permute-done.20.refs_1_, f32[32,8,128]{2,1,0:T(8,128)S(1)} %collective-permute-done.21.refs_2_, ...), custom_call_target="tpu_custom_call" | custom-call | flops 1000000 | tf_op jit(solution)/shard_map/pallas_call | solution.py:676
  103.1 1.6 %shard_map.77 = (f32[1,80,8,256]{3,2,1,0:T(8,128)}, f32[1,80,8,256]{3,2,1,0:T(8,128)}) custom-call(s32[2]{0:T(128)S(1)} %pad_add_fusion.where_ref, f32[48,8,128]{2,1,0:T(8,128)S(1)} %get-tuple-element.112.refs_0_, f32[48,8,128]{2,1,0:T(8,128)S(1)} %collective-permute-done.17.refs_1_, ...), custom_call_target="tpu_custom_call", output_to_operand_aliasing={{0}: (5, {}), {1}: (6, {})} | custom-call | flops 1000000 | tf_op jit(solution)/shard_map/pallas_call | solution.py:676
  (38 shorter events, 13.3 us)
Async XLA Ops:
  4.5 5.3 %collective-permute-start.5 = (f32[8,256]{1,0:T(8,128)S(1)}, f32[8,256]{1,0:T(8,128)S(1)}, u32[]{:S(2)}, u32[]{:S(2)}) collective-permute-start(f32[8,256]{1,0:T(8,128)S(1)} %get-tuple-element.69), channel_id=1, source_target_pairs={{0,16},{16,0},{1,17},{17,1},{2,18},{18,2},{3,19},{19,3},{4,20},{20... | collective-permute-start | bytes 24584 | tf_op jit(solution)/shard_map/ppermute | solution.py:58
  5.1 12.2 %collective-permute-start.3 = (f32[3,10,8,128]{3,2,1,0:T(8,128)S(1)}, f32[3,10,8,128]{3,2,1,0:T(8,128)S(1)}, u32[]{:S(2)}, u32[]{:S(2)}) collective-permute-start(f32[3,10,8,128]{3,2,1,0:T(8,128)S(1)} %get-tuple-element.66), channel_id=1, source_target_pairs={{0,1},{1,2},{2,3},{3,0},{4,5},{5,6},{6,7},{7,4},{8,9},{9,10},{10,1... | collective-permute-start | bytes 368648 | tf_op jit(solution)/shard_map/ppermute | solution.py:737
  7.7 9.5 %collective-permute-start.4 = (f32[3,10,8,128]{3,2,1,0:T(8,128)S(1)}, f32[3,10,8,128]{3,2,1,0:T(8,128)S(1)}, u32[]{:S(2)}, u32[]{:S(2)}) collective-permute-start(f32[3,10,8,128]{3,2,1,0:T(8,128)S(1)} %get-tuple-element.67), channel_id=1, source_target_pairs={{0,3},{1,0},{2,1},{3,2},{4,7},{5,4},{6,5},{7,6},{8,11},{9,8},{10,9... | collective-permute-start | bytes 368648 | tf_op jit(solution)/shard_map/ppermute | solution.py:737
  9.8 6.0 %collective-permute-start.7 = (f32[8,128]{1,0:T(8,128)S(1)}, f32[8,128]{1,0:T(8,128)S(1)}, u32[]{:S(2)}, u32[]{:S(2)}) collective-permute-start(f32[8,128]{1,0:T(8,128)S(1)} %get-tuple-element.122), channel_id=1, source_target_pairs={{0,3},{1,0},{2,1},{3,2},{4,7},{5,4},{6,5},{7,6},{8,11},{9,8},{10,9... | collective-permute-start | bytes 12296 | tf_op jit(solution)/shard_map/ppermute | solution.py:740
  11.8 5.4 %collective-permute-start.6 = (f32[8,128]{1,0:T(8,128)S(1)}, f32[8,128]{1,0:T(8,128)S(1)}, u32[]{:S(2)}, u32[]{:S(2)}) collective-permute-start(f32[8,128]{1,0:T(8,128)S(1)} %get-tuple-element.123), channel_id=1, source_target_pairs={{0,1},{1,2},{2,3},{3,0},{4,5},{5,6},{6,7},{7,4},{8,9},{9,10},{10,1... | collective-permute-start | bytes 12296 | tf_op jit(solution)/shard_map/ppermute | solution.py:739
  17.9 23.1 %collective-permute-start.8 = (f32[2,20,8,128]{3,2,1,0:T(8,128)S(1)}, f32[2,20,8,128]{3,2,1,0:T(8,128)S(1)}, u32[]{:S(2)}, u32[]{:S(2)}) collective-permute-start(f32[2,20,8,128]{3,2,1,0:T(8,128)S(1)} %get-tuple-element.83), channel_id=1, source_target_pairs={{0,4},{4,0},{8,12},{12,8},{1,5},{5,1},{9,13},{13,9},{2,6},{6,2},{1... | collective-permute-start | bytes 491528 | tf_op jit(solution)/shard_map/ppermute | solution.py:694
  19.5 30.3 %collective-permute-start = (f32[2,40,8,128]{3,2,1,0:T(8,128)S(1)}, f32[2,40,8,128]{3,2,1,0:T(8,128)S(1)}, u32[]{:S(2)}, u32[]{:S(2)}) collective-permute-start(f32[2,40,8,128]{3,2,1,0:T(8,128)S(1)} %get-tuple-element.63), channel_id=1, source_target_pairs={{0,4},{4,0},{8,12},{12,8},{1,5},{5,1},{9,13},{13,9},{2,6},{6,2},{1... | collective-permute-start | bytes 983048 | tf_op jit(solution)/shard_map/ppermute | solution.py:694
  20.0 30.4 %collective-permute-start.1 = (f32[2,40,8,128]{3,2,1,0:T(8,128)S(1)}, f32[2,40,8,128]{3,2,1,0:T(8,128)S(1)}, u32[]{:S(2)}, u32[]{:S(2)}) collective-permute-start(f32[2,40,8,128]{3,2,1,0:T(8,128)S(1)} %get-tuple-element.64), channel_id=1, source_target_pairs={{0,8},{4,12},{8,0},{12,4},{1,9},{5,13},{9,1},{13,5},{2,10},{6,14},... | collective-permute-start | bytes 983048 | tf_op jit(solution)/shard_map/ppermute | solution.py:694
  21.5 30.7 %collective-permute-start.2 = (f32[2,40,8,128]{3,2,1,0:T(8,128)S(1)}, f32[2,40,8,128]{3,2,1,0:T(8,128)S(1)}, u32[]{:S(2)}, u32[]{:S(2)}) collective-permute-start(f32[2,40,8,128]{3,2,1,0:T(8,128)S(1)} %get-tuple-element.65), channel_id=1, source_target_pairs={{0,12},{4,8},{8,4},{12,0},{1,13},{5,9},{9,5},{13,1},{2,14},{6,10},... | collective-permute-start | bytes 983048 | tf_op jit(solution)/shard_map/ppermute | solution.py:694
  23.0 16.7 %collective-permute-start.14 = (f32[31,8,128]{2,1,0:T(8,128)S(1)}, f32[31,8,128]{2,1,0:T(8,128)S(1)}, u32[]{:S(2)}, u32[]{:S(2)}) collective-permute-start(f32[31,8,128]{2,1,0:T(8,128)S(1)} %get-tuple-element.93), channel_id=1, source_target_pairs={{0,4},{4,0},{8,12},{12,8},{1,5},{5,1},{9,13},{13,9},{2,6},{6,2},{1... | collective-permute-start | bytes 380936 | tf_op jit(solution)/shard_map/ppermute | solution.py:694
  39.7 6.4 %collective-permute-start.9 = (f32[2,20,8,128]{3,2,1,0:T(8,128)S(1)}, f32[2,20,8,128]{3,2,1,0:T(8,128)S(1)}, u32[]{:S(2)}, u32[]{:S(2)}) collective-permute-start(f32[2,20,8,128]{3,2,1,0:T(8,128)S(1)} %get-tuple-element.84), channel_id=1, source_target_pairs={{0,8},{4,12},{8,0},{12,4},{1,9},{5,13},{9,1},{13,5},{2,10},{6,14},... | collective-permute-start | bytes 491528 | tf_op jit(solution)/shard_map/ppermute | solution.py:694
  41.0 7.7 %collective-permute-start.10 = (f32[2,20,8,128]{3,2,1,0:T(8,128)S(1)}, f32[2,20,8,128]{3,2,1,0:T(8,128)S(1)}, u32[]{:S(2)}, u32[]{:S(2)}) collective-permute-start(f32[2,20,8,128]{3,2,1,0:T(8,128)S(1)} %get-tuple-element.85), channel_id=1, source_target_pairs={{0,12},{4,8},{8,4},{12,0},{1,13},{5,9},{9,5},{13,1},{2,14},{6,10},... | collective-permute-start | bytes 491528 | tf_op jit(solution)/shard_map/ppermute | solution.py:694
  46.1 10.6 %collective-permute-start.15 = (f32[31,8,128]{2,1,0:T(8,128)S(1)}, f32[31,8,128]{2,1,0:T(8,128)S(1)}, u32[]{:S(2)}, u32[]{:S(2)}) collective-permute-start(f32[31,8,128]{2,1,0:T(8,128)S(1)} %get-tuple-element.94), channel_id=1, source_target_pairs={{0,8},{4,12},{8,0},{12,4},{1,9},{5,13},{9,1},{13,5},{2,10},{6,14},... | collective-permute-start | bytes 380936 | tf_op jit(solution)/shard_map/ppermute | solution.py:694
  48.7 8.0 %collective-permute-start.16 = (f32[31,8,128]{2,1,0:T(8,128)S(1)}, f32[31,8,128]{2,1,0:T(8,128)S(1)}, u32[]{:S(2)}, u32[]{:S(2)}) collective-permute-start(f32[31,8,128]{2,1,0:T(8,128)S(1)} %get-tuple-element.95), channel_id=1, source_target_pairs={{0,12},{4,8},{8,4},{12,0},{1,13},{5,9},{9,5},{13,1},{2,14},{6,10},... | collective-permute-start | bytes 380936 | tf_op jit(solution)/shard_map/ppermute | solution.py:694
  49.8 12.7 %collective-permute-start.11 = (f32[31,8,128]{2,1,0:T(8,128)S(1)}, f32[31,8,128]{2,1,0:T(8,128)S(1)}, u32[]{:S(2)}, u32[]{:S(2)}) collective-permute-start(f32[31,8,128]{2,1,0:T(8,128)S(1)} %get-tuple-element.89), channel_id=1, source_target_pairs={{0,4},{4,0},{8,12},{12,8},{1,5},{5,1},{9,13},{13,9},{2,6},{6,2},{1... | collective-permute-start | bytes 380936 | tf_op jit(solution)/shard_map/ppermute | solution.py:694
  50.5 12.1 %collective-permute-start.12 = (f32[31,8,128]{2,1,0:T(8,128)S(1)}, f32[31,8,128]{2,1,0:T(8,128)S(1)}, u32[]{:S(2)}, u32[]{:S(2)}) collective-permute-start(f32[31,8,128]{2,1,0:T(8,128)S(1)} %get-tuple-element.90), channel_id=1, source_target_pairs={{0,8},{4,12},{8,0},{12,4},{1,9},{5,13},{9,1},{13,5},{2,10},{6,14},... | collective-permute-start | bytes 380936 | tf_op jit(solution)/shard_map/ppermute | solution.py:694
  52.2 10.4 %collective-permute-start.13 = (f32[31,8,128]{2,1,0:T(8,128)S(1)}, f32[31,8,128]{2,1,0:T(8,128)S(1)}, u32[]{:S(2)}, u32[]{:S(2)}) collective-permute-start(f32[31,8,128]{2,1,0:T(8,128)S(1)} %get-tuple-element.91), channel_id=1, source_target_pairs={{0,12},{4,8},{8,4},{12,0},{1,13},{5,9},{9,5},{13,1},{2,14},{6,10},... | collective-permute-start | bytes 380936 | tf_op jit(solution)/shard_map/ppermute | solution.py:694
  85.8 6.9 %collective-permute-start.20 = (f32[32,8,128]{2,1,0:T(8,128)S(1)}, f32[32,8,128]{2,1,0:T(8,128)S(1)}, u32[]{:S(2)}, u32[]{:S(2)}) collective-permute-start(f32[32,8,128]{2,1,0:T(8,128)S(1)} %get-tuple-element.117), channel_id=1, source_target_pairs={{0,4},{4,0},{8,12},{12,8},{1,5},{5,1},{9,13},{13,9},{2,6},{6,2},{1... | collective-permute-start | bytes 393224 | tf_op jit(solution)/shard_map/ppermute | solution.py:694
  88.5 14.6 %collective-permute-start.17 = (f32[48,8,128]{2,1,0:T(8,128)S(1)}, f32[48,8,128]{2,1,0:T(8,128)S(1)}, u32[]{:S(2)}, u32[]{:S(2)}) collective-permute-start(f32[48,8,128]{2,1,0:T(8,128)S(1)} %get-tuple-element.113), channel_id=1, source_target_pairs={{0,4},{4,0},{8,12},{12,8},{1,5},{5,1},{9,13},{13,9},{2,6},{6,2},{1... | collective-permute-start | bytes 589832 | tf_op jit(solution)/shard_map/ppermute | solution.py:694
  89.8 13.2 %collective-permute-start.18 = (f32[48,8,128]{2,1,0:T(8,128)S(1)}, f32[48,8,128]{2,1,0:T(8,128)S(1)}, u32[]{:S(2)}, u32[]{:S(2)}) collective-permute-start(f32[48,8,128]{2,1,0:T(8,128)S(1)} %get-tuple-element.114), channel_id=1, source_target_pairs={{0,8},{4,12},{8,0},{12,4},{1,9},{5,13},{9,1},{13,5},{2,10},{6,14},... | collective-permute-start | bytes 589832 | tf_op jit(solution)/shard_map/ppermute | solution.py:694
  90.6 12.5 %collective-permute-start.19 = (f32[48,8,128]{2,1,0:T(8,128)S(1)}, f32[48,8,128]{2,1,0:T(8,128)S(1)}, u32[]{:S(2)}, u32[]{:S(2)}) collective-permute-start(f32[48,8,128]{2,1,0:T(8,128)S(1)} %get-tuple-element.115), channel_id=1, source_target_pairs={{0,12},{4,8},{8,4},{12,0},{1,13},{5,9},{9,5},{13,1},{2,14},{6,10},... | collective-permute-start | bytes 589832 | tf_op jit(solution)/shard_map/ppermute | solution.py:694
  92.1 9.5 %collective-permute-start.21 = (f32[32,8,128]{2,1,0:T(8,128)S(1)}, f32[32,8,128]{2,1,0:T(8,128)S(1)}, u32[]{:S(2)}, u32[]{:S(2)}) collective-permute-start(f32[32,8,128]{2,1,0:T(8,128)S(1)} %get-tuple-element.118), channel_id=1, source_target_pairs={{0,8},{4,12},{8,0},{12,4},{1,9},{5,13},{9,1},{13,5},{2,10},{6,14},... | collective-permute-start | bytes 393224 | tf_op jit(solution)/shard_map/ppermute | solution.py:694
  92.7 8.8 %collective-permute-start.22 = (f32[32,8,128]{2,1,0:T(8,128)S(1)}, f32[32,8,128]{2,1,0:T(8,128)S(1)}, u32[]{:S(2)}, u32[]{:S(2)}) collective-permute-start(f32[32,8,128]{2,1,0:T(8,128)S(1)} %get-tuple-element.119), channel_id=1, source_target_pairs={{0,12},{4,8},{8,4},{12,0},{1,13},{5,9},{9,5},{13,1},{2,14},{6,10},... | collective-permute-start | bytes 393224 | tf_op jit(solution)/shard_map/ppermute | solution.py:694

commit v8 on v7

--- a/solution.py
+++ b/solution.py
@@ -562,10 +562,11 @@
     high, low = gram_ref[0, :, 0], gram_ref[1, :, 0]
     for row in range(1, SUBLANES):
         high, low = add_pairs(high, low, gram_ref[0, :, row], gram_ref[1, :, row])
-    turn = LANES // 2
-    while turn:
-        high, low = add_pairs(high, low, pltpu.roll(high, turn, 1), pltpu.roll(low, turn, 1))
-        turn //= 2
+    for turn, ways in ((32, 4), (8, 4), (2, 4), (1, 2)):
+        pairs = [(high, low)] + [(turned(high, turn * n), turned(low, turn * n)) for n in range(1, ways)]
+        while len(pairs) > 1:
+            pairs = [add_pairs(*pairs[i], *pairs[i + 1]) for i in range(0, len(pairs), 2)]
+        high, low = pairs[0]
     packed = high[:SUBLANES]
     share = LANES // 4
     for g in range(4):
@@ -624,6 +625,12 @@
     answer, residual = iterate(gram)
     for n, coef in enumerate(answer + residual):
         coefs_ref[n] = jnp.broadcast_to(coef, (SUBLANES, LANES))
+
+
+def first_kernel(start, depth, where_ref, sums_ref, *refs):
+    *rest, coefs_ref, gram_ref = refs
+    solve_kernel(sums_ref, coefs_ref, gram_ref)
+    combine_kernel(start, depth, where_ref, coefs_ref, *rest)
 
 
 def combine_kernel(start, depth, where_ref, coefs_ref, *refs):
@@ -767,14 +774,21 @@
         scratch=[gram] + [(depths[1] + 2,) + padded[1:]] * 2 + [(depths[1], rows, LANES)] * 2, limit=32,
     )
     sums = lax.all_to_all(sums, ("gx", "gy"), 0, 0, tiled=True)
-    (coefs,) = call(solve_kernel, [(2 * ITERS + 1, SUBLANES, LANES)], (sums,), scratch=[(SUBLANES, LANES)])
     starts = (0, depths[0])
     arrived = []
-    for start, depth, basis in zip(starts, depths, (below, beyond)):
-        mixed = call(
-            functools.partial(combine_kernel, start, depth),
-            [(depth, block_x, LANES)] * count_x, (where, coefs, *basis, scale), smem=1,
-        )
+    for n, (start, depth, basis) in enumerate(zip(starts, depths, (below, beyond))):
+        outs = [(depth, block_x, LANES)] * count_x
+        if n == 0:
+            *mixed, coefs = call(
+                functools.partial(first_kernel, start, depth),
+                outs + [(2 * ITERS + 1, SUBLANES, LANES)], (where, sums, *basis, scale), smem=1,
+                scratch=[(SUBLANES, LANES)],
+            )
+        else:
+            mixed = call(
+                functools.partial(combine_kernel, start, depth),
+                outs, (where, coefs, *basis, scale), smem=1,
+            )
         arrived.append(exchanged(mixed))
     outs = ()
     for n, (start, depth) in enumerate(zip(starts, depths)):

time: 105 us -> 105 us (level)
    pallas_call x10 -> x9, Pallas kernels: 29.2 us -> 29 us  [call(): pl.pallas_call(kernel, out_shape=[jax.ShapeDtypeStruct(shape, jnp.float32...]
where the time goes in v8:
time: 105 us; the launch traced here: 104 us
  waiting for transfers between devices  31.9 us (30%)
  starting transfers between devices  30 us (29%)
  Pallas kernels  29 us (28%)
  blocking collectives  12.6 us (12%)
    pallas_call x9, Pallas kernels, call(): pl.pallas_call(kernel, out_shape=[jax.ShapeDtypeStruct(shape, jnp.float32...  29 us
    ppermute x18, waiting for transfers between devices, exchanged(): lax.ppermute(parts[k], 'gx', [(i, i ^ k) for i in range(count)])  26.6 us
    ppermute x18, starting transfers between devices, exchanged(): lax.ppermute(parts[k], 'gx', [(i, i ^ k) for i in range(count)])  22.7 us
    all_to_all x1, blocking collectives, in_windows(): sums = lax.all_to_all(sums, ('gx', 'gy'), 0, 0, tiled=True)  12.6 us
    ppermute x1, waiting for transfers between devices, in_windows(): term_after = lax.ppermute(term[:, :LANES], 'gy', down)  3.85 us
    ppermute x1, starting transfers between devices, in_windows(): lax.ppermute(high, 'gy', up)  2.63 us
  transfers between devices with their start and end apart: 23, of which 5 were waited for; matrix products, arithmetic and copies ran while one was open for 0% of the time, Pallas kernels for 12%

profile of v8, /device:TPU:0, one launch (start us, length us, event | category | flops | bytes accessed | tf_op | source)
XLA Modules:
  0.0 104.5 jit_solution(10966047472224335296)
XLA Ops:
  0.7 3.8 %shard_map.68 = (f32[2,40,8,128]{3,2,1,0:T(8,128)S(1)}, f32[2,40,8,128]{3,2,1,0:T(8,128)S(1)}, f32[2,40,8,128]{3,2,1,0:T(8,128)S(1)}, f32[2,40,8,128]{3,2,1,0:T(...) custom-call(s32[3]{0:T(128)S(1)} %pad_add_fusion.1.where_ref, ...), custom_call_target="tpu_custom_call" | custom-call | flops 1000000 | tf_op jit(solution)/shard_map/pallas_call | solution.py:683
  5.1 2.6 %collective-permute-start.3 = (f32[3,10,8,128]{3,2,1,0:T(8,128)S(1)}, f32[3,10,8,128]{3,2,1,0:T(8,128)S(1)}, u32[]{:S(2)}, u32[]{:S(2)}) collective-permute-start(f32[3,10,8,128]{3,2,1,0:T(8,128)S(1)} %get-tuple-element.67), channel_id=1, source_target_pairs={{0,1},{1,2},{2,3},{3,0},{4,5},{5,6},{6,7},{7,4},{8,9},{9,10},{10,1... | collective-permute-start | bytes 368648 | tf_op jit(solution)/shard_map/ppermute | solution.py:744
  7.7 2.1 %collective-permute-start.4 = (f32[3,10,8,128]{3,2,1,0:T(8,128)S(1)}, f32[3,10,8,128]{3,2,1,0:T(8,128)S(1)}, u32[]{:S(2)}, u32[]{:S(2)}) collective-permute-start(f32[3,10,8,128]{3,2,1,0:T(8,128)S(1)} %get-tuple-element.68), channel_id=1, source_target_pairs={{0,3},{1,0},{2,1},{3,2},{4,7},{5,4},{6,5},{7,6},{8,11},{9,8},{10,9... | collective-permute-start | bytes 368648 | tf_op jit(solution)/shard_map/ppermute | solution.py:744
  9.8 2.0 %collective-permute-start.7 = (f32[8,128]{1,0:T(8,128)S(1)}, f32[8,128]{1,0:T(8,128)S(1)}, u32[]{:S(2)}, u32[]{:S(2)}) collective-permute-start(f32[8,128]{1,0:T(8,128)S(1)} %get-tuple-element.124), channel_id=1, source_target_pairs={{0,3},{1,0},{2,1},{3,2},{4,7},{5,4},{6,5},{7,6},{8,11},{9,8},{10,9... | collective-permute-start | bytes 12296 | tf_op jit(solution)/shard_map/ppermute | solution.py:747
  11.9 3.9 %collective-permute-done.7.after_ref = f32[8,128]{1,0:T(8,128)S(1)} collective-permute-done((f32[8,128]{1,0:T(8,128)S(1)}, f32[8,128]{1,0:T(8,128)S(1)}, u32[]{:S(2)}, u32[]{:S(2)}) %collective-permute-start.7) | collective-permute-done | bytes 4128 | tf_op jit(solution)/shard_map/ppermute | solution.py:747
  17.9 1.6 %collective-permute-start.8 = (f32[2,20,8,128]{3,2,1,0:T(8,128)S(1)}, f32[2,20,8,128]{3,2,1,0:T(8,128)S(1)}, u32[]{:S(2)}, u32[]{:S(2)}) collective-permute-start(f32[2,20,8,128]{3,2,1,0:T(8,128)S(1)} %get-tuple-element.84), channel_id=1, source_target_pairs={{0,4},{4,0},{8,12},{12,8},{1,5},{5,1},{9,13},{13,9},{2,6},{6,2},{1... | collective-permute-start | bytes 491528 | tf_op jit(solution)/shard_map/ppermute | solution.py:701
  20.0 1.5 %collective-permute-start.1 = (f32[2,40,8,128]{3,2,1,0:T(8,128)S(1)}, f32[2,40,8,128]{3,2,1,0:T(8,128)S(1)}, u32[]{:S(2)}, u32[]{:S(2)}) collective-permute-start(f32[2,40,8,128]{3,2,1,0:T(8,128)S(1)} %get-tuple-element.65), channel_id=1, source_target_pairs={{0,8},{4,12},{8,0},{12,4},{1,9},{5,13},{9,1},{13,5},{2,10},{6,14},... | collective-permute-start | bytes 983048 | tf_op jit(solution)/shard_map/ppermute | solution.py:701
  21.5 1.4 %collective-permute-start.2 = (f32[2,40,8,128]{3,2,1,0:T(8,128)S(1)}, f32[2,40,8,128]{3,2,1,0:T(8,128)S(1)}, u32[]{:S(2)}, u32[]{:S(2)}) collective-permute-start(f32[2,40,8,128]{3,2,1,0:T(8,128)S(1)} %get-tuple-element.66), channel_id=1, source_target_pairs={{0,12},{4,8},{8,4},{12,0},{1,13},{5,9},{9,5},{13,1},{2,14},{6,10},... | collective-permute-start | bytes 983048 | tf_op jit(solution)/shard_map/ppermute | solution.py:701
  23.5 16.2 %collective-permute-done.14.refs_1_ = f32[31,8,128]{2,1,0:T(8,128)S(1)} collective-permute-done((f32[31,8,128]{2,1,0:T(8,128)S(1)}, f32[31,8,128]{2,1,0:T(8,128)S(1)}, u32[]{:S(2)}, u32[]{:S(2)}) %collective-permute-start.14) | collective-permute-done | bytes 127008 | tf_op jit(solution)/shard_map/ppermute | solution.py:701
  41.0 1.4 %collective-permute-start.10 = (f32[2,20,8,128]{3,2,1,0:T(8,128)S(1)}, f32[2,20,8,128]{3,2,1,0:T(8,128)S(1)}, u32[]{:S(2)}, u32[]{:S(2)}) collective-permute-start(f32[2,20,8,128]{3,2,1,0:T(8,128)S(1)} %get-tuple-element.86), channel_id=1, source_target_pairs={{0,12},{4,8},{8,4},{12,0},{1,13},{5,9},{9,5},{13,1},{2,14},{6,10},... | collective-permute-start | bytes 491528 | tf_op jit(solution)/shard_map/ppermute | solution.py:701
  42.4 3.6 %collective-permute-done.9.refs_6_ = f32[2,20,8,128]{3,2,1,0:T(8,128)S(1)} collective-permute-done((f32[2,20,8,128]{3,2,1,0:T(8,128)S(1)}, f32[2,20,8,128]{3,2,1,0:T(8,128)S(1)}, u32[]{:S(2)}, u32[]{:S(2)}) %collective-permute-start.9) | collective-permute-done | bytes 163872 | tf_op jit(solution)/shard_map/ppermute | solution.py:701
  46.1 2.6 %collective-permute-start.15 = (f32[31,8,128]{2,1,0:T(8,128)S(1)}, f32[31,8,128]{2,1,0:T(8,128)S(1)}, u32[]{:S(2)}, u32[]{:S(2)}) collective-permute-start(f32[31,8,128]{2,1,0:T(8,128)S(1)} %get-tuple-element.95), channel_id=1, source_target_pairs={{0,8},{4,12},{8,0},{12,4},{1,9},{5,13},{9,1},{13,5},{2,10},{6,14},... | collective-permute-start | bytes 380936 | tf_op jit(solution)/shard_map/ppermute | solution.py:701
  50.5 1.7 %collective-permute-start.12 = (f32[31,8,128]{2,1,0:T(8,128)S(1)}, f32[31,8,128]{2,1,0:T(8,128)S(1)}, u32[]{:S(2)}, u32[]{:S(2)}) collective-permute-start(f32[31,8,128]{2,1,0:T(8,128)S(1)} %get-tuple-element.91), channel_id=1, source_target_pairs={{0,8},{4,12},{8,0},{12,4},{1,9},{5,13},{9,1},{13,5},{2,10},{6,14},... | collective-permute-start | bytes 380936 | tf_op jit(solution)/shard_map/ppermute | solution.py:701
  53.5 3.3 %shard_map.70 = (f32[2,80,32,128]{3,2,1,0:T(8,128)S(1)}, f32[80,32,128]{2,1,0:T(8,128)S(1)}) custom-call(s32[1]{0:T(128)} %bitcast.1.place_ref, f32[2,40,8,128]{3,2,1,0:T(8,128)S(1)} %get-tuple-element.63.refs_0_, f32[2,40,8,128]{3,2,1,0:T(8,128)S(1)} %collective-permute-done.refs_1_, f32[2,40,8,128]{3,2,1,0:T(8,128)S(1)} %collective-permute-done.1.refs_2_, ...), custom_call_target="tpu_custom_call" | custom-call | flops 1000000 | tf_op jit(solution)/shard_map/pallas_call | solution.py:683
  56.7 5.8 %shard_map.71 = (f32[40,32,128]{2,1,0:T(8,128)S(1)}, f32[40,32,128]{2,1,0:T(8,128)S(1)}, f32[40,32,128]{2,1,0:T(8,128)S(1)}, f32[40,32,128]{2,1,0:T(8,128)S(1)},...) custom-call(s32[2]{0:T(128)S(1)} %pad_add_fusion.where_ref, ...), custom_call_target="tpu_custom_call" | custom-call | flops 1000000 | tf_op jit(solution)/shard_map/pallas_call | solution.py:683
  62.6 7.5 %shard_map.72 = (f32[48,32,128]{2,1,0:T(8,128)S(1)}, f32[48,32,128]{2,1,0:T(8,128)S(1)}, f32[48,32,128]{2,1,0:T(8,128)S(1)}, f32[48,32,128]{2,1,0:T(8,128)S(1)},...) custom-call(s32[2]{0:T(128)S(1)} %pad_add_fusion.where_ref, ...), custom_call_target="tpu_custom_call" | custom-call | flops 1000000 | tf_op jit(solution)/shard_map/pallas_call | solution.py:683
  70.1 12.6 %all_to_all.5.sums_ref = f32[16,8,128]{2,1,0:T(8,128)S(1)} all-to-all(f32[16,8,128]{2,1,0:T(8,128)S(1)} %get-tuple-element.105), channel_id=1, replica_groups=mesh['group'=2,'gx'=4,'gy'=4] {'gx','gy'}, dimensions={0} | all-to-all | bytes 131072 | tf_op jit(solution)/shard_map/all_to_all | solution.py:776
  82.6 2.9 %shard_map.73 = (f32[32,8,128]{2,1,0:T(8,128)S(1)}, f32[32,8,128]{2,1,0:T(8,128)S(1)}, f32[32,8,128]{2,1,0:T(8,128)S(1)}, f32[32,8,128]{2,1,0:T(8,128)S(1)}, f32[13,8,128]{2,1,0:T(8,128)S(1)}) custom-call(s32[2]{0:T(128)S(1)} %pad_add_fusion.where_ref, f32[16,8,128]{2,1,0:T(8,128)S(1)} %all_to_all.5.sums_ref, ...), custom_call_target="tpu_custom_call" | custom-call | flops 1000000 | tf_op jit(solution)/shard_map/pallas_call | solution.py:683
  86.4 1.9 %shard_map.74 = (f32[48,8,128]{2,1,0:T(8,128)S(1)}, f32[48,8,128]{2,1,0:T(8,128)S(1)}, f32[48,8,128]{2,1,0:T(8,128)S(1)}, f32[48,8,128]{2,1,0:T(8,128)S(1)}) custom-call(s32[2]{0:T(128)S(1)} %pad_add_fusion.where_ref, f32[13,8,128]{2,1,0:T(8,128)S(1)} %get-tuple-element.106.coefs_ref, f32[48,32,128]{2,1,0:T(8,128)S(1)} %get-tuple-element.107.refs_0_, ...), custom_call_target="tpu_custom_call" | custom-call | flops 1000000 | tf_op jit(solution)/shard_map/pallas_call | solution.py:683
  90.4 1.5 %collective-permute-start.19 = (f32[48,8,128]{2,1,0:T(8,128)S(1)}, f32[48,8,128]{2,1,0:T(8,128)S(1)}, u32[]{:S(2)}, u32[]{:S(2)}) collective-permute-start(f32[48,8,128]{2,1,0:T(8,128)S(1)} %get-tuple-element.117), channel_id=1, source_target_pairs={{0,12},{4,8},{8,4},{12,0},{1,13},{5,9},{9,5},{13,1},{2,14},{6,10},... | collective-permute-start | bytes 589832 | tf_op jit(solution)/shard_map/ppermute | solution.py:701
  92.5 2.1 %collective-permute-start.22 = (f32[32,8,128]{2,1,0:T(8,128)S(1)}, f32[32,8,128]{2,1,0:T(8,128)S(1)}, u32[]{:S(2)}, u32[]{:S(2)}) collective-permute-start(f32[32,8,128]{2,1,0:T(8,128)S(1)} %get-tuple-element.121), channel_id=1, source_target_pairs={{0,12},{4,8},{8,4},{12,0},{1,13},{5,9},{9,5},{13,1},{2,14},{6,10},... | collective-permute-start | bytes 393224 | tf_op jit(solution)/shard_map/ppermute | solution.py:701
  94.6 6.7 %collective-permute-done.21.refs_2_ = f32[32,8,128]{2,1,0:T(8,128)S(1)} collective-permute-done((f32[32,8,128]{2,1,0:T(8,128)S(1)}, f32[32,8,128]{2,1,0:T(8,128)S(1)}, u32[]{:S(2)}, u32[]{:S(2)}) %collective-permute-start.21) | collective-permute-done | bytes 131104 | tf_op jit(solution)/shard_map/ppermute | solution.py:701
  101.3 1.5 %shard_map.75 = (f32[1,80,8,256]{3,2,1,0:T(8,128)}, f32[1,80,8,256]{3,2,1,0:T(8,128)}) custom-call(s32[2]{0:T(128)S(1)} %pad_add_fusion.where_ref, f32[32,8,128]{2,1,0:T(8,128)S(1)} %get-tuple-element.118.refs_0_, f32[32,8,128]{2,1,0:T(8,128)S(1)} %collective-permute-done.20.refs_1_, f32[32,8,128]{2,1,0:T(8,128)S(1)} %collective-permute-done.21.refs_2_, ...), custom_call_target="tpu_custom_call" | custom-call | flops 1000000 | tf_op jit(solution)/shard_map/pallas_call | solution.py:683
  102.9 1.6 %shard_map.76 = (f32[1,80,8,256]{3,2,1,0:T(8,128)}, f32[1,80,8,256]{3,2,1,0:T(8,128)}) custom-call(s32[2]{0:T(128)S(1)} %pad_add_fusion.where_ref, f32[48,8,128]{2,1,0:T(8,128)S(1)} %get-tuple-element.114.refs_0_, f32[48,8,128]{2,1,0:T(8,128)S(1)} %collective-permute-done.17.refs_1_, ...), custom_call_target="tpu_custom_call", output_to_operand_aliasing={{0}: (5, {}), {1}: (6, {})} | custom-call | flops 1000000 | tf_op jit(solution)/shard_map/pallas_call | solution.py:683
  (37 shorter events, 11.8 us)
Async XLA Ops:
  4.5 5.3 %collective-permute-start.5 = (f32[8,256]{1,0:T(8,128)S(1)}, f32[8,256]{1,0:T(8,128)S(1)}, u32[]{:S(2)}, u32[]{:S(2)}) collective-permute-start(f32[8,256]{1,0:T(8,128)S(1)} %get-tuple-element.70), channel_id=1, source_target_pairs={{0,16},{16,0},{1,17},{17,1},{2,18},{18,2},{3,19},{19,3},{4,20},{20... | collective-permute-start | bytes 24584 | tf_op jit(solution)/shard_map/ppermute | solution.py:58
  5.1 12.2 %collective-permute-start.3 = (f32[3,10,8,128]{3,2,1,0:T(8,128)S(1)}, f32[3,10,8,128]{3,2,1,0:T(8,128)S(1)}, u32[]{:S(2)}, u32[]{:S(2)}) collective-permute-start(f32[3,10,8,128]{3,2,1,0:T(8,128)S(1)} %get-tuple-element.67), channel_id=1, source_target_pairs={{0,1},{1,2},{2,3},{3,0},{4,5},{5,6},{6,7},{7,4},{8,9},{9,10},{10,1... | collective-permute-start | bytes 368648 | tf_op jit(solution)/shard_map/ppermute | solution.py:744
  7.7 9.5 %collective-permute-start.4 = (f32[3,10,8,128]{3,2,1,0:T(8,128)S(1)}, f32[3,10,8,128]{3,2,1,0:T(8,128)S(1)}, u32[]{:S(2)}, u32[]{:S(2)}) collective-permute-start(f32[3,10,8,128]{3,2,1,0:T(8,128)S(1)} %get-tuple-element.68), channel_id=1, source_target_pairs={{0,3},{1,0},{2,1},{3,2},{4,7},{5,4},{6,5},{7,6},{8,11},{9,8},{10,9... | collective-permute-start | bytes 368648 | tf_op jit(solution)/shard_map/ppermute | solution.py:744
  9.8 6.0 %collective-permute-start.7 = (f32[8,128]{1,0:T(8,128)S(1)}, f32[8,128]{1,0:T(8,128)S(1)}, u32[]{:S(2)}, u32[]{:S(2)}) collective-permute-start(f32[8,128]{1,0:T(8,128)S(1)} %get-tuple-element.124), channel_id=1, source_target_pairs={{0,3},{1,0},{2,1},{3,2},{4,7},{5,4},{6,5},{7,6},{8,11},{9,8},{10,9... | collective-permute-start | bytes 12296 | tf_op jit(solution)/shard_map/ppermute | solution.py:747
  11.8 5.4 %collective-permute-start.6 = (f32[8,128]{1,0:T(8,128)S(1)}, f32[8,128]{1,0:T(8,128)S(1)}, u32[]{:S(2)}, u32[]{:S(2)}) collective-permute-start(f32[8,128]{1,0:T(8,128)S(1)} %get-tuple-element.125), channel_id=1, source_target_pairs={{0,1},{1,2},{2,3},{3,0},{4,5},{5,6},{6,7},{7,4},{8,9},{9,10},{10,1... | collective-permute-start | bytes 12296 | tf_op jit(solution)/shard_map/ppermute | solution.py:746
  17.9 23.1 %collective-permute-start.8 = (f32[2,20,8,128]{3,2,1,0:T(8,128)S(1)}, f32[2,20,8,128]{3,2,1,0:T(8,128)S(1)}, u32[]{:S(2)}, u32[]{:S(2)}) collective-permute-start(f32[2,20,8,128]{3,2,1,0:T(8,128)S(1)} %get-tuple-element.84), channel_id=1, source_target_pairs={{0,4},{4,0},{8,12},{12,8},{1,5},{5,1},{9,13},{13,9},{2,6},{6,2},{1... | collective-permute-start | bytes 491528 | tf_op jit(solution)/shard_map/ppermute | solution.py:701
  19.5 30.3 %collective-permute-start = (f32[2,40,8,128]{3,2,1,0:T(8,128)S(1)}, f32[2,40,8,128]{3,2,1,0:T(8,128)S(1)}, u32[]{:S(2)}, u32[]{:S(2)}) collective-permute-start(f32[2,40,8,128]{3,2,1,0:T(8,128)S(1)} %get-tuple-element.64), channel_id=1, source_target_pairs={{0,4},{4,0},{8,12},{12,8},{1,5},{5,1},{9,13},{13,9},{2,6},{6,2},{1... | collective-permute-start | bytes 983048 | tf_op jit(solution)/shard_map/ppermute | solution.py:701
  20.0 30.4 %collective-permute-start.1 = (f32[2,40,8,128]{3,2,1,0:T(8,128)S(1)}, f32[2,40,8,128]{3,2,1,0:T(8,128)S(1)}, u32[]{:S(2)}, u32[]{:S(2)}) collective-permute-start(f32[2,40,8,128]{3,2,1,0:T(8,128)S(1)} %get-tuple-element.65), channel_id=1, source_target_pairs={{0,8},{4,12},{8,0},{12,4},{1,9},{5,13},{9,1},{13,5},{2,10},{6,14},... | collective-permute-start | bytes 983048 | tf_op jit(solution)/shard_map/ppermute | solution.py:701
  21.5 30.7 %collective-permute-start.2 = (f32[2,40,8,128]{3,2,1,0:T(8,128)S(1)}, f32[2,40,8,128]{3,2,1,0:T(8,128)S(1)}, u32[]{:S(2)}, u32[]{:S(2)}) collective-permute-start(f32[2,40,8,128]{3,2,1,0:T(8,128)S(1)} %get-tuple-element.66), channel_id=1, source_target_pairs={{0,12},{4,8},{8,4},{12,0},{1,13},{5,9},{9,5},{13,1},{2,14},{6,10},... | collective-permute-start | bytes 983048 | tf_op jit(solution)/shard_map/ppermute | solution.py:701
  23.0 16.7 %collective-permute-start.14 = (f32[31,8,128]{2,1,0:T(8,128)S(1)}, f32[31,8,128]{2,1,0:T(8,128)S(1)}, u32[]{:S(2)}, u32[]{:S(2)}) collective-permute-start(f32[31,8,128]{2,1,0:T(8,128)S(1)} %get-tuple-element.94), channel_id=1, source_target_pairs={{0,4},{4,0},{8,12},{12,8},{1,5},{5,1},{9,13},{13,9},{2,6},{6,2},{1... | collective-permute-start | bytes 380936 | tf_op jit(solution)/shard_map/ppermute | solution.py:701
  39.7 6.4 %collective-permute-start.9 = (f32[2,20,8,128]{3,2,1,0:T(8,128)S(1)}, f32[2,20,8,128]{3,2,1,0:T(8,128)S(1)}, u32[]{:S(2)}, u32[]{:S(2)}) collective-permute-start(f32[2,20,8,128]{3,2,1,0:T(8,128)S(1)} %get-tuple-element.85), channel_id=1, source_target_pairs={{0,8},{4,12},{8,0},{12,4},{1,9},{5,13},{9,1},{13,5},{2,10},{6,14},... | collective-permute-start | bytes 491528 | tf_op jit(solution)/shard_map/ppermute | solution.py:701
  41.0 7.7 %collective-permute-start.10 = (f32[2,20,8,128]{3,2,1,0:T(8,128)S(1)}, f32[2,20,8,128]{3,2,1,0:T(8,128)S(1)}, u32[]{:S(2)}, u32[]{:S(2)}) collective-permute-start(f32[2,20,8,128]{3,2,1,0:T(8,128)S(1)} %get-tuple-element.86), channel_id=1, source_target_pairs={{0,12},{4,8},{8,4},{12,0},{1,13},{5,9},{9,5},{13,1},{2,14},{6,10},... | collective-permute-start | bytes 491528 | tf_op jit(solution)/shard_map/ppermute | solution.py:701
  46.1 10.6 %collective-permute-start.15 = (f32[31,8,128]{2,1,0:T(8,128)S(1)}, f32[31,8,128]{2,1,0:T(8,128)S(1)}, u32[]{:S(2)}, u32[]{:S(2)}) collective-permute-start(f32[31,8,128]{2,1,0:T(8,128)S(1)} %get-tuple-element.95), channel_id=1, source_target_pairs={{0,8},{4,12},{8,0},{12,4},{1,9},{5,13},{9,1},{13,5},{2,10},{6,14},... | collective-permute-start | bytes 380936 | tf_op jit(solution)/shard_map/ppermute | solution.py:701
  48.7 8.0 %collective-permute-start.16 = (f32[31,8,128]{2,1,0:T(8,128)S(1)}, f32[31,8,128]{2,1,0:T(8,128)S(1)}, u32[]{:S(2)}, u32[]{:S(2)}) collective-permute-start(f32[31,8,128]{2,1,0:T(8,128)S(1)} %get-tuple-element.96), channel_id=1, source_target_pairs={{0,12},{4,8},{8,4},{12,0},{1,13},{5,9},{9,5},{13,1},{2,14},{6,10},... | collective-permute-start | bytes 380936 | tf_op jit(solution)/shard_map/ppermute | solution.py:701
  49.8 12.7 %collective-permute-start.11 = (f32[31,8,128]{2,1,0:T(8,128)S(1)}, f32[31,8,128]{2,1,0:T(8,128)S(1)}, u32[]{:S(2)}, u32[]{:S(2)}) collective-permute-start(f32[31,8,128]{2,1,0:T(8,128)S(1)} %get-tuple-element.90), channel_id=1, source_target_pairs={{0,4},{4,0},{8,12},{12,8},{1,5},{5,1},{9,13},{13,9},{2,6},{6,2},{1... | collective-permute-start | bytes 380936 | tf_op jit(solution)/shard_map/ppermute | solution.py:701
  50.5 12.1 %collective-permute-start.12 = (f32[31,8,128]{2,1,0:T(8,128)S(1)}, f32[31,8,128]{2,1,0:T(8,128)S(1)}, u32[]{:S(2)}, u32[]{:S(2)}) collective-permute-start(f32[31,8,128]{2,1,0:T(8,128)S(1)} %get-tuple-element.91), channel_id=1, source_target_pairs={{0,8},{4,12},{8,0},{12,4},{1,9},{5,13},{9,1},{13,5},{2,10},{6,14},... | collective-permute-start | bytes 380936 | tf_op jit(solution)/shard_map/ppermute | solution.py:701
  52.2 10.4 %collective-permute-start.13 = (f32[31,8,128]{2,1,0:T(8,128)S(1)}, f32[31,8,128]{2,1,0:T(8,128)S(1)}, u32[]{:S(2)}, u32[]{:S(2)}) collective-permute-start(f32[31,8,128]{2,1,0:T(8,128)S(1)} %get-tuple-element.92), channel_id=1, source_target_pairs={{0,12},{4,8},{8,4},{12,0},{1,13},{5,9},{9,5},{13,1},{2,14},{6,10},... | collective-permute-start | bytes 380936 | tf_op jit(solution)/shard_map/ppermute | solution.py:701
  85.6 6.9 %collective-permute-start.20 = (f32[32,8,128]{2,1,0:T(8,128)S(1)}, f32[32,8,128]{2,1,0:T(8,128)S(1)}, u32[]{:S(2)}, u32[]{:S(2)}) collective-permute-start(f32[32,8,128]{2,1,0:T(8,128)S(1)} %get-tuple-element.119), channel_id=1, source_target_pairs={{0,4},{4,0},{8,12},{12,8},{1,5},{5,1},{9,13},{13,9},{2,6},{6,2},{1... | collective-permute-start | bytes 393224 | tf_op jit(solution)/shard_map/ppermute | solution.py:701
  88.3 14.5 %collective-permute-start.17 = (f32[48,8,128]{2,1,0:T(8,128)S(1)}, f32[48,8,128]{2,1,0:T(8,128)S(1)}, u32[]{:S(2)}, u32[]{:S(2)}) collective-permute-start(f32[48,8,128]{2,1,0:T(8,128)S(1)} %get-tuple-element.115), channel_id=1, source_target_pairs={{0,4},{4,0},{8,12},{12,8},{1,5},{5,1},{9,13},{13,9},{2,6},{6,2},{1... | collective-permute-start | bytes 589832 | tf_op jit(solution)/shard_map/ppermute | solution.py:701
  89.6 13.2 %collective-permute-start.18 = (f32[48,8,128]{2,1,0:T(8,128)S(1)}, f32[48,8,128]{2,1,0:T(8,128)S(1)}, u32[]{:S(2)}, u32[]{:S(2)}) collective-permute-start(f32[48,8,128]{2,1,0:T(8,128)S(1)} %get-tuple-element.116), channel_id=1, source_target_pairs={{0,8},{4,12},{8,0},{12,4},{1,9},{5,13},{9,1},{13,5},{2,10},{6,14},... | collective-permute-start | bytes 589832 | tf_op jit(solution)/shard_map/ppermute | solution.py:701
  90.4 12.5 %collective-permute-start.19 = (f32[48,8,128]{2,1,0:T(8,128)S(1)}, f32[48,8,128]{2,1,0:T(8,128)S(1)}, u32[]{:S(2)}, u32[]{:S(2)}) collective-permute-start(f32[48,8,128]{2,1,0:T(8,128)S(1)} %get-tuple-element.117), channel_id=1, source_target_pairs={{0,12},{4,8},{8,4},{12,0},{1,13},{5,9},{9,5},{13,1},{2,14},{6,10},... | collective-permute-start | bytes 589832 | tf_op jit(solution)/shard_map/ppermute | solution.py:701
  91.8 9.5 %collective-permute-start.21 = (f32[32,8,128]{2,1,0:T(8,128)S(1)}, f32[32,8,128]{2,1,0:T(8,128)S(1)}, u32[]{:S(2)}, u32[]{:S(2)}) collective-permute-start(f32[32,8,128]{2,1,0:T(8,128)S(1)} %get-tuple-element.120), channel_id=1, source_target_pairs={{0,8},{4,12},{8,0},{12,4},{1,9},{5,13},{9,1},{13,5},{2,10},{6,14},... | collective-permute-start | bytes 393224 | tf_op jit(solution)/shard_map/ppermute | solution.py:701
  92.5 8.8 %collective-permute-start.22 = (f32[32,8,128]{2,1,0:T(8,128)S(1)}, f32[32,8,128]{2,1,0:T(8,128)S(1)}, u32[]{:S(2)}, u32[]{:S(2)}) collective-permute-start(f32[32,8,128]{2,1,0:T(8,128)S(1)} %get-tuple-element.121), channel_id=1, source_target_pairs={{0,12},{4,8},{8,4},{12,0},{1,13},{5,9},{9,5},{13,1},{2,14},{6,10},... | collective-permute-start | bytes 393224 | tf_op jit(solution)/shard_map/ppermute | solution.py:701
